TPU v7x, 32 devices: a whole 2x2x4 slice. The times are simulated.
32 devices in a mesh: expert: 8 (over z, x), tensor: 4 (over y, core).
Axes of the slice: x: 2, y: 2, z: 4, core: 2. Of those that a mesh axis runs over, the one named last changes fastest.
Arguments:
- hidden_in: bfloat16 [4096, 2048], P('expert', 'tensor'), may hold values from -6 to 6
- out_grad: bfloat16 [4096, 2048], P('expert', 'tensor'), may hold values from -6 to 6
- first_gain: bfloat16 [2048], P('expert'), may hold values from 0.25 to 1.75
- query_weight: bfloat16 [2048, 3072], P('expert', 'tensor'), may hold values from -0.1875 to 0.1875
- latent_weight: bfloat16 [2048, 576], P('expert'), may hold values from -0.125 to 0.125
- latent_gain: bfloat16 [512], P('expert'), may hold values from 0.25 to 1.75
- expand_weight: bfloat16 [512, 4096], P('expert', 'tensor'), may hold values from -0.25 to 0.25
- output_weight: bfloat16 [2048, 2048], P('expert', 'tensor'), may hold values from -0.75 to 0.75
- second_gain: bfloat16 [2048], P('expert'), may hold values from 0.25 to 1.75
- shared_gate: bfloat16 [2048, 2816], P('expert', 'tensor'), may hold values from -0.125 to 0.125
- shared_up: bfloat16 [2048, 2816], P('expert', 'tensor'), may hold values from -0.125 to 0.125
- shared_down: bfloat16 [2048, 2816], P('expert', 'tensor'), may hold values from -0.109375 to 0.109375
- expert_gate: bfloat16 [16, 2048, 1408], P('expert', None, 'tensor'), may hold values from -0.125 to 0.125
- expert_up: bfloat16 [16, 2048, 1408], P('expert', None, 'tensor'), may hold values from -0.125 to 0.125
- expert_down: bfloat16 [16, 1408, 2048], P('expert', 'tensor'), may hold values from -0.15625 to 0.15625
- routes: int32 [4096, 6], P('expert'), may hold values from 0 to 15, all different within a row
- gate_values: float32 [4096, 6], P('expert'), may hold values from 0.3 to 1
Outputs:
- block_out: bfloat16 [4096, 2048], P('expert', 'tensor')
- input_grad: float32 [4096, 2048], P('expert', 'tensor')
- grad_first_gain: float32 [2048], P('expert')
- grad_query: float32 [2048, 3072], P('expert', 'tensor')
- grad_latent: float32 [2048, 576], P('expert')
- grad_latent_gain: float32 [512], P('expert')
- grad_expand: float32 [512, 4096], P('expert', 'tensor')
- grad_output: float32 [2048, 2048], P('expert', 'tensor')
- grad_second_gain: float32 [2048], P('expert')
- grad_shared_gate: float32 [2048, 2816], P('expert', 'tensor')
- grad_shared_up: float32 [2048, 2816], P('expert', 'tensor')
- grad_shared_down: float32 [2048, 2816], P('expert', 'tensor')
- grad_expert_gate: float32 [16, 2048, 1408], P('expert', None, 'tensor')
- grad_expert_up: float32 [16, 2048, 1408], P('expert', None, 'tensor')
- grad_expert_down: float32 [16, 1408, 2048], P('expert', 'tensor')
Inputs may be any that keep to these rules, and one draw needn't show every extreme that they name: `routes`: each token names 6 different experts, and every expert is named by some token.
All inputs are finite; a program needn't handle non-finite values.
Results may differ from a plain program's by a relative error of at most 0.025.
Values may be sent and summed in bfloat16 or wider, within the bound.
A program may use at most 320 MiB of HBM per device.

v0:
```python
import math

import jax
import jax.numpy as jnp
from jax import lax
from jax.sharding import PartitionSpec as P

D = 2048
H = 16
DN = 128
DR = 64
DV = 128
KV_RANK = 512
TOP = 6
EXP_DEV = 2
SEQ = 256
BLOCK = 128
MB = 2


norm_eps = 1e-06
masked_value = -1000000000.0


def matmul(left, right):
    return jnp.dot(left, right, preferred_element_type=jnp.float32)


def matmul_rows(left, right):
    return lax.dot_general(
        left, right, (((1,), (1,)), ((), ())), preferred_element_type=jnp.float32
    )


def matmul_cols(left, right):
    return lax.dot_general(
        left, right, (((0,), (0,)), ((), ())), preferred_element_type=jnp.float32
    )


def rms_scale(values):
    return lax.rsqrt(jnp.mean(values * values, axis=-1, keepdims=True) + norm_eps)


def rope_tables(length, width):
    position = jnp.arange(length, dtype=jnp.float32)
    rates = jnp.exp(jnp.arange(width // 2, dtype=jnp.float32) * (-2.0 * math.log(10000.0) / width))
    angle = position[:, None] * rates[None, :]
    return (jnp.cos(angle), jnp.sin(angle))


def rotate(values, cosine, sine):
    half = values.shape[-1] // 2
    first = values[..., :half]
    second = values[..., half:]
    return jnp.concatenate(
        [first * cosine - second * sine, second * cosine + first * sine], axis=-1
    )


def unrotate(grads, cosine, sine):
    half = grads.shape[-1] // 2
    first = grads[..., :half]
    second = grads[..., half:]
    return jnp.concatenate(
        [first * cosine + second * sine, second * cosine - first * sine], axis=-1
    )


def norm_back(grad_hat, hat, scale_rows):
    return scale_rows * (grad_hat - hat * jnp.mean(grad_hat * hat, axis=-1, keepdims=True))


def slot_targets(route_rows, experts_all, capacity):
    length = route_rows.shape[0]
    onehot = (
        route_rows[:, :, None] == jnp.arange(experts_all, dtype=jnp.int32)[None, None, :]
    ).astype(jnp.int32)
    per_token = jnp.sum(onehot, axis=1)
    prior = jnp.cumsum(per_token, axis=0) - per_token
    rank = jnp.take_along_axis(prior, route_rows, axis=1)
    kept = rank < capacity
    targets = jnp.where(kept, route_rows * capacity + rank, experts_all * capacity)
    owners = (
        jnp.full((experts_all * capacity,), length, jnp.int32)
        .at[targets.reshape(-1)]
        .set(jnp.repeat(jnp.arange(length, dtype=jnp.int32), route_rows.shape[1]), mode="drop")
    )
    return (targets, owners)


def local(
    hidden_in,
    out_grad,
    first_gain,
    query_weight,
    latent_weight,
    latent_gain,
    expand_weight,
    output_weight,
    second_gain,
    shared_gate,
    shared_up,
    shared_down,
    expert_gate,
    expert_up,
    expert_down,
    routes,
    gate_values,
):
    groups = lax.axis_size("expert")
    tensors = lax.axis_size("tensor")
    tensor_place = lax.axis_index("tensor")
    experts_all = EXP_DEV * groups
    capacity = SEQ * TOP * 4 // (3 * experts_all)
    width = D // tensors
    local_heads = H // tensors
    scale = (DN + DR) ** (-0.5)
    cosine, sine = rope_tables(SEQ, DR)
    blocks = jnp.arange(SEQ, dtype=jnp.int32) // BLOCK
    allowed = (blocks[None, :] <= blocks[:, None])[None]
    total_gate = jnp.zeros(expert_gate.shape, jnp.float32)
    total_up = jnp.zeros(expert_up.shape, jnp.float32)
    total_down = jnp.zeros(expert_down.shape, jnp.float32)
    dense_total = ()
    out_blocks = []
    input_blocks = []
    for micro_step in range(MB):
        lower = micro_step * SEQ
        route_rows = routes[lower : lower + SEQ]
        gate_rows = gate_values[lower : lower + SEQ]
        whole_in, whole_grad = (
            lax.all_gather(hidden_in[lower : lower + SEQ], "tensor", axis=1, tiled=True),
            lax.all_gather(out_grad[lower : lower + SEQ], "tensor", axis=1, tiled=True),
        )
        (
            gain_one,
            full_query,
            full_latent,
            gain_latent,
            full_expand,
            full_output,
            gain_two,
            full_sgate,
            full_sup,
            full_sdown,
        ) = (
            lax.all_gather(first_gain, "expert", axis=0, tiled=True),
            lax.all_gather(query_weight, "expert", axis=0, tiled=True),
            lax.all_gather(latent_weight, "expert", axis=0, tiled=True),
            lax.all_gather(latent_gain, "expert", axis=0, tiled=True),
            lax.all_gather(expand_weight, "expert", axis=0, tiled=True),
            lax.all_gather(output_weight, "expert", axis=0, tiled=True),
            lax.all_gather(second_gain, "expert", axis=0, tiled=True),
            lax.all_gather(shared_gate, "expert", axis=0, tiled=True),
            lax.all_gather(shared_up, "expert", axis=0, tiled=True),
            lax.all_gather(shared_down, "expert", axis=0, tiled=True),
        )
        gain_first = gain_one.astype(jnp.float32)
        gain_kv = gain_latent.astype(jnp.float32)
        gain_mid = gain_two.astype(jnp.float32)
        inputs = whole_in.astype(jnp.float32)
        first_scale = rms_scale(inputs)
        first_hat = inputs * first_scale
        normed = (first_hat * gain_first).astype(jnp.bfloat16)
        query = matmul(normed, full_query).reshape(SEQ, local_heads, DN + DR)
        latent = matmul(normed, full_latent)
        compressed = latent[:, :KV_RANK]
        latent_scale = rms_scale(compressed)
        latent_hat = compressed * latent_scale
        latent_normed = (latent_hat * gain_kv).astype(jnp.bfloat16)
        expanded = matmul(latent_normed, full_expand).reshape(SEQ, local_heads, DN + DV)
        queries = jnp.concatenate(
            [query[..., :DN], rotate(query[..., DN:], cosine[:, None, :], sine[:, None, :])],
            axis=-1,
        ).astype(jnp.bfloat16)
        key_rope = rotate(latent[:, KV_RANK:], cosine, sine).astype(jnp.bfloat16)
        keys = jnp.concatenate(
            [
                expanded[..., :DN].astype(jnp.bfloat16),
                jnp.broadcast_to(key_rope[:, None, :], (SEQ, local_heads, DR)),
            ],
            axis=-1,
        )
        values = expanded[..., DN:].astype(jnp.bfloat16)
        scores = jnp.where(
            allowed,
            jnp.einsum("qhc,khc->hqk", queries, keys, preferred_element_type=jnp.float32) * scale,
            masked_value,
        )
        peak = jnp.max(scores, axis=-1, keepdims=True)
        log_total = peak + jnp.log(jnp.sum(jnp.exp(scores - peak), axis=-1, keepdims=True))
        softmax_weights = jnp.exp(scores - log_total)
        mixed = (
            jnp.einsum(
                "hqk,khc->qhc",
                softmax_weights.astype(jnp.bfloat16),
                values,
                preferred_element_type=jnp.float32,
            )
            .astype(jnp.bfloat16)
            .reshape(SEQ, local_heads * DV)
        )
        attended = lax.psum(matmul_rows(mixed, full_output).astype(jnp.bfloat16), "tensor").astype(
            jnp.float32
        )
        middle = inputs + attended
        second_scale = rms_scale(middle)
        second_hat = middle * second_scale
        mixer_in = (second_hat * gain_mid).astype(jnp.bfloat16)
        shared_g = matmul(mixer_in, full_sgate)
        shared_u = matmul(mixer_in, full_sup)
        shared_sig = jax.nn.sigmoid(shared_g)
        shared_hidden = (shared_g * shared_sig * shared_u).astype(jnp.bfloat16)
        shared_part = matmul_rows(shared_hidden, full_sdown)
        targets, owners = slot_targets(route_rows, experts_all, capacity)
        padded_in = jnp.concatenate([mixer_in, jnp.zeros((1, D), jnp.bfloat16)], axis=0)
        dispatched = padded_in[owners].reshape(experts_all, capacity, D)
        arrived = lax.all_to_all(dispatched, "expert", split_axis=0, concat_axis=0, tiled=True)
        arrived = arrived.reshape(groups, EXP_DEV, capacity, D)
        gated = jnp.einsum(
            "nlcd,ldf->nlcf", arrived, expert_gate, preferred_element_type=jnp.float32
        )
        upper = jnp.einsum("nlcd,ldf->nlcf", arrived, expert_up, preferred_element_type=jnp.float32)
        gate_sig = jax.nn.sigmoid(gated)
        gate_act = gated * gate_sig
        expert_hidden = (gate_act * upper).astype(jnp.bfloat16)
        expert_part = jnp.einsum(
            "nlcf,lfd->nlcd", expert_hidden, expert_down, preferred_element_type=jnp.float32
        ).astype(jnp.bfloat16)
        returned = lax.all_to_all(
            expert_part.reshape(experts_all, capacity, D),
            "expert",
            split_axis=0,
            concat_axis=0,
            tiled=True,
        )
        padded_out = jnp.concatenate(
            [returned.reshape(experts_all * capacity, D), jnp.zeros((1, D), jnp.bfloat16)], axis=0
        )
        picked = padded_out[targets]
        routed_part = jnp.sum(gate_rows[:, :, None] * picked.astype(jnp.float32), axis=1)
        summed = lax.psum_scatter(
            (shared_part + routed_part).astype(jnp.bfloat16),
            "tensor",
            scatter_dimension=1,
            tiled=True,
        ).astype(jnp.float32)
        middle_part = lax.dynamic_slice_in_dim(middle, tensor_place * width, width, 1)
        out_blocks.append((middle_part + summed).astype(jnp.bfloat16))
        gate_slot = (
            jnp.zeros((experts_all * capacity,), jnp.float32)
            .at[targets.reshape(-1)]
            .set(gate_rows.reshape(-1), mode="drop")
        )
        padded_grad = jnp.concatenate([whole_grad, jnp.zeros((1, D), jnp.bfloat16)], axis=0)
        slot_grad = (
            (padded_grad[owners].astype(jnp.float32) * gate_slot[:, None])
            .astype(jnp.bfloat16)
            .reshape(experts_all, capacity, D)
        )
        grad_arrived = lax.all_to_all(
            slot_grad, "expert", split_axis=0, concat_axis=0, tiled=True
        ).reshape(groups, EXP_DEV, capacity, D)
        grad_hidden = jnp.einsum(
            "nlcd,lfd->nlcf", grad_arrived, expert_down, preferred_element_type=jnp.float32
        )
        total_down = total_down + jnp.einsum(
            "nlcf,nlcd->lfd", expert_hidden, grad_arrived, preferred_element_type=jnp.float32
        )
        grad_gated = (grad_hidden * upper * gate_sig * (1.0 + gated * (1.0 - gate_sig))).astype(
            jnp.bfloat16
        )
        grad_upper = (grad_hidden * gate_act).astype(jnp.bfloat16)
        total_gate = total_gate + jnp.einsum(
            "nlcd,nlcf->ldf", arrived, grad_gated, preferred_element_type=jnp.float32
        )
        total_up = total_up + jnp.einsum(
            "nlcd,nlcf->ldf", arrived, grad_upper, preferred_element_type=jnp.float32
        )
        row_grad = (
            jnp.einsum(
                "nlcf,ldf->nlcd", grad_gated, expert_gate, preferred_element_type=jnp.float32
            )
            + jnp.einsum(
                "nlcf,ldf->nlcd", grad_upper, expert_up, preferred_element_type=jnp.float32
            )
        ).astype(jnp.bfloat16)
        back_rows = lax.all_to_all(
            row_grad.reshape(experts_all, capacity, D),
            "expert",
            split_axis=0,
            concat_axis=0,
            tiled=True,
        )
        padded_back = jnp.concatenate(
            [back_rows.reshape(experts_all * capacity, D), jnp.zeros((1, D), jnp.bfloat16)], axis=0
        )
        routed_grad = jnp.sum(padded_back[targets].astype(jnp.float32), axis=1)
        grad_shared = matmul(whole_grad, full_sdown)
        step_sdown = matmul_cols(whole_grad, shared_hidden)
        grad_sg = (
            grad_shared * shared_u * shared_sig * (1.0 + shared_g * (1.0 - shared_sig))
        ).astype(jnp.bfloat16)
        grad_su = (grad_shared * shared_g * shared_sig).astype(jnp.bfloat16)
        step_sgate = matmul_cols(mixer_in, grad_sg)
        step_sup = matmul_cols(mixer_in, grad_su)
        mixer_part = matmul_rows(grad_sg, full_sgate) + matmul_rows(grad_su, full_sup) + routed_grad
        grad_mixer = lax.psum(mixer_part.astype(jnp.bfloat16), "tensor").astype(jnp.float32)
        step_gain_two = jnp.sum(grad_mixer * second_hat, axis=0)
        grad_middle = whole_grad.astype(jnp.float32) + norm_back(
            grad_mixer * gain_mid, second_hat, second_scale
        )
        grad_att = grad_middle.astype(jnp.bfloat16)
        step_output = matmul_cols(grad_att, mixed)
        grad_mixed = (
            matmul(grad_att, full_output).astype(jnp.bfloat16).reshape(SEQ, local_heads, DV)
        )
        scores_again = jnp.where(
            allowed,
            jnp.einsum("qhc,khc->hqk", queries, keys, preferred_element_type=jnp.float32) * scale,
            masked_value,
        )
        weights_again = jnp.exp(scores_again - log_total)
        grad_weights = jnp.einsum(
            "qhc,khc->hqk", grad_mixed, values, preferred_element_type=jnp.float32
        )
        grad_scores = (
            weights_again
            * (grad_weights - jnp.sum(weights_again * grad_weights, axis=-1, keepdims=True))
        ).astype(jnp.bfloat16)
        grad_values = jnp.einsum(
            "hqk,qhc->khc",
            weights_again.astype(jnp.bfloat16),
            grad_mixed,
            preferred_element_type=jnp.float32,
        )
        grad_queries = (
            jnp.einsum("hqk,khc->qhc", grad_scores, keys, preferred_element_type=jnp.float32)
            * scale
        )
        grad_keys = (
            jnp.einsum("hqk,qhc->khc", grad_scores, queries, preferred_element_type=jnp.float32)
            * scale
        )
        grad_query = (
            jnp.concatenate(
                [
                    grad_queries[..., :DN],
                    unrotate(grad_queries[..., DN:], cosine[:, None, :], sine[:, None, :]),
                ],
                axis=-1,
            )
            .astype(jnp.bfloat16)
            .reshape(SEQ, local_heads * (DN + DR))
        )
        step_query = matmul_cols(normed, grad_query)
        query_part = matmul_rows(grad_query, full_query)
        rope_part = unrotate(jnp.sum(grad_keys[..., DN:], axis=1), cosine, sine)
        grad_expanded = (
            jnp.concatenate([grad_keys[..., :DN], grad_values], axis=-1)
            .astype(jnp.bfloat16)
            .reshape(SEQ, local_heads * (DN + DV))
        )
        step_expand = matmul_cols(latent_normed, grad_expanded)
        latent_part = matmul_rows(grad_expanded, full_expand)
        grad_lnormed, grad_rope = (
            lax.psum(latent_part.astype(jnp.bfloat16), "tensor").astype(jnp.float32),
            lax.psum(rope_part.astype(jnp.bfloat16), "tensor").astype(jnp.float32),
        )
        step_gain_latent = jnp.sum(grad_lnormed * latent_hat, axis=0)
        grad_compressed = norm_back(grad_lnormed * gain_kv, latent_hat, latent_scale)
        grad_lat = jnp.concatenate([grad_compressed, grad_rope], axis=-1).astype(jnp.bfloat16)
        step_latent = matmul_cols(normed, grad_lat)
        grad_normed = lax.psum(query_part.astype(jnp.bfloat16), "tensor").astype(
            jnp.float32
        ) + matmul_rows(grad_lat, full_latent)
        step_gain_one = jnp.sum(grad_normed * first_hat, axis=0)
        grad_inputs = grad_middle + norm_back(grad_normed * gain_first, first_hat, first_scale)
        input_blocks.append(lax.dynamic_slice_in_dim(grad_inputs, tensor_place * width, width, 1))
        shards = (
            lax.psum_scatter(
                step_gain_one.astype(jnp.bfloat16), "expert", scatter_dimension=0, tiled=True
            ).astype(jnp.float32),
            lax.psum_scatter(
                step_query.astype(jnp.bfloat16), "expert", scatter_dimension=0, tiled=True
            ).astype(jnp.float32),
            lax.psum_scatter(
                step_latent.astype(jnp.bfloat16), "expert", scatter_dimension=0, tiled=True
            ).astype(jnp.float32),
            lax.psum_scatter(
                step_gain_latent.astype(jnp.bfloat16), "expert", scatter_dimension=0, tiled=True
            ).astype(jnp.float32),
            lax.psum_scatter(
                step_expand.astype(jnp.bfloat16), "expert", scatter_dimension=0, tiled=True
            ).astype(jnp.float32),
            lax.psum_scatter(
                step_output.astype(jnp.bfloat16), "expert", scatter_dimension=0, tiled=True
            ).astype(jnp.float32),
            lax.psum_scatter(
                step_gain_two.astype(jnp.bfloat16), "expert", scatter_dimension=0, tiled=True
            ).astype(jnp.float32),
            lax.psum_scatter(
                step_sgate.astype(jnp.bfloat16), "expert", scatter_dimension=0, tiled=True
            ).astype(jnp.float32),
            lax.psum_scatter(
                step_sup.astype(jnp.bfloat16), "expert", scatter_dimension=0, tiled=True
            ).astype(jnp.float32),
            lax.psum_scatter(
                step_sdown.astype(jnp.bfloat16), "expert", scatter_dimension=0, tiled=True
            ).astype(jnp.float32),
        )
        if micro_step == 0:
            dense_total = shards
        else:
            dense_total = jax.tree.map(jnp.add, dense_total, shards)
    block_out = jnp.concatenate(out_blocks, axis=0)
    input_grad = jnp.concatenate(input_blocks, axis=0)
    return (
        block_out,
        input_grad,
        dense_total[0],
        dense_total[1],
        dense_total[2],
        dense_total[3],
        dense_total[4],
        dense_total[5],
        dense_total[6],
        dense_total[7],
        dense_total[8],
        dense_total[9],
        total_gate,
        total_up,
        total_down,
    )


def solution(mesh):
    return jax.shard_map(
        local,
        mesh=mesh,
        in_specs=(
            P("expert", "tensor"),
            P("expert", "tensor"),
            P("expert"),
            P("expert", "tensor"),
            P("expert", None),
            P("expert"),
            P("expert", "tensor"),
            P("expert", "tensor"),
            P("expert"),
            P("expert", "tensor"),
            P("expert", "tensor"),
            P("expert", "tensor"),
            P("expert", None, "tensor"),
            P("expert", None, "tensor"),
            P("expert", "tensor", None),
            P("expert", None),
            P("expert", None),
        ),
        out_specs=(
            P("expert", "tensor"),
            P("expert", "tensor"),
            P("expert"),
            P("expert", "tensor"),
            P("expert", None),
            P("expert"),
            P("expert", "tensor"),
            P("expert", "tensor"),
            P("expert"),
            P("expert", "tensor"),
            P("expert", "tensor"),
            P("expert", "tensor"),
            P("expert", None, "tensor"),
            P("expert", None, "tensor"),
            P("expert", "tensor", None),
        ),
        check_vma=False,
    )
```

profile of v0, /device:TPU:0, one launch (start us, length us, event | category | flops | bytes accessed | tf_op | source)
XLA Modules:
  0.0 3179.2 jit_solution(11205304669784932112)
XLA Ops:
  14.3 10.3 gather_fusion.9
  40.8 17.7 gather_fusion.6
  58.5 8.2 fusion
  80.6 10.3 gather_fusion.8
  107.3 17.7 gather_fusion.4
  125.0 8.2 fusion.1
  133.2 152.7 %all-to-all-done.6 = bf16[16,128,2048]{2,1,0:T(8,128)(2,1)} async-done(((bf16[16,128,2048]{2,1,0:T(8,128)(2,1)}), bf16[16,128,2048]{2,1,0:T(8,128)(2,1)}, u32[]{:S(2)}, u32[]{:S(2)}) %all-to-all-start.6) | async-done | bytes 8388640 | tf_op jit(solution)/shard_map/all_to_all | solution.py:262
  293.1 158.8 %all-reduce.8 = bf16[512]{0:T(512)(128)(2,1)S(1)} all-reduce(bf16[512]{0:T(512)(128)(2,1)S(1)} %dynamic-update-slice), channel_id=1, replica_groups=mesh['expert'=8,'tensor'=4] {'expert'}, use_global_device_ids=true, to_apply=%add.8 | all-reduce | flops 512 | bytes 2048
  452.0 60.5 %all-gather = bf16[8,1,256]{2,1,0:T(2,128)(2,1)S(1)} all-gather(bf16[1,1,256]{2,1,0:T(2,128)(2,1)S(1)} %reshape.626), channel_id=1, replica_groups=mesh['expert'=8,'tensor'=4] {'expert'}, dimensions={0}, use_global_device_ids=true | all-gather | bytes 4608 | tf_op jit(solution)/shard_map/all_gather | solution.py:148
  537.4 8.7 all-gather.20.cloned.1.call-done
  554.6 41.6 %all-gather.22.cloned.1.call-done = bf16[2048,512]{1,0:T(8,128)(2,1)} async-done(((bf16[256,512]{1,0:T(8,128)(2,1)}), bf16[2048,512]{1,0:T(8,128)(2,1)}) %all-gather.22.cloned.1.call-update) | async-done | bytes 2097168 | tf_op jit(solution)/shard_map/all_gather | solution.py:153
  601.5 29.1 all-gather.1
  630.6 21.1 all-reduce.31.cloned.1.call-done
  660.0 17.7 gather_fusion.2
  685.5 17.7 gather_fusion
  703.3 163.1 %all-to-all-done.2 = bf16[16,128,2048]{2,1,0:T(8,128)(2,1)} async-done(((bf16[16,128,2048]{2,1,0:T(8,128)(2,1)}), bf16[16,128,2048]{2,1,0:T(8,128)(2,1)}, u32[]{:S(2)}, u32[]{:S(2)}) %all-to-all-start.2) | async-done | bytes 8388640 | tf_op jit(solution)/shard_map/all_to_all | solution.py:219
  883.6 7.7 fusion.27
  891.3 8.3 fusion.45
  899.5 11.2 fusion.3
  910.7 8.4 copy.204
  919.1 134.3 %all-to-all-done = bf16[16,128,2048]{2,1,0:T(8,128)(2,1)} async-done(((bf16[16,128,2048]{2,1,0:T(8,128)(2,1)}), bf16[16,128,2048]{2,1,0:T(8,128)(2,1)}, u32[]{:S(2)}, u32[]{:S(2)}) %all-to-all-start) | async-done | bytes 8388640 | tf_op jit(solution)/shard_map/all_to_all | solution.py:219
  1071.2 7.7 fusion.31
  1078.9 8.3 fusion.47
  1087.1 11.2 fusion.2
  1098.3 8.3 copy.194
  1106.7 168.5 %all-to-all-done.7 = bf16[16,128,2048]{2,1,0:T(8,128)(2,1)} async-done(((bf16[16,128,2048]{2,1,0:T(8,128)(2,1)}), bf16[16,128,2048]{2,1,0:T(8,128)(2,1)}, u32[]{:S(2)}, u32[]{:S(2)}) %all-to-all-start.7) | async-done | bytes 8388640 | tf_op jit(solution)/shard_map/all_to_all | solution.py:289
  1288.1 176.7 %all-gather.24.cloned.1.call-done = bf16[2048,704]{0,1:T(8,128)(2,1)} async-done(((bf16[256,704]{0,1:T(8,128)(2,1)}), bf16[2048,704]{0,1:T(8,128)(2,1)}) %all-gather.24.cloned.1.call-update) | async-done | bytes 2883600 | tf_op jit(solution)/shard_map/all_gather | solution.py:155
  1470.7 63.7 %all-gather.28.cloned.1.call-done = bf16[2048,704]{0,1:T(8,128)(2,1)} async-done(((bf16[256,704]{0,1:T(8,128)(2,1)}), bf16[2048,704]{0,1:T(8,128)(2,1)}) %all-gather.28.cloned.1.call-update) | async-done | bytes 2883600 | tf_op jit(solution)/shard_map/all_gather | solution.py:157
  1546.7 8.4 concatenate.110
  1555.1 17.4 gather_fusion.7
  1572.4 11.7 reshape.618
  1584.2 9.8 reduce_sum.288
  1594.0 8.4 concatenate.104
  1602.4 17.2 gather_fusion.5
  1619.6 11.7 reshape.617
  1631.3 9.8 reduce_sum.282
  1648.8 50.6 %all-reduce.29.cloned.1.call-done = (bf16[256,2048]{1,0:T(8,128)(2,1)}, bf16[256,2048]{1,0:T(8,128)(2,1)}) async-done(((bf16[256,2048]{1,0:T(8,128)(2,1)}, bf16[256,2048]{1,0:T(8,128)(2,1)}), (bf16[256,2048]{1,0:T(8,128)(2,1)}, bf16[256,2048]{1,0:T(8,128)(2,1)})) %all-reduce.29.cloned.1.call-update) | async-done | bytes 2097168 | tf_op jit(solution)/shard_map/psum | solution.py:309
  1752.1 8.2 convert_bitcast_fusion.1
  1760.3 8.4 copy.177
  1783.0 8.3 convert_bitcast_fusion
  1791.3 8.4 copy.191
  1799.7 181.1 %all-to-all-done.1 = bf16[16,128,2048]{2,1,0:T(8,128)(2,1)} async-done(((bf16[16,128,2048]{2,1,0:T(8,128)(2,1)}), bf16[16,128,2048]{2,1,0:T(8,128)(2,1)}, u32[]{:S(2)}, u32[]{:S(2)}) %all-to-all-start.1) | async-done | bytes 8388640 | tf_op jit(solution)/shard_map/all_to_all | solution.py:231
  1993.9 8.4 concatenate.96
  2002.3 17.1 gather_fusion.1
  2019.4 11.7 reshape.615
  2031.2 9.5 multiply_reduce_fusion.1
  2043.2 159.6 %all-to-all-done.3 = bf16[16,128,2048]{2,1,0:T(8,128)(2,1)} async-done(((bf16[16,128,2048]{2,1,0:T(8,128)(2,1)}), bf16[16,128,2048]{2,1,0:T(8,128)(2,1)}, u32[]{:S(2)}, u32[]{:S(2)}) %all-to-all-start.3) | async-done | bytes 8388640 | tf_op jit(solution)/shard_map/all_to_all | solution.py:231
  2202.8 8.4 concatenate.101
  2211.2 17.2 gather_fusion.3
  2228.3 11.8 reshape.616
  2240.1 9.5 multiply_reduce_fusion
  2285.4 29.1 reduce-scatter.41.cloned.1.call-done
  2314.5 76.1 %reduce-scatter.43.cloned.1.call-done = bf16[256,704]{0,1:T(8,128)(2,1)} async-done(((bf16[2048,704]{0,1:T(8,128)(2,1)}), bf16[256,704]{0,1:T(8,128)(2,1)}) %reduce-scatter.43.cloned.1.call-update) | async-done | bytes 360464 | tf_op jit(solution)/shard_map/reduce_scatter | solution.py:406
  2392.6 73.4 %reduce-scatter.47.cloned.1.call-done = bf16[256,704]{0,1:T(8,128)(2,1)} async-done(((bf16[2048,704]{0,1:T(8,128)(2,1)}), bf16[256,704]{0,1:T(8,128)(2,1)}) %reduce-scatter.47.cloned.1.call-update) | async-done | bytes 360464 | tf_op jit(solution)/shard_map/reduce_scatter | solution.py:409
  2466.0 75.6 %reduce-scatter.45.cloned.1.call-done = bf16[256,704]{0,1:T(8,128)(2,1)} async-done(((bf16[2048,704]{0,1:T(8,128)(2,1)}), bf16[256,704]{0,1:T(8,128)(2,1)}) %reduce-scatter.45.cloned.1.call-update) | async-done | bytes 360464 | tf_op jit(solution)/shard_map/reduce_scatter | solution.py:409
  2606.9 37.2 %all-reduce.15 = (bf16[2048]{0:T(1024)(128)(2,1)S(1)}, bf16[2048]{0:T(1024)(128)(2,1)S(1)}, bf16[512]{0:T(512)(128)(2,1)S(1)}, bf16[512]{0:T(512)(128)(2,1)S(1)}...) all-reduce(bf16[2048]{0:T(1024)(128)(2,1)S(1)} %get-tuple-element.2, ...), channel_id=5, replica_groups=mesh['expert'=8,'tensor'=4] {'expert'}, use_global_device_ids=true, to_apply=%region_49.51.clone | all-reduce | flops 9216 | bytes 36864
  2650.1 13.3 reduce-scatter.29.cloned.1.call-done
  2663.5 65.9 %reduce-scatter.31.cloned.1.call-done = bf16[64,1024]{1,0:T(8,128)(2,1)} async-done(((bf16[512,1024]{1,0:T(8,128)(2,1)}), bf16[64,1024]{1,0:T(8,128)(2,1)}) %reduce-scatter.31.cloned.1.call-update) | async-done | bytes 131088 | tf_op jit(solution)/shard_map/reduce_scatter | solution.py:394
  2731.1 68.6 %reduce-scatter.35.cloned.1.call-done = bf16[256,512]{1,0:T(8,128)(2,1)} async-done(((bf16[2048,512]{1,0:T(8,128)(2,1)}), bf16[256,512]{1,0:T(8,128)(2,1)}) %reduce-scatter.35.cloned.1.call-update) | async-done | bytes 262160 | tf_op jit(solution)/shard_map/reduce_scatter | solution.py:397
  2799.7 70.4 %reduce-scatter.33.cloned.1.call-done = bf16[256,512]{1,0:T(8,128)(2,1)} async-done(((bf16[2048,512]{1,0:T(8,128)(2,1)}), bf16[256,512]{1,0:T(8,128)(2,1)}) %reduce-scatter.33.cloned.1.call-update) | async-done | bytes 262160 | tf_op jit(solution)/shard_map/reduce_scatter | solution.py:397
  2872.0 70.6 %reduce-scatter.25.cloned.1.call-done = bf16[256,576]{0,1:T(8,128)(2,1)} async-done(((bf16[2048,576]{0,1:T(8,128)(2,1)}), bf16[256,576]{0,1:T(8,128)(2,1)}) %reduce-scatter.25.cloned.1.call-update) | async-done | bytes 294928 | tf_op jit(solution)/shard_map/reduce_scatter | solution.py:388
  2942.6 72.6 %reduce-scatter.27.cloned.1.call-done = bf16[256,576]{0,1:T(8,128)(2,1)} async-done(((bf16[2048,576]{0,1:T(8,128)(2,1)}), bf16[256,576]{0,1:T(8,128)(2,1)}) %reduce-scatter.27.cloned.1.call-update) | async-done | bytes 294928 | tf_op jit(solution)/shard_map/reduce_scatter | solution.py:388
  3017.1 75.3 %reduce-scatter.21.cloned.1.call-done = bf16[256,768]{1,0:T(8,128)(2,1)} async-done(((bf16[2048,768]{1,0:T(8,128)(2,1)}), bf16[256,768]{1,0:T(8,128)(2,1)}) %reduce-scatter.21.cloned.1.call-update) | async-done | bytes 393232 | tf_op jit(solution)/shard_map/reduce_scatter | solution.py:385
  3092.4 77.7 %reduce-scatter.23.cloned.1.call-done = bf16[256,768]{1,0:T(8,128)(2,1)} async-done(((bf16[2048,768]{1,0:T(8,128)(2,1)}), bf16[256,768]{1,0:T(8,128)(2,1)}) %reduce-scatter.23.cloned.1.call-update) | async-done | bytes 393232 | tf_op jit(solution)/shard_map/reduce_scatter | solution.py:385
  (614 shorter events, 384.3 us)
Async XLA Ops:
  7.2 876.4 %copy-start = (bf16[2,352,2048]{2,1,0:T(8,128)(2,1)S(1)}, bf16[2,352,2048]{2,1,0:T(8,128)(2,1)}, u32[]{:S(2)}) copy-start(bf16[2,352,2048]{2,1,0:T(8,128)(2,1)} %param.33) | copy-start | bytes 8650756
  7.2 31.3 all-gather.34.cloned.1.call-start
  25.8 32.7 %copy-start.147 = (s32[1536]{0:T(1024)}, s32[1536]{0:T(1024)S(1)}, u32[]{:S(2)}) copy-start(s32[1536]{0:T(1024)S(1)} %reshape.577) | copy-start | bytes 18436
  38.4 20.1 copy-start.118
  66.7 11.5 copy-start.121
  66.7 11.7 copy-start.109
  66.7 219.2 %all-to-all-start.6 = ((bf16[16,128,2048]{2,1,0:T(8,128)(2,1)}), bf16[16,128,2048]{2,1,0:T(8,128)(2,1)}, u32[]{:S(2)}, u32[]{:S(2)}) async-start(bf16[16,128,2048]{2,1,0:T(8,128)(2,1)} %fusion), calls=%async_computation.8 | async-start | bytes 16777216 | tf_op jit(solution)/shard_map/all_to_all | solution.py:262
  74.0 30.9 all-gather.32.cloned.1.call-start
  74.8 439.0 %all-gather.30.cloned.1.call-start = ((), (), s32[]{:S(2)}) async-start(), calls=%async_computation.33 | async-start | bytes 1310720 | tf_op jit(solution)/shard_map/all_gather | solution.py:133
  75.7 439.6 %all-gather.14.cloned.1.call-start = ((), (), s32[]{:S(2)}) async-start(), calls=%async_computation.24 | async-start | bytes 1310720 | tf_op jit(solution)/shard_map/all_gather | solution.py:133
  76.3 440.6 %all-gather.16.cloned.1.call-start = ((), (), s32[]{:S(2)}) async-start(), calls=%async_computation.25 | async-start | bytes 2654208 | tf_op jit(solution)/shard_map/all_gather | solution.py:150
  76.9 443.1 %all-gather.18.cloned.1.call-start = ((), (), s32[]{:S(2)}) async-start(), calls=%async_computation.26 | async-start | bytes 1179648 | tf_op jit(solution)/shard_map/all_gather | solution.py:152
  77.4 468.7 %all-gather.20.cloned.1.call-start = ((), (), s32[]{:S(2)}) async-start(), calls=%async_computation.27 | async-start | bytes 3538944 | tf_op jit(solution)/shard_map/all_gather | solution.py:149
  133.2 158.4 %copy-start.152 = (bf16[256]{0:T(256)(128)(2,1)S(1)}, bf16[256]{0:T(256)(128)(2,1)}, u32[]{:S(2)}) copy-start(bf16[256]{0:T(256)(128)(2,1)} %param.21) | copy-start | bytes 1540
  133.2 158.5 %copy-start.149 = (u32[32]{0:T(128)S(1)}, u32[32]{0:T(128)}, u32[]{:S(2)}) copy-start(u32[32]{0:T(128)} %constant.137) | copy-start | bytes 388
  133.2 159.7 %copy-start.153 = (bf16[64]{0:T(256)(128)(2,1)S(1)}, bf16[64]{0:T(256)(128)(2,1)}, u32[]{:S(2)}) copy-start(bf16[64]{0:T(256)(128)(2,1)} %param.24) | copy-start | bytes 388
  285.8 391.9 %all-to-all-start.4 = ((bf16[16,128,2048]{2,1,0:T(8,128)(2,1)}), bf16[16,128,2048]{2,1,0:T(8,128)(2,1)}, u32[]{:S(2)}, u32[]{:S(2)}) async-start(bf16[16,128,2048]{2,1,0:T(8,128)(2,1)} %fusion.1), calls=%async_computation.6 | async-start | bytes 16777216 | tf_op jit(solution)/shard_map/all_to_all | solution.py:262
  290.8 305.4 %all-gather.22.cloned.1.call-start = ((), (), s32[]{:S(2)}) async-start(), calls=%async_computation.28 | async-start | bytes 2359296 | tf_op jit(solution)/shard_map/all_gather | solution.py:153
  291.5 360.1 %all-reduce.31.cloned.1.call-start = ((), (), s32[]{:S(2)}) async-start(), calls=%async_computation.54 | async-start | bytes 4194304 | tf_op jit(solution)/shard_map/psum | solution.py:204
  452.0 78.1 %copy-start.112 = (f32[512]{0:T(512)}, f32[512]{0:T(512)S(1)}, u32[]{:S(2)}) copy-start(f32[512]{0:T(512)S(1)} %convert_element_type.417) | copy-start | bytes 6148
  512.5 37.5 %copy-start.97 = (f32[8,1,256]{2,1,0:T(1,128)}, f32[8,1,256]{2,1,0:T(1,128)S(1)}, u32[]{:S(2)}) copy-start(f32[8,1,256]{2,1,0:T(1,128)S(1)} %convert_element_type.545) | copy-start | bytes 24580
  526.2 10.3 copy-start.30
  537.4 14.2 copy-start.99
  537.4 14.2 copy-start.101
  537.4 12.5 copy-start.139
  554.2 47.2 %copy-start.70 = (bf16[4,128,256]{2,1,0:T(8,128)(2,1)}, bf16[4,128,256]{2,1,0:T(8,128)(2,1)S(1)}, u32[]{:S(2)}) copy-start(bf16[4,128,256]{2,1,0:T(8,128)(2,1)S(1)} %convolution_convert_fusion.27) | copy-start | bytes 786436
  554.6 46.8 %copy-start.71 = (bf16[4,128,256]{2,1,0:T(8,128)(2,1)}, bf16[4,128,256]{2,1,0:T(8,128)(2,1)S(1)}, u32[]{:S(2)}) copy-start(bf16[4,128,256]{2,1,0:T(8,128)(2,1)S(1)} %convolution_convert_fusion.26) | copy-start | bytes 786436
  630.6 27.4 copy-start.107
  677.7 188.6 %all-to-all-start.2 = ((bf16[16,128,2048]{2,1,0:T(8,128)(2,1)}), bf16[16,128,2048]{2,1,0:T(8,128)(2,1)}, u32[]{:S(2)}, u32[]{:S(2)}) async-start(bf16[16,128,2048]{2,1,0:T(8,128)(2,1)} %bitcast.308), calls=%async_computation.3 | async-start | bytes 16777216 | tf_op jit(solution)/shard_map/all_to_all | solution.py:219
  866.3 187.1 %all-to-all-start = ((bf16[16,128,2048]{2,1,0:T(8,128)(2,1)}), bf16[16,128,2048]{2,1,0:T(8,128)(2,1)}, u32[]{:S(2)}, u32[]{:S(2)}) async-start(bf16[16,128,2048]{2,1,0:T(8,128)(2,1)} %bitcast.307), calls=%async_computation | async-start | bytes 16777216 | tf_op jit(solution)/shard_map/all_to_all | solution.py:219
  1053.4 221.8 %all-to-all-start.7 = ((bf16[16,128,2048]{2,1,0:T(8,128)(2,1)}), bf16[16,128,2048]{2,1,0:T(8,128)(2,1)}, u32[]{:S(2)}, u32[]{:S(2)}) async-start(bf16[16,128,2048]{2,1,0:T(8,128)(2,1)} %bitcast.314), calls=%async_computation.9 | async-start | bytes 16777216 | tf_op jit(solution)/shard_map/all_to_all | solution.py:289
  1058.3 223.8 %all-gather.26.cloned.1.call-start = ((), (), s32[]{:S(2)}) async-start(), calls=%async_computation.30 | async-start | bytes 3244032 | tf_op jit(solution)/shard_map/all_gather | solution.py:156
  1275.2 318.8 %all-to-all-start.5 = ((bf16[16,128,2048]{2,1,0:T(8,128)(2,1)}), bf16[16,128,2048]{2,1,0:T(8,128)(2,1)}, u32[]{:S(2)}, u32[]{:S(2)}) async-start(bf16[16,128,2048]{2,1,0:T(8,128)(2,1)} %bitcast.311), calls=%async_computation.7 | async-start | bytes 16777216 | tf_op jit(solution)/shard_map/all_to_all | solution.py:289
  1280.3 184.5 %all-gather.24.cloned.1.call-start = ((), (), s32[]{:S(2)}) async-start(), calls=%async_computation.29 | async-start | bytes 3244032 | tf_op jit(solution)/shard_map/all_gather | solution.py:155
  1281.0 253.4 %all-gather.28.cloned.1.call-start = ((), (), s32[]{:S(2)}) async-start(), calls=%async_computation.31 | async-start | bytes 3244032 | tf_op jit(solution)/shard_map/all_gather | solution.py:157
  1281.6 417.9 %all-reduce.29.cloned.1.call-start = ((), (), s32[]{:S(2)}) async-start(), calls=%async_computation.53 | async-start | bytes 4194304 | tf_op jit(solution)/shard_map/psum | solution.py:309
  1282.1 273.0 %copy-start.46 = (s32[2048]{0:T(1024)}, s32[2048]{0:T(1024)S(1)}, u32[]{:S(2)}) copy-start(s32[2048]{0:T(1024)S(1)} %pad_clamp_fusion) | copy-start | bytes 24580
  1539.0 102.2 %copy-start.57 = (bf16[256,704]{0,1:T(8,128)(2,1)}, bf16[256,704]{0,1:T(8,128)(2,1)S(1)}, u32[]{:S(2)}) copy-start(bf16[256,704]{0,1:T(8,128)(2,1)S(1)} %get-tuple-element.63) | copy-start | bytes 1081348
  1646.4 53.1 %copy-start.108 = (f32[8,1,256]{2,1,0:T(1,128)S(1)}, f32[8,1,256]{2,1,0:T(1,128)}, u32[]{:S(2)}) copy-start(f32[8,1,256]{2,1,0:T(1,128)} %copy-done.107) | copy-start | bytes 24580
  1646.4 53.1 %copy-start.142 = (f32[256]{0:T(256)S(1)}, f32[256]{0:T(256)}, u32[]{:S(2)}) copy-start(f32[256]{0:T(256)} %copy-done.141) | copy-start | bytes 3076
  1648.4 54.7 %copy-start.146 = (f32[256]{0:T(256)S(1)}, f32[256]{0:T(256)}, u32[]{:S(2)}) copy-start(f32[256]{0:T(256)} %copy-done.145) | copy-start | bytes 3076
  1648.4 616.3 %all-reduce.27.cloned.1.call-start = ((), (), s32[]{:S(2)}) async-start(), calls=%async_computation.52 | async-start | bytes 5242880 | tf_op jit(solution)/shard_map/psum | solution.py:375
  1740.1 528.3 %all-reduce.25.cloned.1.call-start = ((), (), s32[]{:S(2)}) async-start(), calls=%async_computation.51 | async-start | bytes 131072 | tf_op jit(solution)/shard_map/psum | solution.py:369
  1743.6 539.7 %reduce-scatter.37.cloned.1.call-start = ((), (), s32[]{:S(2)}) async-start(), calls=%async_computation.45 | async-start | bytes 3244032 | tf_op jit(solution)/shard_map/reduce_scatter | solution.py:403
  1747.4 535.9 %reduce-scatter.39.cloned.1.call-start = ((), (), s32[]{:S(2)}) async-start(), calls=%async_computation.46 | async-start | bytes 3244032 | tf_op jit(solution)/shard_map/reduce_scatter | solution.py:403
  1768.7 212.0 %all-to-all-start.1 = ((bf16[16,128,2048]{2,1,0:T(8,128)(2,1)}), bf16[16,128,2048]{2,1,0:T(8,128)(2,1)}, u32[]{:S(2)}, u32[]{:S(2)}) async-start(bf16[16,128,2048]{2,1,0:T(8,128)(2,1)} %bitcast.313), calls=%async_computation.1 | async-start | bytes 16777216 | tf_op jit(solution)/shard_map/all_to_all | solution.py:231
  1774.4 540.1 %reduce-scatter.41.cloned.1.call-start = ((), (), s32[]{:S(2)}) async-start(), calls=%async_computation.47 | async-start | bytes 3244032 | tf_op jit(solution)/shard_map/reduce_scatter | solution.py:406
  1778.2 612.4 %reduce-scatter.43.cloned.1.call-start = ((), (), s32[]{:S(2)}) async-start(), calls=%async_computation.48 | async-start | bytes 3244032 | tf_op jit(solution)/shard_map/reduce_scatter | solution.py:406
  1980.8 222.0 %all-to-all-start.3 = ((bf16[16,128,2048]{2,1,0:T(8,128)(2,1)}), bf16[16,128,2048]{2,1,0:T(8,128)(2,1)}, u32[]{:S(2)}, u32[]{:S(2)}) async-start(bf16[16,128,2048]{2,1,0:T(8,128)(2,1)} %bitcast.312), calls=%async_computation.4 | async-start | bytes 16777216 | tf_op jit(solution)/shard_map/all_to_all | solution.py:231
  1985.9 480.2 %reduce-scatter.47.cloned.1.call-start = ((), (), s32[]{:S(2)}) async-start(), calls=%async_computation.50 | async-start | bytes 3244032 | tf_op jit(solution)/shard_map/reduce_scatter | solution.py:409
  1989.7 551.9 %reduce-scatter.45.cloned.1.call-start = ((), (), s32[]{:S(2)}) async-start(), calls=%async_computation.49 | async-start | bytes 3244032 | tf_op jit(solution)/shard_map/reduce_scatter | solution.py:409
  1993.6 594.9 %reduce-scatter.17.cloned.1.call-start = ((), (), s32[]{:S(2)}) async-start(), calls=%async_computation.32 | async-start | bytes 1310720 | tf_op jit(solution)/shard_map/reduce_scatter | solution.py:243
  2019.4 11.8 copy-start.82
  2042.7 553.6 %reduce-scatter.19.cloned.1.call-start = ((), (), s32[]{:S(2)}) async-start(), calls=%async_computation.34 | async-start | bytes 1310720 | tf_op jit(solution)/shard_map/reduce_scatter | solution.py:243
  2228.3 11.8 copy-start.80
  2251.7 411.8 %reduce-scatter.29.cloned.1.call-start = ((), (), s32[]{:S(2)}) async-start(), calls=%async_computation.41 | async-start | bytes 1179648 | tf_op jit(solution)/shard_map/reduce_scatter | solution.py:394
  2254.5 474.8 %reduce-scatter.31.cloned.1.call-start = ((), (), s32[]{:S(2)}) async-start(), calls=%async_computation.42 | async-start | bytes 1179648 | tf_op jit(solution)/shard_map/reduce_scatter | solution.py:394
  2257.1 542.5 %reduce-scatter.35.cloned.1.call-start = ((), (), s32[]{:S(2)}) async-start(), calls=%async_computation.44 | async-start | bytes 2359296 | tf_op jit(solution)/shard_map/reduce_scatter | solution.py:397
  2260.9 609.2 %reduce-scatter.33.cloned.1.call-start = ((), (), s32[]{:S(2)}) async-start(), calls=%async_computation.43 | async-start | bytes 2359296 | tf_op jit(solution)/shard_map/reduce_scatter | solution.py:397
  2264.7 677.9 %reduce-scatter.25.cloned.1.call-start = ((), (), s32[]{:S(2)}) async-start(), calls=%async_computation.39 | async-start | bytes 2654208 | tf_op jit(solution)/shard_map/reduce_scatter | solution.py:388
  2272.1 743.1 %reduce-scatter.27.cloned.1.call-start = ((), (), s32[]{:S(2)}) async-start(), calls=%async_computation.40 | async-start | bytes 2654208 | tf_op jit(solution)/shard_map/reduce_scatter | solution.py:388
  2277.7 814.7 %reduce-scatter.21.cloned.1.call-start = ((), (), s32[]{:S(2)}) async-start(), calls=%async_computation.37 | async-start | bytes 3538944 | tf_op jit(solution)/shard_map/reduce_scatter | solution.py:385
  2281.8 888.3 %reduce-scatter.23.cloned.1.call-start = ((), (), s32[]{:S(2)}) async-start(), calls=%async_computation.38 | async-start | bytes 3538944 | tf_op jit(solution)/shard_map/reduce_scatter | solution.py:385
  2567.6 13.6 slice-start
  (136 other events, 520.3 us)
Sparse Core Ops, SparseCore 0:
  10.2 19.4 all-gather.33
  77.0 18.1 all-gather.31
  97.4 16.7 all-gather.29
  116.1 16.7 all-gather.13
  134.8 153.3 all-gather.15
  290.1 195.9 all-gather.17
  488.3 57.7 all-gather.19
  548.2 47.9 all-gather.21
  601.6 50.0 all-reduce.30
  1061.1 182.3 all-gather.25
  1283.3 181.3 all-gather.23
  1466.9 67.4 all-gather.27
  1648.5 50.9 all-reduce.28
  1740.2 60.5 all-reduce.26
  1803.0 31.1 all-reduce.24
  1838.7 298.6 reduce-scatter.36
  2141.7 97.3 reduce-scatter.38
  2242.9 71.4 reduce-scatter.40
  2319.0 71.5 reduce-scatter.42
  2394.4 71.5 reduce-scatter.46
  2470.0 71.5 reduce-scatter.44
  2544.3 23.9 reduce-scatter.16
  2571.4 24.9 reduce-scatter.18
  2600.0 63.3 reduce-scatter.28
  2666.9 62.4 reduce-scatter.30
  2733.2 66.4 reduce-scatter.34
  2803.4 66.5 reduce-scatter.32
  2874.0 68.5 reduce-scatter.24
  2946.5 68.6 reduce-scatter.26
  3019.0 73.3 reduce-scatter.20
  3096.4 73.6 reduce-scatter.22
where the time goes:
time: 3190 us; the launch traced here: 3180 us
  waiting for transfers between devices  2100 us (66%)
  local copies, waits for them, and re-layouts  340 us (11%)
  blocking collectives  286 us (9%)
  matrix products  271 us (8%)
  other arithmetic  114 us (4%)
  starting transfers between devices  46.7 us (1%)
    all_to_all x2, waiting for transfers between devices, local(): lax.all_to_all(expert_part.reshape(experts_all, capacity, D), 'expert', s...  341 us
    all_to_all x2, waiting for transfers between devices, local(): lax.all_to_all(dispatched, 'expert', split_axis=0, concat_axis=0, tiled=T...  297 us
    unnamed x2, blocking collectives  196 us
    all_gather x1, waiting for transfers between devices, local(): lax.all_gather(shared_gate, 'expert', axis=0, tiled=True)  177 us
    all_to_all x2, waiting for transfers between devices, local(): lax.all_to_all(row_grad.reshape(experts_all, capacity, D), 'expert', spli...  168 us
    reduce_scatter x2, waiting for transfers between devices, local(): lax.psum_scatter(step_query.astype(jnp.bfloat16), 'expert', scatter_dimen...  153 us
    all_to_all x2, waiting for transfers between devices, local(): lax.all_to_all(slot_grad, 'expert', split_axis=0, concat_axis=0, tiled=True)  153 us
    reduce_scatter x2, waiting for transfers between devices, local(): lax.psum_scatter(step_sdown.astype(jnp.bfloat16), 'expert', scatter_dimen...  149 us
  transfers between devices with their start and end apart: 39, of which 25 were waited for; matrix products, arithmetic and copies ran while one was open for 19% of the time, Pallas kernels for 0%

commit v1 on v0

v1 whole, which is shorter than its diff:
```python
import functools
import math

import jax
import jax.numpy as jnp
from jax import lax
from jax.experimental import pallas as pl
from jax.experimental.pallas import tpu as pltpu
from jax.sharding import PartitionSpec as P

D = 2048
H = 16
DN = 128
DR = 64
DV = 128
KV_RANK = 512
TOP = 6
EXP_DEV = 2
SEQ = 256
BLOCK = 128

norm_eps = 1e-06
masked_value = -1000000000.0
BF = jnp.bfloat16
F32 = jnp.float32


def matmul(left, right):
    return jnp.dot(left, right, preferred_element_type=F32)


def matmul_rows(left, right):
    return lax.dot_general(left, right, (((1,), (1,)), ((), ())), preferred_element_type=F32)


def matmul_cols(left, right):
    return lax.dot_general(left, right, (((0,), (0,)), ((), ())), preferred_element_type=F32)


def rms_scale(values):
    return lax.rsqrt(jnp.mean(values * values, axis=-1, keepdims=True) + norm_eps)


def rope_tables(length, width):
    position = jnp.arange(length, dtype=F32)
    rates = jnp.exp(jnp.arange(width // 2, dtype=F32) * (-2.0 * math.log(10000.0) / width))
    angle = position[:, None] * rates[None, :]
    return (jnp.cos(angle), jnp.sin(angle))


def rotate(values, cosine, sine):
    half = values.shape[-1] // 2
    first = values[..., :half]
    second = values[..., half:]
    return jnp.concatenate(
        [first * cosine - second * sine, second * cosine + first * sine], axis=-1
    )


def unrotate(grads, cosine, sine):
    half = grads.shape[-1] // 2
    first = grads[..., :half]
    second = grads[..., half:]
    return jnp.concatenate(
        [first * cosine + second * sine, second * cosine - first * sine], axis=-1
    )


def norm_back(grad_hat, hat, scale_rows):
    return scale_rows * (grad_hat - hat * jnp.mean(grad_hat * hat, axis=-1, keepdims=True))


def expert_kernel(
    seqs, cap, tensors, slots, gates, x, og, wgu, wd, out, dgu, dd, xs, gs, parts, backs, acc_gu, acc_d, sems
):
    step = pl.program_id(0)
    width = x.shape[-1]
    half = wd.shape[1]

    @pl.when(step == 0)
    def _():
        acc_gu[...] = jnp.zeros_like(acc_gu)
        acc_d[...] = jnp.zeros_like(acc_d)

    iota = lax.broadcasted_iota(jnp.int32, (cap, SEQ), 0)
    picks = []
    slot_gates = []
    for s in range(seqs):
        chosen = []
        for e in range(EXP_DEV):
            row = s * EXP_DEV + e
            hit = iota == slots[0, row : row + 1, :]
            slot_gates.append(
                jnp.sum(jnp.where(hit, gates[0, row : row + 1, :], 0.0), axis=1, keepdims=True)
            )
            chosen.append(hit.astype(F32).astype(BF))
        picks.append(jnp.concatenate(chosen, axis=0))
    for s in range(seqs):
        for t in range(tensors):
            cols = slice(t * width, (t + 1) * width)
            rows = slice(s * SEQ, (s + 1) * SEQ)
            got = matmul(picks[s], x[0, t, rows, :])
            grad = matmul(picks[s], og[0, t, rows, :])
            for e in range(EXP_DEV):
                xs[e, s * cap : (s + 1) * cap, cols] = got[e * cap : (e + 1) * cap].astype(BF)
                gs[e, s * cap : (s + 1) * cap, cols] = (
                    grad[e * cap : (e + 1) * cap] * slot_gates[s * EXP_DEV + e]
                ).astype(BF)
    for e in range(EXP_DEV):
        gate_col = jnp.concatenate([slot_gates[s * EXP_DEV + e] for s in range(seqs)], axis=0)
        both = matmul(xs[e], wgu[e])
        gated = both[:, :half]
        upper = both[:, half:]
        sig = jax.nn.sigmoid(gated)
        act = gated * sig
        hidden = (act * upper).astype(BF)
        grad_hidden = matmul_rows(gs[e], wd[e])
        grad_gu = jnp.concatenate(
            [
                (grad_hidden * upper * sig * (1.0 + gated * (1.0 - sig))).astype(BF),
                (grad_hidden * act).astype(BF),
            ],
            axis=1,
        )
        part = (matmul(hidden, wd[e]) * gate_col).astype(BF)
        back = matmul_rows(grad_gu, wgu[e]).astype(BF)
        for s in range(seqs):
            parts[s, e * cap : (e + 1) * cap, :] = part[s * cap : (s + 1) * cap]
            backs[s, e * cap : (e + 1) * cap, :] = back[s * cap : (s + 1) * cap]
        acc_d[e] += matmul_cols(hidden, gs[e])
        acc_gu[e] += matmul_cols(xs[e], grad_gu)
    for s in range(seqs):
        for t in range(tensors):
            cols = slice(t * width, (t + 1) * width)
            rows = slice(s * SEQ, (s + 1) * SEQ)
            out[0, t, 0, rows, :] = matmul_cols(picks[s], parts[s, :, cols]).astype(BF)
            out[0, t, 1, rows, :] = matmul_cols(picks[s], backs[s, :, cols]).astype(BF)

    @pl.when(step == pl.num_programs(0) - 1)
    def _():
        first = pltpu.make_async_copy(acc_gu, dgu, sems.at[0])
        second = pltpu.make_async_copy(acc_d, dd, sems.at[1])
        first.start()
        second.start()
        first.wait()
        second.wait()


def run_experts(slots, gates, x, og, wgu, wd, cap):
    groups, tensors, count, width = x.shape
    seqs = count // SEQ
    half = wd.shape[1]
    rows = slots.shape[1]
    stream = lambda g: (g, 0, 0, 0)
    return pl.pallas_call(
        functools.partial(expert_kernel, seqs, cap, tensors),
        grid=(groups,),
        in_specs=[
            pl.BlockSpec((1, rows, SEQ), lambda g: (g, 0, 0)),
            pl.BlockSpec((1, rows, SEQ), lambda g: (g, 0, 0)),
            pl.BlockSpec((1, tensors, count, width), stream),
            pl.BlockSpec((1, tensors, count, width), stream),
            pl.BlockSpec(wgu.shape, lambda g: (0, 0, 0), pipeline_mode=pl.Buffered(1)),
            pl.BlockSpec(wd.shape, lambda g: (0, 0, 0), pipeline_mode=pl.Buffered(1)),
        ],
        out_specs=[
            pl.BlockSpec((1, tensors, 2, count, width), lambda g: (g, 0, 0, 0, 0)),
            pl.BlockSpec(memory_space=pl.ANY),
            pl.BlockSpec(memory_space=pl.ANY),
        ],
        out_shape=[
            jax.ShapeDtypeStruct((groups, tensors, 2, count, width), BF),
            jax.ShapeDtypeStruct(wgu.shape, F32),
            jax.ShapeDtypeStruct(wd.shape, F32),
        ],
        scratch_shapes=[
            pltpu.VMEM((EXP_DEV, seqs * cap, D), BF),
            pltpu.VMEM((EXP_DEV, seqs * cap, D), BF),
            pltpu.VMEM((seqs, EXP_DEV * cap, D), BF),
            pltpu.VMEM((seqs, EXP_DEV * cap, D), BF),
            pltpu.VMEM(wgu.shape, F32),
            pltpu.VMEM(wd.shape, F32),
            pltpu.SemaphoreType.DMA((2,)),
        ],
        compiler_params=pltpu.CompilerParams(
            dimension_semantics=("arbitrary",), vmem_limit_bytes=60 * 1024 * 1024
        ),
        cost_estimate=pl.CostEstimate(
            flops=groups * EXP_DEV * seqs * cap * D * (half * 18 + SEQ * 8),
            bytes_accessed=groups * tensors * count * width * 8 + wgu.size * 9,
            transcendentals=groups * EXP_DEV * seqs * cap * half,
        ),
        name="experts",
    )(slots, gates, x, og, wgu, wd)


def local(
    hidden_in,
    out_grad,
    first_gain,
    query_weight,
    latent_weight,
    latent_gain,
    expand_weight,
    output_weight,
    second_gain,
    shared_gate,
    shared_up,
    shared_down,
    expert_gate,
    expert_up,
    expert_down,
    routes,
    gate_values,
):
    groups = lax.axis_size("expert")
    tensors = lax.axis_size("tensor")
    place = lax.axis_index("tensor")
    mine = lax.axis_index("expert")
    experts_all = EXP_DEV * groups
    cap = SEQ * TOP * 4 // (3 * experts_all)
    width = D // tensors
    heads = H // tensors
    count = hidden_in.shape[0]
    seqs = count // SEQ
    rows_dev = D // groups
    scale = (DN + DR) ** (-0.5)
    cosine, sine = rope_tables(SEQ, DR)
    blocks = jnp.arange(SEQ, dtype=jnp.int32) // BLOCK
    allowed = (blocks[None, :] <= blocks[:, None])[None, None]

    whole_in = lax.all_gather(hidden_in, "tensor", axis=1, tiled=True)
    qc = query_weight.shape[1]
    oc = output_weight.shape[1]
    lc = latent_weight.shape[1]
    sc = shared_gate.shape[1]
    er, ec = expand_weight.shape
    cut = er * ec // rows_dev
    fold = rows_dev // er
    expand_rows = jnp.concatenate(
        [expand_weight[:, i * cut : (i + 1) * cut] for i in range(fold)], axis=0
    )
    attn_all = lax.all_gather(
        jnp.concatenate([query_weight, output_weight, expand_rows, latent_weight], axis=1),
        "expert",
        axis=0,
        tiled=True,
    )
    full_query = attn_all[:, :qc]
    full_output = attn_all[:, qc : qc + oc]
    full_latent = attn_all[:, qc + oc + cut :]
    full_expand = (
        attn_all[:, qc + oc : qc + oc + cut]
        .reshape(groups, fold, er, cut)
        .transpose(0, 2, 1, 3)
        .reshape(groups * er, ec)
    )
    gains = lax.all_gather(
        jnp.concatenate([first_gain, second_gain, latent_gain]).astype(F32), "expert", axis=0
    )
    gain_first = gains[:, :rows_dev].reshape(-1)
    gain_mid = gains[:, rows_dev : 2 * rows_dev].reshape(-1)
    gain_kv = gains[:, 2 * rows_dev :].reshape(-1)
    table = lax.all_gather(
        jnp.concatenate([routes.T.astype(F32), gate_values.T], axis=0), "expert", axis=0
    )
    pieces = max(1, min(seqs, groups // 8))
    per = count // pieces

    def to_all(rows):
        return lax.all_gather(rows, ("expert", "tensor"), axis=0).reshape(
            groups, tensors, per, width
        )

    og_first = to_all(out_grad[:per])
    shared_all = lax.all_gather(
        jnp.concatenate([shared_gate, shared_up, shared_down], axis=1), "expert", axis=0, tiled=True
    )
    full_sgu = shared_all[:, : 2 * sc]
    full_sdown = shared_all[:, 2 * sc :]

    inputs = whole_in.astype(F32)
    first_scale = rms_scale(inputs)
    first_hat = inputs * first_scale
    normed = (first_hat * gain_first).astype(BF)
    query = matmul(normed, full_query).reshape(seqs, SEQ, heads, DN + DR)
    latent = matmul(normed, full_latent)
    compressed = latent[:, :KV_RANK]
    latent_scale = rms_scale(compressed)
    latent_hat = compressed * latent_scale
    latent_normed = (latent_hat * gain_kv).astype(BF)
    expanded = matmul(latent_normed, full_expand).reshape(seqs, SEQ, heads, DN + DV)
    queries = jnp.concatenate(
        [query[..., :DN], rotate(query[..., DN:], cosine[:, None, :], sine[:, None, :])], axis=-1
    ).astype(BF)
    key_rope = rotate(latent[:, KV_RANK:].reshape(seqs, SEQ, DR), cosine, sine).astype(BF)
    keys = jnp.concatenate(
        [
            expanded[..., :DN].astype(BF),
            jnp.broadcast_to(key_rope[:, :, None, :], (seqs, SEQ, heads, DR)),
        ],
        axis=-1,
    )
    values = expanded[..., DN:].astype(BF)
    scores = jnp.where(
        allowed,
        jnp.einsum("nqhc,nkhc->nhqk", queries, keys, preferred_element_type=F32) * scale,
        masked_value,
    )
    peak = jnp.max(scores, axis=-1, keepdims=True)
    log_total = peak + jnp.log(jnp.sum(jnp.exp(scores - peak), axis=-1, keepdims=True))
    weights = jnp.exp(scores - log_total)
    mixed = (
        jnp.einsum("nhqk,nkhc->nqhc", weights.astype(BF), values, preferred_element_type=F32)
        .astype(BF)
        .reshape(count, heads * DV)
    )
    attended = lax.psum(matmul_rows(mixed, full_output).astype(BF), "tensor").astype(F32)
    middle = inputs + attended
    second_scale = rms_scale(middle)
    second_hat = middle * second_scale
    mixer_in = (second_hat * gain_mid).astype(BF)
    mixer_slice = lax.dynamic_slice_in_dim(mixer_in, place * width, width, 1)

    local_experts = (mine * EXP_DEV + jnp.arange(EXP_DEV, dtype=jnp.int32)).astype(F32)
    route_t = table[:, :TOP].reshape(groups, TOP, seqs, SEQ)
    gate_t = table[:, TOP:].reshape(groups, TOP, seqs, SEQ)
    named = route_t[:, :, :, None, :] == local_experts[None, None, None, :, None]
    gate_of = jnp.sum(jnp.where(named, gate_t[:, :, :, None, :], 0.0), axis=1)
    used = jnp.any(named, axis=1)
    before = (
        jnp.arange(SEQ, dtype=jnp.int32)[:, None] < jnp.arange(SEQ, dtype=jnp.int32)[None, :]
    ).astype(BF)
    prior = jnp.einsum("gset,tu->gseu", used.astype(BF), before, preferred_element_type=F32)
    slot_of = jnp.where(used & (prior < cap), prior, -1.0).astype(jnp.int32)
    slot_of = slot_of.reshape(groups, seqs * EXP_DEV, SEQ)
    gate_of = gate_of.reshape(groups, seqs * EXP_DEV, SEQ)

    ff = expert_gate.shape[2]
    half = -(-ff // 128) * 128
    wide = ((0, 0), (0, 0), (0, half - ff))
    wgu = jnp.concatenate([jnp.pad(expert_gate, wide), jnp.pad(expert_up, wide)], axis=2)
    wd = jnp.pad(expert_down, ((0, 0), (0, half - ff), (0, 0)))
    rows = slot_of.shape[1] // pieces
    sums = []
    dgu = dd = None
    for i in range(pieces):
        span = slice(i * per, (i + 1) * per)
        mixer_rows, og_rows = mixer_slice[span], out_grad[span]
        if i > 0:
            mixer_rows, og_rows, *sums = lax.optimization_barrier((mixer_rows, og_rows, *sums))
        outs, g_gu, g_d = run_experts(
            slot_of[:, i * rows : (i + 1) * rows],
            gate_of[:, i * rows : (i + 1) * rows],
            to_all(mixer_rows),
            og_first if i == 0 else to_all(og_rows),
            wgu,
            wd,
            cap,
        )
        dgu = g_gu if dgu is None else dgu + g_gu
        dd = g_d if dd is None else dd + g_d
        summed = lax.psum_scatter(
            outs.reshape(groups * tensors * 2 * per, width),
            ("expert", "tensor"),
            scatter_dimension=0,
            tiled=True,
        )
        sums.append(summed.reshape(2, per, width))
    summed = jnp.concatenate(sums, axis=1) if pieces > 1 else sums[0]
    total_gate = dgu[:, :, :ff]
    total_up = dgu[:, :, half : half + ff]
    total_down = dd[:, :ff]

    if pieces == 1:
        whole_grad = lax.dynamic_slice_in_dim(og_first, mine, 1, 0)[0]
        whole_grad = whole_grad.transpose(1, 0, 2).reshape(count, D)
    else:
        whole_grad = lax.all_gather(out_grad, "tensor", axis=1, tiled=True)
    shared_gu = matmul(mixer_in, full_sgu)
    shared_g = shared_gu[:, :sc]
    shared_u = shared_gu[:, sc:]
    shared_sig = jax.nn.sigmoid(shared_g)
    shared_hidden = (shared_g * shared_sig * shared_u).astype(BF)
    shared_part = matmul_rows(shared_hidden, full_sdown)
    grad_shared = matmul(whole_grad, full_sdown)
    step_sdown = matmul_cols(whole_grad, shared_hidden)
    grad_sg = (grad_shared * shared_u * shared_sig * (1.0 + shared_g * (1.0 - shared_sig))).astype(
        BF
    )
    grad_su = (grad_shared * shared_g * shared_sig).astype(BF)
    grad_sgu = jnp.concatenate([grad_sg, grad_su], axis=1)
    step_sgu = matmul_cols(mixer_in, grad_sgu)
    mixer_part = matmul_rows(grad_sgu, full_sgu)
    shared_sums = lax.psum_scatter(
        jnp.concatenate([shared_part.astype(BF), mixer_part.astype(BF)], axis=0),
        "tensor",
        scatter_dimension=1,
        tiled=True,
    )
    middle_slice = lax.dynamic_slice_in_dim(middle, place * width, width, 1)
    block_out = (
        middle_slice + summed[0].astype(F32) + shared_sums[:count].astype(F32)
    ).astype(BF)
    grad_mixer = lax.all_gather(
        (summed[1].astype(F32) + shared_sums[count:].astype(F32)).astype(BF),
        "tensor",
        axis=1,
        tiled=True,
    ).astype(F32)
    shared_steps = lax.psum_scatter(
        jnp.concatenate([step_sgu.astype(BF), step_sdown.astype(BF)], axis=1),
        "expert",
        scatter_dimension=0,
        tiled=True,
    ).astype(F32)

    step_gain_two = jnp.sum(grad_mixer * second_hat, axis=0)
    grad_middle = whole_grad.astype(F32) + norm_back(
        grad_mixer * gain_mid, second_hat, second_scale
    )
    grad_att = grad_middle.astype(BF)
    step_output = matmul_cols(grad_att, mixed)
    grad_mixed = matmul(grad_att, full_output).astype(BF).reshape(seqs, SEQ, heads, DV)
    grad_weights = jnp.einsum(
        "nqhc,nkhc->nhqk", grad_mixed, values, preferred_element_type=F32
    )
    grad_scores = (
        weights * (grad_weights - jnp.sum(weights * grad_weights, axis=-1, keepdims=True))
    ).astype(BF)
    grad_values = jnp.einsum(
        "nhqk,nqhc->nkhc", weights.astype(BF), grad_mixed, preferred_element_type=F32
    )
    grad_queries = (
        jnp.einsum("nhqk,nkhc->nqhc", grad_scores, keys, preferred_element_type=F32) * scale
    )
    grad_keys = (
        jnp.einsum("nhqk,nqhc->nkhc", grad_scores, queries, preferred_element_type=F32) * scale
    )
    grad_query = (
        jnp.concatenate(
            [
                grad_queries[..., :DN],
                unrotate(grad_queries[..., DN:], cosine[:, None, :], sine[:, None, :]),
            ],
            axis=-1,
        )
        .astype(BF)
        .reshape(count, heads * (DN + DR))
    )
    step_query = matmul_cols(normed, grad_query)
    query_part = matmul_rows(grad_query, full_query)
    rope_part = unrotate(jnp.sum(grad_keys[..., DN:], axis=2), cosine, sine).reshape(count, DR)
    grad_expanded = (
        jnp.concatenate([grad_keys[..., :DN], grad_values], axis=-1)
        .astype(BF)
        .reshape(count, heads * (DN + DV))
    )
    step_expand = matmul_cols(latent_normed, grad_expanded)
    latent_part = matmul_rows(grad_expanded, full_expand)
    latent_sum = lax.psum(
        jnp.concatenate([latent_part.astype(BF), rope_part.astype(BF)], axis=1), "tensor"
    ).astype(F32)
    grad_lnormed = latent_sum[:, :KV_RANK]
    step_gain_latent = jnp.sum(grad_lnormed * latent_hat, axis=0)
    grad_compressed = norm_back(grad_lnormed * gain_kv, latent_hat, latent_scale)
    grad_lat = jnp.concatenate([grad_compressed, latent_sum[:, KV_RANK:]], axis=-1).astype(BF)
    step_latent = matmul_cols(normed, grad_lat)
    query_sum = lax.psum_scatter(
        query_part.astype(BF), "tensor", scatter_dimension=1, tiled=True
    ).astype(F32)
    latent_slice = lax.dynamic_slice_in_dim(full_latent, place * width, width, 0)
    grad_normed = query_sum + matmul_rows(grad_lat, latent_slice)
    first_hat_slice = lax.dynamic_slice_in_dim(first_hat, place * width, width, 1)
    gain_first_slice = lax.dynamic_slice_in_dim(gain_first, place * width, width, 0)
    grad_hat = grad_normed * gain_first_slice
    row_dot = lax.psum(jnp.sum(grad_hat * first_hat_slice, axis=1), "tensor") / D
    grad_middle_slice = lax.dynamic_slice_in_dim(grad_middle, place * width, width, 1)
    input_grad = grad_middle_slice + first_scale * (grad_hat - first_hat_slice * row_dot[:, None])
    step_gain_one = jnp.sum(grad_normed * first_hat_slice, axis=0)

    expand_back = (
        step_expand.astype(BF)
        .reshape(groups, er, fold, cut)
        .transpose(0, 2, 1, 3)
        .reshape(groups * rows_dev, cut)
    )
    attn_steps = lax.psum_scatter(
        jnp.concatenate(
            [step_query.astype(BF), step_output.astype(BF), expand_back, step_latent.astype(BF)],
            axis=1,
        ),
        "expert",
        scatter_dimension=0,
        tiled=True,
    ).astype(F32)
    grad_expand = attn_steps[:, qc + oc : qc + oc + cut]
    grad_expand = jnp.concatenate(
        [grad_expand[i * er : (i + 1) * er] for i in range(fold)], axis=1
    )
    one_full = lax.dynamic_update_slice_in_dim(
        jnp.zeros((D,), F32), step_gain_one, place * width, 0
    )
    gain_sums = lax.psum(
        jnp.concatenate([one_full, step_gain_two / tensors, step_gain_latent / tensors]),
        ("expert", "tensor"),
    )
    kv_dev = latent_gain.shape[0]
    return (
        block_out,
        input_grad,
        lax.dynamic_slice_in_dim(gain_sums, mine * rows_dev, rows_dev, 0),
        attn_steps[:, :qc],
        attn_steps[:, qc + oc + cut :],
        lax.dynamic_slice_in_dim(gain_sums, 2 * D + mine * kv_dev, kv_dev, 0),
        grad_expand,
        attn_steps[:, qc : qc + oc],
        lax.dynamic_slice_in_dim(gain_sums, D + mine * rows_dev, rows_dev, 0),
        shared_steps[:, :sc],
        shared_steps[:, sc : 2 * sc],
        shared_steps[:, 2 * sc :],
        total_gate,
        total_up,
        total_down,
    )


def solution(mesh):
    both = P("expert", "tensor")
    cols = P("expert", None, "tensor")
    rows = P("expert", "tensor", None)
    one = P("expert")
    flat = P("expert", None)
    return jax.shard_map(
        local,
        mesh=mesh,
        in_specs=(
            both, both, one, both, flat, one, both, both, one, both, both, both,
            cols, cols, rows, flat, flat,
        ),
        out_specs=(
            both, both, one, both, flat, one, both, both, one, both, both, both,
            cols, cols, rows,
        ),
        check_vma=False,
    )
```

time: 3190 us -> 1530 us (0.48)
  waiting for transfers between devices: 2100 us -> 1060 us
  local copies, waits for them, and re-layouts: 340 us -> 103 us
  matrix products: 271 us -> 72.7 us
  blocking collectives: 286 us -> 114 us
  Pallas kernels: 0 us -> 98.7 us
  other arithmetic: 114 us -> 55.5 us
  starting transfers between devices: 46.7 us -> 1.45 us
    all_to_all x8 -> x0, waiting for transfers between devices: 959 us -> none  [the longest x2 341 us: local(): lax.all_to_all(expert_part.reshape(experts_all, capacity, D), 'expert', s...]
    unnamed x2 -> x0, blocking collectives: 196 us -> none
    reduce_scatter x16 -> x5, waiting for transfers between devices: 775 us -> 596 us  [the longest x1 352 us: local(): lax.psum_scatter(outs.reshape(groups * tensors * 2 * per, width), ('exper...]
    gather x14 -> x0, local copies, waits for them, and re-layouts: 161 us -> none  [the longest x2 35.4 us: local(): dispatched = padded_in[owners].reshape(experts_all, capacity, D)]
    dot_general x44 -> x13, matrix products: 187 us -> 30.7 us  [the longest x6 24.7 us: matmul(): return jnp.dot(left, right, preferred_element_type=F32)]
    all_gather x11 -> x6, waiting for transfers between devices: 291 us -> 420 us  [the longest x2 189 us: to_all(): lax.all_gather(rows, ('expert', 'tensor'), axis=0)]
    pallas_call x0 -> x1, Pallas kernels: none -> 98.7 us  [run_experts(): pl.pallas_call(functools.partial(expert_kernel, seqs, cap, tensors), grid...]
    convert_element_type x8 -> x3, local copies, waits for them, and re-layouts: 80.5 us -> 2.67 us  [the longest x1 2.38 us: local(): grad_expanded = jnp.concatenate([grad_keys[..., :DN], grad_values], axis=...]
  transfers between devices with their start and end apart: 39 -> 13, of which waited for: 25 -> 10; matrix products, arithmetic and copies ran while one was open for 19% -> 10% of each run, Pallas kernels for 0% -> 6%
where the time goes in v1:
time: 1530 us; the launch traced here: 1520 us
  waiting for transfers between devices  1060 us (69%)
  blocking collectives  114 us (7%)
  local copies, waits for them, and re-layouts  103 us (7%)
  Pallas kernels  98.7 us (6%)
  matrix products  72.7 us (5%)
  other arithmetic  55.5 us (4%)
  between operations  15.3 us (1%)
    reduce_scatter x1, waiting for transfers between devices, local(): lax.psum_scatter(outs.reshape(groups * tensors * 2 * per, width), ('exper...  352 us
    all_gather x2, waiting for transfers between devices, to_all(): lax.all_gather(rows, ('expert', 'tensor'), axis=0)  189 us
    all_gather x1, waiting for transfers between devices, local(): lax.all_gather(jnp.concatenate([query_weight, output_weight, expand_rows,...  121 us
    reduce_scatter x1, waiting for transfers between devices, local(): lax.psum_scatter(jnp.concatenate([step_sgu.astype(BF), step_sdown.astype(...  113 us
    reduce_scatter x1, waiting for transfers between devices, local(): lax.psum_scatter(jnp.concatenate([step_query.astype(BF), step_output.asty...  102 us
    pallas_call x1, Pallas kernels, run_experts(): pl.pallas_call(functools.partial(expert_kernel, seqs, cap, tensors), grid...  98.7 us
    all_gather x1, waiting for transfers between devices, local(): lax.all_gather(jnp.concatenate([shared_gate, shared_up, shared_down], axi...  95.3 us
    psum x1, waiting for transfers between devices, local(): lax.psum(matmul_rows(mixed, full_output).astype(BF), 'tensor').astype(F32)  46.5 us
  transfers between devices with their start and end apart: 13, of which 10 were waited for; matrix products, arithmetic and copies ran while one was open for 10% of the time, Pallas kernels for 6%

profile of v1, /device:TPU:0, one launch (start us, length us, event | category | flops | bytes accessed | tf_op | source)
XLA Modules:
  0.0 1523.8 jit_solution(5023507900146481199)
XLA Ops:
  10.0 2.2 pad_maximum_fusion.4
  12.3 32.0 %all-gather.3 = f32[8,1,576]{2,1,0:T(1,128)S(1)} all-gather(f32[1,1,576]{2,1,0:T(1,128)S(1)} %fusion.57), channel_id=1, replica_groups=mesh['expert'=8,'tensor'=4] {'expert'}, dimensions={0}, use_global_device_ids=true | all-gather | bytes 20736 | tf_op jit(solution)/shard_map/all_gather | solution.py:258
  46.0 2.2 fusion.13
  48.2 121.1 %all-gather.14.cloned.1.call-done = bf16[2048,2112]{1,0:T(8,128)(2,1)} async-done(((bf16[256,2112]{1,0:T(8,128)(2,1)}), bf16[2048,2112]{1,0:T(8,128)(2,1)}) %all-gather.14.cloned.1.call-update) | async-done | bytes 8650768 | tf_op jit(solution)/shard_map/all_gather | solution.py:243
  169.4 4.0 fusion.66
  175.4 3.1 fusion.18
  178.5 3.0 reshape.347
  181.5 1.9 fusion.69
  183.5 2.4 slice.237
  185.8 1.6 reshape.348
  191.2 2.1 copy.179
  195.8 2.2 convolution_convert_fusion.9
  201.8 4.4 convolution_convert_fusion.7
  209.5 46.5 %all-reduce.6.cloned.1.call-done = bf16[512,2048]{1,0:T(8,128)(2,1)} async-done(((bf16[512,2048]{1,0:T(8,128)(2,1)}), bf16[512,2048]{1,0:T(8,128)(2,1)}) %all-reduce.6.cloned.1.call-update) | async-done | bytes 2097168 | tf_op jit(solution)/shard_map/psum | solution.py:318
  256.0 4.5 convert_multiply_fusion
  263.8 31.9 %all-gather.4 = f32[8,12,512]{2,1,0:T(8,128)S(1)} all-gather(f32[1,12,512]{2,1,0:T(8,128)S(1)} %maximum_bitcast_fusion.1), channel_id=2, replica_groups=mesh['expert'=8,'tensor'=4] {'expert'}, dimensions={0}, use_global_device_ids=true | all-gather | bytes 221184 | tf_op jit(solution)/shard_map/all_gather | solution.py:264
  295.8 95.3 %all-gather.16.cloned.1.call-done = bf16[2048,2112]{0,1:T(8,128)(2,1)} async-done(((bf16[256,2112]{0,1:T(8,128)(2,1)}), bf16[2048,2112]{0,1:T(8,128)(2,1)}) %all-gather.16.cloned.1.call-update) | async-done | bytes 8650768 | tf_op jit(solution)/shard_map/all_gather | solution.py:276
  391.0 8.3 fusion.5
  399.3 107.9 %all-gather.22.cloned.1.call-done = bf16[16384,512]{1,0:T(8,128)(2,1)} async-done(((bf16[512,512]{1,0:T(8,128)(2,1)}), bf16[16384,512]{1,0:T(8,128)(2,1)}) %all-gather.22.cloned.1.call-update) | async-done | bytes 16777232 | tf_op jit(solution)/shard_map/all_gather | solution.py:271
  507.3 1.9 dynamic-slice_bitcast_fusion
  509.7 5.0 multiply_convert_fusion.4
  514.8 1.8 convolution_convert_fusion.6
  516.7 3.7 fusion.14
  520.4 2.6 pad_maximum_fusion.2
  524.9 4.6 copy.149
  529.5 4.6 copy.150
  534.1 4.1 pad.13.wd
  538.2 5.2 fusion.2.wgu
  543.4 80.6 %all-gather.20.cloned.1.call-done = bf16[16384,512]{1,0:T(8,128)(2,1)} async-done(((bf16[512,512]{1,0:T(8,128)(2,1)}), bf16[16384,512]{1,0:T(8,128)(2,1)}) %all-gather.20.cloned.1.call-update) | async-done | bytes 16777232 | tf_op jit(solution)/shard_map/all_gather | solution.py:271
  624.0 98.7 %experts.1 = (bf16[8,4,2,512,512]{4,3,2,1,0:T(8,128)(2,1)}, f32[2,2048,768]{2,1,0:T(8,128)}, f32[2,384,2048]{2,1,0:T(8,128)}) custom-call(s32[8,4,256]{2,1,0:T(4,128)} %copy.182.slots, f32[8,4,256]{2,1,0:T(4,128)} %copy.185.gates, bf16[8,4,512,512]{3,2,1,0:T(8,128)(2,1)} %bitcast.152, bf16[8,4,512,512]{3,2,1,0:T(8,128)(2,1)} %bitcast.131, ...), custom_call_target="tpu_custom_call" | custom-call | flops 75161927680 | bytes 95420416 | tf_op jit(solution)/shard_map/experts/pallas_call | solution.py:155
  722.9 352.3 %reduce-scatter.6.cloned.1.call-done = bf16[1024,512]{1,0:T(8,128)(2,1)} async-done(((bf16[32768,512]{1,0:T(8,128)(2,1)}), bf16[1024,512]{1,0:T(8,128)(2,1)}) %reduce-scatter.6.cloned.1.call-update) | async-done | bytes 1048592 | tf_op jit(solution)/shard_map/reduce_scatter | solution.py:363
  1075.2 2.1 add_convert_fusion
  1077.8 5.0 convolution_convert_fusion.2
  1082.9 5.8 convolution_convert_fusion
  1088.7 14.9 all-gather.18.cloned.1.call-done
  1103.6 3.9 fusion.12
  1107.7 4.3 fusion.11
  1112.1 2.0 copy-done.3
  1114.1 2.0 fusion.27
  1117.6 2.2 convolution_bitcast_fusion
  1123.4 2.4 copy.161
  1129.3 7.3 pad_maximum_fusion.1
  1141.0 5.1 convolution_convert_fusion.5
  1146.3 2.9 convolution_convert_fusion.8
  1149.3 1.9 reshape.357
  1152.3 2.3 copy.164
  1154.6 4.9 convolution_convert_fusion.4
  1159.6 3.6 convolution_convert_fusion.1
  1167.6 1.5 convolution_convert_fusion.3
  1170.5 4.2 pad_maximum_fusion
  1174.7 3.5 slice.231
  1178.2 10.1 fusion.68
  1188.3 6.4 copy.168
  1194.7 6.5 copy.169
  1201.2 5.9 slice.229
  1207.1 113.3 %reduce-scatter.14.cloned.1.call-done = bf16[256,2112]{0,1:T(8,128)(2,1)} async-done(((bf16[2048,2112]{0,1:T(8,128)(2,1)}), bf16[256,2112]{0,1:T(8,128)(2,1)}) %reduce-scatter.14.cloned.1.call-update) | async-done | bytes 1081360 | tf_op jit(solution)/shard_map/reduce_scatter | solution.py:411
  1320.4 2.6 fusion.70
  1323.0 2.3 add_convert_fusion.1
  1325.3 28.1 %reduce-scatter.10.cloned.1.call-done = bf16[512,512]{1,0:T(8,128)(2,1)} async-done(((bf16[512,2048]{1,0:T(8,128)(2,1)}), bf16[512,512]{1,0:T(8,128)(2,1)}) %reduce-scatter.10.cloned.1.call-update) | async-done | bytes 524304 | tf_op jit(solution)/shard_map/reduce_scatter | solution.py:469
  1353.4 2.4 multiply_reduce_fusion.2
  1356.1 42.8 %psum.31 = f32[4608]{0:T(1024)S(1)} all-reduce(f32[4608]{0:T(1024)S(1)} %pad_maximum_fusion.21), channel_id=1, replica_groups=mesh['expert'=8,'tensor'=4] {'expert','tensor'}, use_global_device_ids=true, to_apply=%region_21.22 | all-reduce | flops 4608 | bytes 36864 | tf_op jit(solution)/shard_map/psum | solution.py:504
  1399.5 7.0 psum.30
  1407.1 2.8 multiply_add_fusion
  1409.9 102.1 %reduce-scatter.12.cloned.1.call-done = bf16[256,2112]{0,1:T(8,128)(2,1)} async-done(((bf16[2048,2112]{0,1:T(8,128)(2,1)}), bf16[256,2112]{0,1:T(8,128)(2,1)}) %reduce-scatter.12.cloned.1.call-update) | async-done | bytes 1081360 | tf_op jit(solution)/shard_map/reduce_scatter | solution.py:488
  (288 shorter events, 52.5 us)
Async XLA Ops:
  7.2 38.8 %all-gather.12.cloned.1.call-start = ((), (), s32[]{:S(2)}) async-start(), calls=%async_computation.5 | async-start | bytes 2621440 | tf_op jit(solution)/shard_map/all_gather | solution.py:232
  7.9 4.3 copy-start.67
  7.9 4.3 copy-start.68
  7.9 4.3 copy-start.66
  7.9 161.4 %all-gather.14.cloned.1.call-start = ((), (), s32[]{:S(2)}) async-start(), calls=%async_computation.6 | async-start | bytes 10027008 | tf_op jit(solution)/shard_map/all_gather | solution.py:243
  12.2 243.8 %all-reduce.6.cloned.1.call-start = ((), (), s32[]{:S(2)}) async-start(), calls=%async_computation.7 | async-start | bytes 4194304 | tf_op jit(solution)/shard_map/psum | solution.py:318
  44.3 130.4 %copy-start.64 = (f32[1,2,8,128]{3,1,2,0:T(2,128)}, f32[1,2,8,128]{3,1,2,0:T(2,128)S(1)}, u32[]{:S(2)}) copy-start(f32[1,2,8,128]{3,1,2,0:T(2,128)S(1)} %copy.194) | copy-start | bytes 24580
  44.4 145.3 %copy-start.56 = (f32[512]{0:T(512)}, f32[512]{0:T(512)S(1)}, u32[]{:S(2)}) copy-start(f32[512]{0:T(512)S(1)} %mul.506) | copy-start | bytes 6148
  48.2 207.7 %copy-start.60 = (f32[512]{0:T(512)}, f32[512]{0:T(512)S(1)}, u32[]{:S(2)}) copy-start(f32[512]{0:T(512)S(1)} %add_rsqrt_fusion.2) | copy-start | bytes 6148
  169.4 5.4 copy-start
  169.4 6.1 copy-start.17
  173.4 16.3 %copy-start.7 = (f32[512,576]{0,1:T(8,128)}, f32[512,576]{0,1:T(8,128)S(1)}, u32[]{:S(2)}) copy-start(f32[512,576]{0,1:T(8,128)S(1)} %fusion.66) | copy-start | bytes 3538948
  194.4 3.6 copy-start.15
  195.8 2.3 copy-start.26
  195.8 2.4 copy-start.34
  195.8 2.4 copy-start.36
  195.8 2.4 copy-start.47
  195.8 2.5 copy-start.48
  195.8 2.5 copy-start.31
  201.8 4.4 copy-start.24
  206.2 184.8 %all-gather.16.cloned.1.call-start = ((), (), s32[]{:S(2)}) async-start(), calls=%async_computation.9 | async-start | bytes 9732096 | tf_op jit(solution)/shard_map/all_gather | solution.py:276
  208.5 298.8 %all-gather.22.cloned.1.call-start = ((), (), s32[]{:S(2)}) async-start(), calls=%async_computation.17 | async-start | bytes 17301504 | tf_op jit(solution)/shard_map/all_gather | solution.py:271
  209.1 415.0 %all-gather.20.cloned.1.call-start = ((), (), s32[]{:S(2)}) async-start(), calls=%async_computation.16 | async-start | bytes 17301504 | tf_op jit(solution)/shard_map/all_gather | solution.py:271
  256.0 4.5 copy-start.4
  260.5 3.3 copy-start.62
  260.5 3.3 copy-start.63
  263.7 459.1 %reduce-scatter.8.cloned.1.call-start = ((), (), s32[]{:S(2)}) async-start(), calls=%async_computation.10 | async-start | bytes 5242880 | tf_op jit(solution)/shard_map/reduce_scatter | solution.py:395
  507.3 2.4 copy-start.69
  509.1 5.6 slice-start.4
  509.5 5.3 copy-start.10
  509.7 5.1 slice-start.5
  509.7 5.1 slice-start.6
  523.0 552.2 %reduce-scatter.6.cloned.1.call-start = ((), (), s32[]{:S(2)}) async-start(), calls=%async_computation.8 | async-start | bytes 34603008 | tf_op jit(solution)/shard_map/reduce_scatter | solution.py:363
  534.1 4.1 copy-start.9
  722.8 380.8 %all-gather.18.cloned.1.call-start = ((), (), s32[]{:S(2)}) async-start(), calls=%async_computation.11 | async-start | bytes 2621440 | tf_op jit(solution)/shard_map/all_gather | solution.py:405
  1077.3 85.8 %all-reduce.8.cloned.1.call-start = ((), (), s32[]{:S(2)}) async-start(), calls=%async_computation.13 | async-start | bytes 1179648 | tf_op jit(solution)/shard_map/psum | solution.py:461
  1077.8 5.1 copy-start.19
  1077.8 5.1 copy-start.71
  1077.8 5.1 copy-start.73
  1103.6 3.9 copy-start.5
  1103.6 3.9 copy-start.11
  1103.6 4.1 copy-start.12
  1103.6 10.4 slice-start
  1107.7 6.3 slice-start.1
  1107.7 6.3 slice-start.2
  1114.1 3.5 copy-start.50
  1117.6 2.5 copy-start.22
  1123.4 3.9 copy-start.35
  1123.4 3.9 copy-start.37
  1129.2 191.2 %reduce-scatter.14.cloned.1.call-start = ((), (), s32[]{:S(2)}) async-start(), calls=%async_computation.15 | async-start | bytes 9732096 | tf_op jit(solution)/shard_map/reduce_scatter | solution.py:411
  1136.6 216.8 %reduce-scatter.10.cloned.1.call-start = ((), (), s32[]{:S(2)}) async-start(), calls=%async_computation.12 | async-start | bytes 2621440 | tf_op jit(solution)/shard_map/reduce_scatter | solution.py:469
  1141.0 5.4 copy-start.23
  1146.1 365.8 %reduce-scatter.12.cloned.1.call-start = ((), (), s32[]{:S(2)}) async-start(), calls=%async_computation.14 | async-start | bytes 9732096 | tf_op jit(solution)/shard_map/reduce_scatter | solution.py:488
  1152.3 2.3 copy-start.25
  1154.6 4.9 copy-start.39
  1154.6 4.9 copy-start.61
  1154.6 4.9 copy-start.65
  1159.5 4.5 copy-start.8
  1159.5 4.5 copy-start.57
  1159.5 4.5 copy-start.59
  1167.6 2.8 copy-start.20
  1207.1 115.9 %copy-start.28 = (bf16[1024,512]{1,0:T(8,128)(2,1)S(1)}, bf16[1024,512]{1,0:T(8,128)(2,1)}, u32[]{:S(2)}) copy-start(bf16[1024,512]{1,0:T(8,128)(2,1)} %reduce-scatter.8.cloned.1.call-done) | copy-start | bytes 3145732
  1207.1 115.9 %copy-start.29 = (bf16[1024,512]{1,0:T(8,128)(2,1)S(1)}, bf16[1024,512]{1,0:T(8,128)(2,1)}, u32[]{:S(2)}) copy-start(bf16[1024,512]{1,0:T(8,128)(2,1)} %reduce-scatter.6.cloned.1.call-done) | copy-start | bytes 3145732
  1323.0 30.4 %copy-start.41 = (bf16[512,512]{0,1:T(8,128)(2,1)S(1)}, bf16[512,512]{0,1:T(8,128)(2,1)}, u32[]{:S(2)}) copy-start(bf16[512,512]{0,1:T(8,128)(2,1)} %copy-done.40) | copy-start | bytes 1572868
  (30 other events, 41.0 us)
Sparse Core Ops, SparseCore 0:
  9.6 25.2 all-gather.11
  37.7 131.6 all-gather.13
  206.4 49.5 all-reduce.5
  258.6 132.3 all-gather.15
  394.2 113.0 all-gather.21
  511.0 113.0 all-gather.19
  627.3 42.6 reduce-scatter.7
  722.9 352.2 reduce-scatter.5
  1077.5 26.1 all-gather.17
  1129.3 33.4 all-reduce.7
  1166.5 153.8 reduce-scatter.13
  1322.9 30.4 reduce-scatter.9
  1357.0 154.8 reduce-scatter.11

commit v2 on v1

--- a/solution.py
+++ b/solution.py
@@ -194,7 +194,7 @@
     )(slots, gates, x, og, wgu, wd)
 
 
-def local(
+def local_wide(
     hidden_in,
     out_grad,
     first_gain,
@@ -525,14 +525,727 @@
     )
 
 
+def group_kernel(
+    k,
+    xr,
+    seqs,
+    cap,
+    slots, gates, mx_own, mx_peer, og_all, wgu, wd, shared,
+    s_xs, s_gs, s_gu, s_hid,
+    back_keep, back_send, rout_keep, rout_send, d_shared, o_xs, o_gs, o_gu, o_hid,
+    full_x, og, full_og, xs, gs, parts, backs, hid_s, gu_s, sem,
+):
+    del s_xs, s_gs, s_gu, s_hid
+    e = pl.program_id(0)
+    place = lax.axis_index("tensor")
+    mine = lax.axis_index("expert")
+    ring = lax.axis_size("expert") // 2
+    group = lax.rem(mine // 2 + ring - k, ring) * 2 + jnp.bitwise_xor(lax.rem(mine, 2), xr)
+    width = og_all.shape[-1]
+    half = wd.shape[1]
+    units = shared.shape[0] // 3
+
+    def cols_of(rel):
+        return pl.ds(pl.multiple_of(jnp.bitwise_xor(place, rel) * width, width), width)
+
+    iota = lax.broadcasted_iota(jnp.int32, (cap, SEQ), 0)
+
+    def pick_of(s):
+        chosen = []
+        for j in range(EXP_DEV):
+            row = s * EXP_DEV + j
+            chosen.append((iota == slots[group, row : row + 1, :]).astype(F32).astype(BF))
+        return jnp.concatenate(chosen, axis=0)
+
+    def gate_of(s, j):
+        row = s * EXP_DEV + j
+        hit = iota == slots[group, pl.ds(row, 1), :]
+        return jnp.sum(jnp.where(hit, gates[group, pl.ds(row, 1), :], 0.0), axis=1, keepdims=True)
+
+    @pl.when(e == 0)
+    def _():
+        fetch = pltpu.make_async_copy(og_all.at[group], og, sem)
+        fetch.start()
+        for rel, ref in ((0, mx_own.at[0]), (2, mx_own.at[1]), (1, mx_peer.at[0]), (3, mx_peer.at[1])):
+            full_x[:, cols_of(rel)] = ref[...]
+        fetch.wait()
+        for t in range(D // width):
+            full_og[:, t * width : (t + 1) * width] = og[t]
+        for s in range(seqs):
+            pick = pick_of(s)
+            gate_cols = [gate_of(s, j) for j in range(EXP_DEV)]
+            rows = slice(s * SEQ, (s + 1) * SEQ)
+            for c in range(D // width):
+                cols = slice(c * width, (c + 1) * width)
+                got = matmul(pick, full_x[rows, cols])
+                grad = matmul(pick, full_og[rows, cols])
+                for j in range(EXP_DEV):
+                    here = slice(s * cap, (s + 1) * cap)
+                    xs[j, here, cols] = got[j * cap : (j + 1) * cap].astype(BF)
+                    gs[j, here, cols] = (grad[j * cap : (j + 1) * cap] * gate_cols[j]).astype(BF)
+        both = matmul_rows(full_x[...], shared[: 2 * units])
+        gated = both[:, :units]
+        upper = both[:, units:]
+        sig = jax.nn.sigmoid(gated)
+        act = gated * sig
+        grad = matmul_rows(full_og[...], shared[2 * units :])
+        hid_s[...] = (act * upper).astype(BF)
+        gu_s[:, :units] = (grad * upper * sig * (1.0 + gated * (1.0 - sig))).astype(BF)
+        gu_s[:, units:] = (grad * act).astype(BF)
+        d_shared[: 2 * units] = matmul_cols(gu_s[...], full_x[...])
+        d_shared[2 * units :] = matmul_cols(hid_s[...], full_og[...])
+
+    x_rows = xs[e]
+    g_rows = gs[e]
+    both = matmul(x_rows, wgu[0])
+    gated = both[:, :half]
+    upper = both[:, half:]
+    sig = jax.nn.sigmoid(gated)
+    act = gated * sig
+    hidden = (act * upper).astype(BF)
+    grad_hidden = matmul_rows(g_rows, wd[0])
+    grad_gu = jnp.concatenate(
+        [
+            (grad_hidden * upper * sig * (1.0 + gated * (1.0 - sig))).astype(BF),
+            (grad_hidden * act).astype(BF),
+        ],
+        axis=1,
+    )
+    o_xs[0, 0] = x_rows
+    o_gs[0, 0] = g_rows
+    o_gu[0, 0] = grad_gu
+    o_hid[0, 0] = hidden
+    gate_col = jnp.concatenate([gate_of(s, e) for s in range(seqs)], axis=0)
+    part = (matmul(hidden, wd[0]) * gate_col).astype(BF)
+    back = matmul_rows(grad_gu, wgu[0]).astype(BF)
+    for s in range(seqs):
+        here = pl.ds(pl.multiple_of(e * cap, cap), cap)
+        parts[s, here, :] = part[s * cap : (s + 1) * cap]
+        backs[s, here, :] = back[s * cap : (s + 1) * cap]
+
+    @pl.when(e == EXP_DEV - 1)
+    def _():
+        for s in range(seqs):
+            pick = pick_of(s)
+            rows = slice(s * SEQ, (s + 1) * SEQ)
+            for rel, b_ref, r_ref, at in (
+                (0, back_keep, rout_keep, 0),
+                (2, back_keep, rout_keep, 1),
+                (1, back_send, rout_send, 0),
+                (3, back_send, rout_send, 1),
+            ):
+                cols = cols_of(rel)
+                b_ref[at, rows, :] = (
+                    matmul_cols(pick, backs[s, :, cols])
+                    + matmul(gu_s[rows, :], shared[: 2 * units, cols])
+                ).astype(BF)
+                r_ref[at, rows, :] = (
+                    matmul_cols(pick, parts[s, :, cols])
+                    + matmul(hid_s[rows, :], shared[2 * units :, cols])
+                ).astype(BF)
+
+
+def run_group(k, xr, cap, slots, gates, mx, og, wgu, wd, shared, saved):
+    count, width = og.shape[-2:]
+    seqs = count // SEQ
+    half = wd.shape[1]
+    units = shared.shape[0] // 3
+    call = k * 2 + xr
+    groups = slots.shape[0]
+    whole = lambda shape: pl.BlockSpec(shape, lambda e: (0,) * len(shape))
+    slab = lambda last: pl.BlockSpec((1, 1, seqs * cap, last), lambda e: (e, call, 0, 0))
+    hbm = pl.BlockSpec(memory_space=pl.ANY)
+    slab_shape = lambda last: jax.ShapeDtypeStruct((EXP_DEV, groups, seqs * cap, last), BF)
+    pair = jax.ShapeDtypeStruct((2, count, width), BF)
+    first = 8
+    args = [slots, gates, *mx, og, wgu, wd, shared]
+    aliases = {}
+    if saved is None:
+        saved = [jnp.zeros((8, 128), BF)] * 4
+    else:
+        aliases = {first + i: 5 + i for i in range(4)}
+    return pl.pallas_call(
+        functools.partial(group_kernel, k, xr, seqs, cap),
+        grid=(EXP_DEV,),
+        in_specs=[
+            whole(slots.shape),
+            whole(gates.shape),
+            whole((2, count, width)),
+            whole((2, count, width)),
+            hbm,
+            pl.BlockSpec((1, D, 2 * half), lambda e: (e, 0, 0)),
+            pl.BlockSpec((1, half, D), lambda e: (e, 0, 0)),
+            whole(shared.shape),
+            hbm, hbm, hbm, hbm,
+        ],
+        out_specs=[
+            whole((2, count, width)),
+            whole((2, count, width)),
+            whole((2, count, width)),
+            whole((2, count, width)),
+            whole((3 * units, D)),
+            slab(D),
+            slab(D),
+            slab(2 * half),
+            slab(half),
+        ],
+        out_shape=[
+            pair, pair, pair, pair,
+            jax.ShapeDtypeStruct((3 * units, D), F32),
+            slab_shape(D), slab_shape(D), slab_shape(2 * half), slab_shape(half),
+        ],
+        scratch_shapes=[
+            pltpu.VMEM((count, D), BF),
+            pltpu.VMEM((D // width, count, width), BF),
+            pltpu.VMEM((count, D), BF),
+            pltpu.VMEM((EXP_DEV, seqs * cap, D), BF),
+            pltpu.VMEM((EXP_DEV, seqs * cap, D), BF),
+            pltpu.VMEM((seqs, EXP_DEV * cap, D), BF),
+            pltpu.VMEM((seqs, EXP_DEV * cap, D), BF),
+            pltpu.VMEM((count, units), BF),
+            pltpu.VMEM((count, 2 * units), BF),
+            pltpu.SemaphoreType.DMA,
+        ],
+        input_output_aliases=aliases,
+        compiler_params=pltpu.CompilerParams(
+            dimension_semantics=("arbitrary",), vmem_limit_bytes=60 * 1024 * 1024
+        ),
+        cost_estimate=pl.CostEstimate(
+            flops=EXP_DEV * seqs * cap * D * (half * 12 + SEQ * 8),
+            bytes_accessed=40 * 1024 * 1024,
+            transcendentals=EXP_DEV * seqs * cap * half,
+        ),
+        name=f"group_{k}_{xr}",
+    )(*args, *saved)
+
+
+def weight_kernel(xs, gs, gu, hid, d_gate, d_up, d_down, acc_gu, acc_d):
+    g = pl.program_id(1)
+    ff = d_gate.shape[-1]
+    half = hid.shape[-1]
+
+    @pl.when(g == 0)
+    def _():
+        acc_gu[...] = jnp.zeros_like(acc_gu)
+        acc_d[...] = jnp.zeros_like(acc_d)
+
+    for i in range(xs.shape[1]):
+        acc_gu[...] += matmul_cols(xs[0, i], gu[0, i])
+        acc_d[...] += matmul_cols(hid[0, i], gs[0, i])
+
+    @pl.when(g == pl.num_programs(1) - 1)
+    def _():
+        d_gate[0] = acc_gu[:, :ff]
+        d_up[0] = acc_gu[:, half : half + ff]
+        d_down[0] = acc_d[:ff]
+
+
+def weight_grads(xs, gs, gu, hid, ff):
+    groups, rows = xs.shape[1:3]
+    half = hid.shape[-1]
+    step = 2
+    slab = lambda last: pl.BlockSpec((1, step, rows, last), lambda e, g: (e, g, 0, 0))
+    out = lambda *dims: pl.BlockSpec((1, *dims), lambda e, g: (e, 0, 0))
+    return pl.pallas_call(
+        weight_kernel,
+        grid=(EXP_DEV, groups // step),
+        in_specs=[slab(D), slab(D), slab(2 * half), slab(half)],
+        out_specs=[out(D, ff), out(D, ff), out(ff, D)],
+        out_shape=[
+            jax.ShapeDtypeStruct((EXP_DEV, D, ff), F32),
+            jax.ShapeDtypeStruct((EXP_DEV, D, ff), F32),
+            jax.ShapeDtypeStruct((EXP_DEV, ff, D), F32),
+        ],
+        scratch_shapes=[pltpu.VMEM((D, 2 * half), F32), pltpu.VMEM((half, D), F32)],
+        compiler_params=pltpu.CompilerParams(
+            dimension_semantics=("arbitrary", "arbitrary"), vmem_limit_bytes=60 * 1024 * 1024
+        ),
+        cost_estimate=pl.CostEstimate(
+            flops=EXP_DEV * groups * rows * D * half * 6,
+            bytes_accessed=64 * 1024 * 1024,
+            transcendentals=0,
+        ),
+        name="weight_grads",
+    )(xs, gs, gu, hid)
+
+
+def place_kernel(targets, n, *refs):
+    blocks, out, sems = refs[:n], refs[n], refs[n + 1]
+    copies = [
+        pltpu.make_async_copy(block, out.at[target()], sems.at[i])
+        for i, (block, target) in enumerate(zip(blocks, targets))
+    ]
+    for copy in copies:
+        copy.start()
+    for copy in copies:
+        copy.wait()
+
+
+def place(blocks, targets, count):
+    n = len(blocks)
+    return pl.pallas_call(
+        functools.partial(place_kernel, targets, n),
+        in_specs=[pl.BlockSpec(memory_space=pltpu.VMEM)] * n,
+        out_specs=pl.BlockSpec(memory_space=pl.ANY),
+        out_shape=jax.ShapeDtypeStruct((count, *blocks[0].shape), blocks[0].dtype),
+        scratch_shapes=[pltpu.SemaphoreType.DMA((n,))],
+        compiler_params=pltpu.CompilerParams(vmem_limit_bytes=16 * 1024 * 1024),
+        name="place",
+    )(*blocks)
+
+
+def flip_tensor(x, mask):
+    size = lax.axis_size("tensor")
+    return lax.ppermute(x, "tensor", [(i, i ^ mask) for i in range(size)])
+
+
+def to_core(x):
+    return flip_tensor(x, 1)
+
+
+def to_y(x):
+    return flip_tensor(x, 2)
+
+
+def to_x(x):
+    size = lax.axis_size("expert")
+    return lax.ppermute(x, "expert", [(i, i ^ 1) for i in range(size)])
+
+
+def to_z(x):
+    size = lax.axis_size("expert")
+    return lax.ppermute(x, "expert", [(i, (i + 2) % size) for i in range(size)])
+
+
+def after(x, done):
+    return lax.optimization_barrier((x, done))[0]
+
+
+def add(*terms):
+    total = terms[0].astype(F32)
+    for term in terms[1:]:
+        total = total + term.astype(F32)
+    return total.astype(BF)
+
+
+def gather_pairs(block):
+    ring = lax.axis_size("expert") // 2
+    pairs = []
+    for k in range(ring):
+        pairs.append((block, to_x(block)))
+        if k < ring - 1:
+            block = to_z(block)
+    return pairs
+
+
+def group_at(k, xr):
+    def target():
+        mine = lax.axis_index("expert")
+        ring = lax.axis_size("expert") // 2
+        return lax.rem(mine // 2 + ring - k, ring) * 2 + jnp.bitwise_xor(lax.rem(mine, 2), xr)
+
+    return target
+
+
+def gather_rows(block):
+    groups = lax.axis_size("expert")
+    pairs = gather_pairs(block)
+    blocks = [b for pair in pairs for b in pair]
+    targets = [group_at(k, xr) for k in range(groups // 2) for xr in range(2)]
+    return place(blocks, targets, groups)
+
+
+def ring_sum(totals):
+    ring = len(totals)
+    moving = totals[1]()
+    for k in range(2, ring):
+        moving = add(to_z(moving), totals[k]())
+    return to_z(moving), totals[0]()
+
+
+def scatter_rows(blocks):
+    ring = lax.axis_size("expert") // 2
+    at = lambda k, xr: lax.dynamic_index_in_dim(blocks, group_at(k, xr)(), 0, keepdims=False)
+    came = {}
+    last = None
+    for k in [*range(1, ring), 0]:
+        sent = at(k, 1)
+        if last is not None:
+            sent = after(sent, last)
+        last = to_x(sent)
+        came[k] = last
+    return ring_sum([lambda k=k: add(at(k, 0), came[k]) for k in range(ring)])
+
+
+def pieces_of(x):
+    other = to_y(x)
+    return x, other, to_core(x), to_core(other)
+
+
+def join(pieces, axis):
+    place_t = lax.axis_index("tensor")
+    low_y = place_t // 2 == 0
+    low_c = lax.rem(place_t, 2) == 0
+    o0, o2, o1, o3 = pieces
+    a = (jnp.where(low_y, o0, o2), jnp.where(low_y, o2, o0))
+    b = (jnp.where(low_y, o1, o3), jnp.where(low_y, o3, o1))
+    out = []
+    for y in range(2):
+        out += [jnp.where(low_c, a[y], b[y]), jnp.where(low_c, b[y], a[y])]
+    return jnp.concatenate(out, axis=axis)
+
+
+def scatter_cols(x):
+    place_t = lax.axis_index("tensor")
+    rows = x.shape[0]
+    view = x.reshape(rows, 2, 2, -1)
+    low_y = place_t // 2 == 0
+    low_c = lax.rem(place_t, 2) == 0
+    keep = jnp.where(low_c, view[:, :, 0], view[:, :, 1])
+    send = jnp.where(low_c, view[:, :, 1], view[:, :, 0])
+    half = add(keep, to_core(send))
+    mine = jnp.where(low_y, half[:, 0], half[:, 1])
+    theirs = jnp.where(low_y, half[:, 1], half[:, 0])
+    return mine, to_y(theirs)
+
+
+def sum_cols(x):
+    place_t = lax.axis_index("tensor")
+    rows = x.shape[0]
+    view = x.reshape(rows, 2, 2, -1)
+    low_c = lax.rem(place_t, 2) == 0
+    keep = jnp.where(low_c, view[:, :, 0], view[:, :, 1])
+    send = jnp.where(low_c, view[:, :, 1], view[:, :, 0])
+    half = add(keep, to_core(send))
+    half = add(half, to_y(half))
+    other = to_core(half)
+    return jnp.stack(
+        [jnp.where(low_c, half, other), jnp.where(low_c, other, half)], axis=2
+    ).reshape(rows, -1)
+
+
+def small_sum(x):
+    x = x + to_core(x)
+    return x + to_y(x)
+
+
+def local(
+    hidden_in,
+    out_grad,
+    first_gain,
+    query_weight,
+    latent_weight,
+    latent_gain,
+    expand_weight,
+    output_weight,
+    second_gain,
+    shared_gate,
+    shared_up,
+    shared_down,
+    expert_gate,
+    expert_up,
+    expert_down,
+    routes,
+    gate_values,
+):
+    groups = lax.axis_size("expert")
+    tensors = lax.axis_size("tensor")
+    ring = groups // 2
+    place_t = lax.axis_index("tensor")
+    mine = lax.axis_index("expert")
+    experts_all = EXP_DEV * groups
+    cap = SEQ * TOP * 4 // (3 * experts_all)
+    width = D // tensors
+    heads = H // tensors
+    count = hidden_in.shape[0]
+    seqs = count // SEQ
+    rows_dev = D // groups
+    scale = (DN + DR) ** (-0.5)
+    cosine, sine = rope_tables(SEQ, DR)
+    blocks = jnp.arange(SEQ, dtype=jnp.int32) // BLOCK
+    allowed = (blocks[None, :] <= blocks[:, None])[None, None]
+    qc = query_weight.shape[1]
+    oc = output_weight.shape[1]
+    lc = latent_weight.shape[1]
+    sc = shared_gate.shape[1]
+    er, ec = expand_weight.shape
+    kv_dev = latent_gain.shape[0]
+    cut = er * ec // rows_dev
+    fold = rows_dev // er
+    quarter = rows_dev // tensors
+
+    gain_row = jnp.concatenate([first_gain, second_gain, latent_gain]).reshape(1, -1)
+    lat_rows = lax.dynamic_slice_in_dim(latent_weight, place_t * quarter, quarter, 0)
+    lat_all = gather_rows(jnp.concatenate([lat_rows, gain_row], axis=0))
+    gains = lat_all[:, quarter].astype(F32)
+    gain_first = gains[:, :rows_dev].reshape(-1)
+    gain_mid = gains[:, rows_dev : 2 * rows_dev].reshape(-1)
+    gain_kv = gains[:, 2 * rows_dev :].reshape(-1)
+    full_latent = join(pieces_of(lat_all[:, :quarter]), 1).reshape(D, lc)
+    expand_rows = jnp.concatenate(
+        [expand_weight[:, i * cut : (i + 1) * cut] for i in range(fold)], axis=0
+    )
+    qe_all = gather_rows(jnp.concatenate([query_weight, output_weight, expand_rows], axis=1))
+    full_query = qe_all[:, :, :qc].reshape(D, qc)
+    full_expand = (
+        qe_all[:, :, qc + oc :].reshape(groups, fold, er, cut).transpose(0, 2, 1, 3).reshape(groups * er, ec)
+    )
+    full_output = qe_all[:, :, qc : qc + oc].reshape(D, oc)
+
+    units = sc // groups
+    wide_units = -(-units // 128) * 128
+    shared_t = jnp.stack([shared_gate.T, shared_up.T, shared_down.T]).reshape(3, groups, units, rows_dev)
+    shared_t = shared_t.transpose(1, 0, 2, 3).reshape(groups, 3 * units, rows_dev)
+    shared_t = lax.all_to_all(shared_t, "expert", split_axis=0, concat_axis=0, tiled=True)
+    shared_t = shared_t.reshape(groups, 3, units, rows_dev).transpose(1, 2, 0, 3).reshape(3, units, D)
+    shared_w = jnp.pad(shared_t, ((0, 0), (0, wide_units - units), (0, 0))).reshape(3 * wide_units, D)
+
+    table = gather_rows(jnp.concatenate([routes.T.astype(F32), gate_values.T], axis=0))
+    og_all = lax.all_gather(out_grad, ("expert", "tensor"), axis=0)
+    og_all = og_all.reshape(groups, tensors, count, width)
+    whole_grad = lax.dynamic_index_in_dim(og_all, mine, 0, keepdims=False)
+    whole_grad = whole_grad.transpose(1, 0, 2).reshape(count, D)
+
+    whole_in = join(pieces_of(hidden_in), 1)
+    inputs = whole_in.astype(F32)
+    first_scale = rms_scale(inputs)
+    first_hat = inputs * first_scale
+    normed = (first_hat * gain_first).astype(BF)
+    query = matmul(normed, full_query).reshape(seqs, SEQ, heads, DN + DR)
+    latent = matmul(normed, full_latent)
+    compressed = latent[:, :KV_RANK]
+    latent_scale = rms_scale(compressed)
+    latent_hat = compressed * latent_scale
+    latent_normed = (latent_hat * gain_kv).astype(BF)
+    expanded = matmul(latent_normed, full_expand).reshape(seqs, SEQ, heads, DN + DV)
+    queries = jnp.concatenate(
+        [query[..., :DN], rotate(query[..., DN:], cosine[:, None, :], sine[:, None, :])], axis=-1
+    ).astype(BF)
+    key_rope = rotate(latent[:, KV_RANK:].reshape(seqs, SEQ, DR), cosine, sine).astype(BF)
+    keys = jnp.concatenate(
+        [
+            expanded[..., :DN].astype(BF),
+            jnp.broadcast_to(key_rope[:, :, None, :], (seqs, SEQ, heads, DR)),
+        ],
+        axis=-1,
+    )
+    values = expanded[..., DN:].astype(BF)
+    scores = jnp.where(
+        allowed,
+        jnp.einsum("nqhc,nkhc->nhqk", queries, keys, preferred_element_type=F32) * scale,
+        masked_value,
+    )
+    peak = jnp.max(scores, axis=-1, keepdims=True)
+    log_total = peak + jnp.log(jnp.sum(jnp.exp(scores - peak), axis=-1, keepdims=True))
+    weights = jnp.exp(scores - log_total)
+    mixed = (
+        jnp.einsum("nhqk,nkhc->nqhc", weights.astype(BF), values, preferred_element_type=F32)
+        .astype(BF)
+        .reshape(count, heads * DV)
+    )
+    attended = sum_cols(matmul_rows(mixed, full_output).astype(BF)).astype(F32)
+    middle = inputs + attended
+    second_scale = rms_scale(middle)
+    second_hat = middle * second_scale
+    mixer_in = (second_hat * gain_mid).astype(BF)
+    low_y = place_t // 2 == 0
+    low_c = lax.rem(place_t, 2) == 0
+    view = mixer_in.reshape(count, 2, 2, width)
+    view = jnp.where(low_c, view[:, :, 0], view[:, :, 1])
+    mixer_half = jnp.stack(
+        [jnp.where(low_y, view[:, 0], view[:, 1]), jnp.where(low_y, view[:, 1], view[:, 0])]
+    )
+    mixer_pairs = gather_pairs(mixer_half)
+
+    local_experts = (mine * EXP_DEV + jnp.arange(EXP_DEV, dtype=jnp.int32)).astype(F32)
+    route_t = table[:, :TOP].reshape(groups, TOP, seqs, SEQ)
+    gate_t = table[:, TOP:].reshape(groups, TOP, seqs, SEQ)
+    named = route_t[:, :, :, None, :] == local_experts[None, None, None, :, None]
+    gate_of = jnp.sum(jnp.where(named, gate_t[:, :, :, None, :], 0.0), axis=1)
+    used = jnp.any(named, axis=1)
+    before = (
+        jnp.arange(SEQ, dtype=jnp.int32)[:, None] < jnp.arange(SEQ, dtype=jnp.int32)[None, :]
+    ).astype(BF)
+    prior = jnp.einsum("gset,tu->gseu", used.astype(BF), before, preferred_element_type=F32)
+    slot_of = jnp.where(used & (prior < cap), prior, -1.0).astype(jnp.int32)
+    slot_of = slot_of.reshape(groups, seqs * EXP_DEV, SEQ)
+    gate_of = gate_of.reshape(groups, seqs * EXP_DEV, SEQ)
+
+    ff = expert_gate.shape[2]
+    half = -(-ff // 128) * 128
+    wide = ((0, 0), (0, 0), (0, half - ff))
+    wgu = jnp.concatenate([jnp.pad(expert_gate, wide), jnp.pad(expert_up, wide)], axis=2)
+    wd = jnp.pad(expert_down, ((0, 0), (0, half - ff), (0, 0)))
+    saved = None
+    outs = {}
+    d_shared = []
+    for k in range(ring):
+        for xr in range(2):
+            rows = mixer_pairs[k][xr]
+            *out, d_sh, s0, s1, s2, s3 = run_group(
+                k, xr, cap, slot_of, gate_of, (rows, to_core(rows)), og_all, wgu, wd, shared_w, saved
+            )
+            saved = [s0, s1, s2, s3]
+            outs[k, xr] = out
+            d_shared.append(d_sh)
+
+    def over_tensor(keep, send):
+        came = to_core(send)
+        return add(keep[0], came[0], to_y(add(keep[1], came[1])))
+
+    def combine(at):
+        def total(k):
+            other = over_tensor(outs[k, 1][at], outs[k, 1][at + 1])
+            return add(over_tensor(outs[k, 0][at], outs[k, 0][at + 1]), to_x(other))
+
+        return ring_sum([functools.partial(total, k) for k in range(ring)])
+
+    back_sum = add(*combine(0))
+    rout_sum = combine(2)
+    total_gate, total_up, total_down = weight_grads(*saved, ff)
+    middle_slice = lax.dynamic_slice_in_dim(middle, place_t * width, width, 1)
+    block_out = (
+        middle_slice + rout_sum[0].astype(F32) + rout_sum[1].astype(F32)
+    ).astype(BF)
+    shared_step = d_shared[0]
+    for term in d_shared[1:]:
+        shared_step = shared_step + term
+    shared_step = shared_step.reshape(3, wide_units, groups, rows_dev)[:, :units].astype(BF)
+    shared_step = shared_step.transpose(2, 0, 1, 3).reshape(groups, 3 * units, rows_dev)
+    shared_step = lax.all_to_all(shared_step, "expert", split_axis=0, concat_axis=0, tiled=True)
+    shared_step = shared_step.reshape(groups, 3, units, rows_dev).transpose(1, 3, 0, 2)
+    shared_step = shared_step.reshape(3, rows_dev, sc).astype(F32)
+
+    grad_mixer = join(pieces_of(back_sum), 1).astype(F32)
+    step_gain_two = jnp.sum(grad_mixer * second_hat, axis=0)
+    grad_middle = whole_grad.astype(F32) + norm_back(
+        grad_mixer * gain_mid, second_hat, second_scale
+    )
+    grad_att = grad_middle.astype(BF)
+    step_output = matmul_cols(grad_att, mixed)
+    output_sum = scatter_rows(step_output.astype(BF).reshape(groups, rows_dev, -1))
+    grad_mixed = matmul(grad_att, full_output).astype(BF).reshape(seqs, SEQ, heads, DV)
+    grad_weights = jnp.einsum(
+        "nqhc,nkhc->nhqk", grad_mixed, values, preferred_element_type=F32
+    )
+    grad_scores = (
+        weights * (grad_weights - jnp.sum(weights * grad_weights, axis=-1, keepdims=True))
+    ).astype(BF)
+    grad_values = jnp.einsum(
+        "nhqk,nqhc->nkhc", weights.astype(BF), grad_mixed, preferred_element_type=F32
+    )
+    grad_queries = (
+        jnp.einsum("nhqk,nkhc->nqhc", grad_scores, keys, preferred_element_type=F32) * scale
+    )
+    grad_keys = (
+        jnp.einsum("nhqk,nqhc->nkhc", grad_scores, queries, preferred_element_type=F32) * scale
+    )
+    grad_query = (
+        jnp.concatenate(
+            [
+                grad_queries[..., :DN],
+                unrotate(grad_queries[..., DN:], cosine[:, None, :], sine[:, None, :]),
+            ],
+            axis=-1,
+        )
+        .astype(BF)
+        .reshape(count, heads * (DN + DR))
+    )
+    step_query = matmul_cols(normed, grad_query)
+    query_part = matmul_rows(grad_query, full_query)
+    rope_part = unrotate(jnp.sum(grad_keys[..., DN:], axis=2), cosine, sine).reshape(count, DR)
+    grad_expanded = (
+        jnp.concatenate([grad_keys[..., :DN], grad_values], axis=-1)
+        .astype(BF)
+        .reshape(count, heads * (DN + DV))
+    )
+    step_expand = matmul_cols(latent_normed, grad_expanded)
+    expand_back = (
+        step_expand.astype(BF)
+        .reshape(groups, er, fold, cut)
+        .transpose(0, 2, 1, 3)
+        .reshape(groups * rows_dev, cut)
+    )
+    qe_sum = scatter_rows(
+        jnp.concatenate([step_query.astype(BF), expand_back], axis=1).reshape(groups, rows_dev, -1)
+    )
+    latent_part = matmul_rows(grad_expanded, full_expand)
+    lat_part = jnp.concatenate([latent_part, rope_part], axis=1).astype(BF)
+    lat_part = add(lat_part, to_core(lat_part))
+    latent_sum = lat_part.astype(F32) + to_y(lat_part).astype(F32)
+    grad_lnormed = latent_sum[:, :KV_RANK]
+    step_gain_latent = jnp.sum(grad_lnormed * latent_hat, axis=0)
+    grad_compressed = norm_back(grad_lnormed * gain_kv, latent_hat, latent_scale)
+    grad_lat = jnp.concatenate([grad_compressed, latent_sum[:, KV_RANK:]], axis=-1).astype(BF)
+    query_sum = scatter_cols(query_part.astype(BF))
+    latent_slice = lax.dynamic_slice_in_dim(full_latent, place_t * width, width, 0)
+    grad_normed = (
+        query_sum[0].astype(F32) + query_sum[1].astype(F32) + matmul_rows(grad_lat, latent_slice)
+    )
+    first_hat_slice = lax.dynamic_slice_in_dim(first_hat, place_t * width, width, 1)
+    gain_first_slice = lax.dynamic_slice_in_dim(gain_first, place_t * width, width, 0)
+    grad_hat = grad_normed * gain_first_slice
+    row_dot = small_sum(jnp.sum(grad_hat * first_hat_slice, axis=1).reshape(-1, 128)) / D
+    grad_middle_slice = lax.dynamic_slice_in_dim(grad_middle, place_t * width, width, 1)
+    input_grad = grad_middle_slice + first_scale * (
+        grad_hat - first_hat_slice * row_dot.reshape(-1, 1)
+    )
+    step_gain_one = jnp.sum(grad_normed * first_hat_slice, axis=0)
+
+    normed_part = lax.dynamic_index_in_dim(
+        normed.reshape(count, groups, tensors, quarter), place_t, 2, keepdims=False
+    ).reshape(count, groups * quarter)
+    step_latent = matmul_cols(normed_part, grad_lat).reshape(groups, quarter, lc)
+    one_full = lax.dynamic_update_slice_in_dim(
+        jnp.zeros((D,), F32), step_gain_one, place_t * width, 0
+    )
+    once = jnp.where(place_t == 0, 1.0, 0.0)
+    gain_rows = jnp.concatenate(
+        [
+            one_full.reshape(groups, rows_dev),
+            (step_gain_two * once).reshape(groups, rows_dev),
+            (step_gain_latent * once).reshape(groups, kv_dev),
+        ],
+        axis=1,
+    )
+    lat_sum = add(
+        *scatter_rows(jnp.concatenate([step_latent, gain_rows[:, None]], axis=1).astype(BF))
+    )
+    lat_pieces = pieces_of(lat_sum)
+    gain_sum = sum(piece[quarter].astype(F32) for piece in lat_pieces)
+    grad_latent = join([piece[:quarter] for piece in lat_pieces], 0).astype(F32)
+    qe = qe_sum[0].astype(F32) + qe_sum[1].astype(F32)
+    grad_expand = jnp.concatenate(
+        [qe[i * er : (i + 1) * er, qc:] for i in range(fold)], axis=1
+    )
+    return (
+        block_out,
+        input_grad,
+        gain_sum[:rows_dev],
+        qe[:, :qc],
+        grad_latent,
+        gain_sum[2 * rows_dev :],
+        grad_expand,
+        output_sum[0].astype(F32) + output_sum[1].astype(F32),
+        gain_sum[rows_dev : 2 * rows_dev],
+        shared_step[0],
+        shared_step[1],
+        shared_step[2],
+        total_gate,
+        total_up,
+        total_down,
+    )
+
+
 def solution(mesh):
+    body = local if mesh.shape["expert"] == 8 and mesh.shape["tensor"] == 4 else local_wide
     both = P("expert", "tensor")
     cols = P("expert", None, "tensor")
     rows = P("expert", "tensor", None)
     one = P("expert")
     flat = P("expert", None)
     return jax.shard_map(
-        local,
+        body,
         mesh=mesh,
         in_specs=(
             both, both, one, both, flat, one, both, both, one, both, both, both,

time: 1530 us -> 1070 us (0.70)
  waiting for transfers between devices: 1060 us -> 440 us
  blocking collectives: 114 us -> 0 us
  Pallas kernels: 98.7 us -> 212 us
  starting transfers between devices: 1.45 us -> 106 us
  other arithmetic: 55.5 us -> 114 us
  matrix products: 72.7 us -> 35.3 us
  local copies, waits for them, and re-layouts: 103 us -> 134 us
    reduce_scatter x5 -> x0, waiting for transfers between devices: 596 us -> none  [the longest x1 352 us: local(): lax.psum_scatter(outs.reshape(groups * tensors * 2 * per, width), ('exper...]
    ppermute x0 -> x124, waiting for transfers between devices: none -> 439 us  [the longest x61 192 us: flip_tensor(): return lax.ppermute(x, 'tensor', [(i, i ^ mask) for i in range(size)])]
    all_gather x6 -> x1, waiting for transfers between devices: 420 us -> 0.01 us  [local(): og_all = lax.all_gather(out_grad, ('expert', 'tensor'), axis=0)]
    pallas_call x1 -> x12, Pallas kernels: 98.7 us -> 212 us  [the longest x8 175 us: run_group(): pl.pallas_call(functools.partial(group_kernel, k, xr, seqs, cap), grid=(E...]
    ppermute x0 -> x124, starting transfers between devices: none -> 95.8 us  [the longest x36 33.9 us: to_x(): return lax.ppermute(x, 'expert', [(i, i ^ 1) for i in range(size)])]
    all_gather x2 -> x0, blocking collectives: 64 us -> none  [the longest x1 32 us: local(): lax.all_gather(jnp.concatenate([first_gain, second_gain, latent_gain]).as...]
    psum x2 -> x0, blocking collectives: 49.8 us -> none  [the longest x1 42.8 us: local(): lax.psum(jnp.concatenate([one_full, step_gain_two / tensors, step_gain_la...]
    psum x2 -> x0, waiting for transfers between devices: 46.5 us -> none  [the longest x1 46.5 us: local(): lax.psum(matmul_rows(mixed, full_output).astype(BF), 'tensor').astype(F32)]
  transfers between devices with their start and end apart: 13 -> 127, of which waited for: 10 -> 46; matrix products, arithmetic and copies ran while one was open for 10% -> 21% of each run, Pallas kernels for 6% -> 20%
where the time goes in v2:
time: 1070 us; the launch traced here: 1060 us
  waiting for transfers between devices  440 us (41%)
  Pallas kernels  212 us (20%)
  local copies, waits for them, and re-layouts  134 us (13%)
  other arithmetic  114 us (11%)
  starting transfers between devices  106 us (10%)
  matrix products  35.3 us (3%)
  between operations  16.6 us (2%)
    ppermute x61, waiting for transfers between devices, flip_tensor(): return lax.ppermute(x, 'tensor', [(i, i ^ mask) for i in range(size)])  192 us
    pallas_call x8, Pallas kernels, run_group(): pl.pallas_call(functools.partial(group_kernel, k, xr, seqs, cap), grid=(E...  175 us
    ppermute x27, waiting for transfers between devices, to_z(): return lax.ppermute(x, 'expert', [(i, (i + 2) % size) for i in range(size)])  161 us
    ppermute x36, waiting for transfers between devices, to_x(): return lax.ppermute(x, 'expert', [(i, i ^ 1) for i in range(size)])  86.1 us
    unnamed x268, local copies, waits for them, and re-layouts  46.2 us
    ppermute x36, starting transfers between devices, to_x(): return lax.ppermute(x, 'expert', [(i, i ^ 1) for i in range(size)])  33.9 us
    ppermute x27, starting transfers between devices, to_z(): return lax.ppermute(x, 'expert', [(i, (i + 2) % size) for i in range(size)])  33.4 us
    convert_element_type x45, other arithmetic, add(): return total.astype(BF)  33.1 us
  transfers between devices with their start and end apart: 127, of which 46 were waited for; matrix products, arithmetic and copies ran while one was open for 21% of the time, Pallas kernels for 20%

profile of v2, /device:TPU:0, one launch (start us, length us, event | category | flops | bytes accessed | tf_op | source)
XLA Modules:
  0.0 1057.6 jit_solution(17473341247615656941)
XLA Ops:
  20.2 30.3 %collective-permute-done.6.refs_4_ = bf16[65,576]{1,0:T(8,128)(2,1)S(1)} collective-permute-done((bf16[65,576]{1,0:T(8,128)(2,1)S(1)}, bf16[65,576]{1,0:T(8,128)(2,1)S(1)}, u32[]{:S(2)}, u32[]{:S(2)}) %collective-permute-start.6) | collective-permute-done | bytes 74912 | tf_op jit(solution)/shard_map/ppermute | solution.py:817
  52.7 5.7 collective-permute-done.8.refs_6_
  61.5 4.4 collective-permute-done.9.refs_7_
  68.8 10.9 %collective-permute-done.10 = bf16[8,64,576]{2,1,0:T(8,128)(2,1)} collective-permute-done((bf16[8,64,576]{2,1,0:T(8,128)(2,1)}, bf16[8,64,576]{2,1,0:T(8,128)(2,1)}, u32[]{:S(2)}, u32[]{:S(2)}) %collective-permute-start.10) | collective-permute-done | bytes 589856 | tf_op jit(solution)/shard_map/ppermute | solution.py:799
  85.4 13.6 %collective-permute-done.16.refs_4_ = bf16[256,1536]{1,0:T(8,128)(2,1)} collective-permute-done((bf16[256,1536]{1,0:T(8,128)(2,1)S(1)}, bf16[256,1536]{1,0:T(8,128)(2,1)}, u32[]{:S(2)}, u32[]{:S(2)}) %collective-permute-start.16) | collective-permute-done | bytes 786464 | tf_op jit(solution)/shard_map/ppermute | solution.py:817
  103.1 30.0 %collective-permute-done.18.refs_6_ = bf16[256,1536]{1,0:T(8,128)(2,1)} collective-permute-done((bf16[256,1536]{1,0:T(8,128)(2,1)}, bf16[256,1536]{1,0:T(8,128)(2,1)}, u32[]{:S(2)}, u32[]{:S(2)}) %collective-permute-start.18) | collective-permute-done | bytes 786464 | tf_op jit(solution)/shard_map/ppermute | solution.py:817
  137.5 6.2 collective-permute-done.17.refs_5_
  143.6 27.0 %collective-permute-done.19.refs_7_ = bf16[256,1536]{1,0:T(8,128)(2,1)} collective-permute-done((bf16[256,1536]{1,0:T(8,128)(2,1)}, bf16[256,1536]{1,0:T(8,128)(2,1)}, u32[]{:S(2)}, u32[]{:S(2)}) %collective-permute-start.19) | collective-permute-done | bytes 786464 | tf_op jit(solution)/shard_map/ppermute | solution.py:812
  182.9 4.9 copy.183
  187.8 3.8 fusion.14
  195.6 4.4 convolution_convert_fusion.3
  200.0 3.9 copy.188
  216.4 25.0 %collective-permute-done.21 = bf16[512,2,512]{2,0,1:T(8,128)(2,1)S(1)} collective-permute-done((bf16[512,2,512]{2,0,1:T(8,128)(2,1)S(1)}, bf16[512,2,512]{2,0,1:T(8,128)(2,1)S(1)}, u32[]{:S(2)}, u32[]{:S(2)}) %collective-permute-start.21) | collective-permute-done | bytes 1048608 | tf_op jit(solution)/shard_map/ppermute | solution.py:799
  245.2 6.6 reshape.832
  257.1 5.2 copy.191
  262.3 5.4 copy.192
  267.7 5.9 multiply_reduce_fusion.1
  278.0 4.9 all-to-all-start
  283.0 21.9 %collective-permute-done.30.mx_own = bf16[2,512,512]{2,1,0:T(8,128)(2,1)} collective-permute-done((bf16[2,512,512]{2,1,0:T(8,128)(2,1)}, bf16[2,512,512]{2,1,0:T(8,128)(2,1)}, u32[]{:S(2)}, u32[]{:S(2)}) %collective-permute-start.30) | collective-permute-done | bytes 1048608 | tf_op jit(solution)/shard_map/ppermute | solution.py:817
  308.0 37.0 %collective-permute-done.24.refs_2_ = f32[12,512]{1,0:T(8,128)S(1)} collective-permute-done((f32[12,512]{1,0:T(8,128)S(1)}, f32[12,512]{1,0:T(8,128)S(1)}, u32[]{:S(2)}, u32[]{:S(2)}) %collective-permute-start.24) | collective-permute-done | bytes 24608 | tf_op jit(solution)/shard_map/ppermute | solution.py:817
  345.0 4.2 collective-permute-start.26
  349.2 4.6 copy.201
  353.8 4.6 copy.202
  362.9 6.6 fusion.2.wgu
  371.6 4.0 pad.17.wd
  375.6 11.3 %collective-permute-done.25.refs_3_ = f32[12,512]{1,0:T(8,128)S(1)} collective-permute-done((f32[12,512]{1,0:T(8,128)S(1)}, f32[12,512]{1,0:T(8,128)S(1)}, u32[]{:S(2)}, u32[]{:S(2)}) %collective-permute-start.25) | collective-permute-done | bytes 24608 | tf_op jit(solution)/shard_map/ppermute | solution.py:812
  404.6 4.2 convert_bitcast_fusion
  408.8 5.6 copy.204
  419.6 21.6 %group_0_0.1 = (bf16[2,512,512]{2,1,0:T(8,128)(2,1)}, bf16[2,512,512]{2,1,0:T(8,128)(2,1)}, bf16[2,512,512]{2,1,0:T(8,128)(2,1)}, bf16[2,512,512]{2,1,0:T(8,128)...) custom-call(s32[8,4,256]{2,1,0:T(4,128)} %copy.241.slots, ...), custom_call_target="tpu_custom_call" | custom-call | flops 6979321856 | bytes 41943040 | tf_op jit(solution)/shard_map/group_0_0/pallas_call | solution.py:667
  441.8 21.8 %group_0_1.1 = (bf16[2,512,512]{2,1,0:T(8,128)(2,1)}, bf16[2,512,512]{2,1,0:T(8,128)(2,1)}, bf16[2,512,512]{2,1,0:T(8,128)(2,1)}, bf16[2,512,512]{2,1,0:T(8,128)...) custom-call(s32[8,4,256]{2,1,0:T(4,128)} %copy.241.slots, ...), custom_call_target="tpu_custom_call", output_to_operand_aliasing={{5}: (8, {}), {6}: (9, {}), {7}: (10, {}), {8}: (11, {})} | custom-call | flops 6979321856 | bytes 41943040 | tf_op jit(solution)/shard_map/group_0_1/pallas_call | solution.py:667
  464.8 21.9 %group_1_0.1 = (bf16[2,512,512]{2,1,0:T(8,128)(2,1)}, bf16[2,512,512]{2,1,0:T(8,128)(2,1)}, bf16[2,512,512]{2,1,0:T(8,128)(2,1)}, bf16[2,512,512]{2,1,0:T(8,128)...) custom-call(s32[8,4,256]{2,1,0:T(4,128)} %copy.241.slots, ...), custom_call_target="tpu_custom_call", output_to_operand_aliasing={{5}: (8, {}), {6}: (9, {}), {7}: (10, {}), {8}: (11, {})} | custom-call | flops 6979321856 | bytes 41943040 | tf_op jit(solution)/shard_map/group_1_0/pallas_call | solution.py:667
  487.2 21.9 %group_1_1.1 = (bf16[2,512,512]{2,1,0:T(8,128)(2,1)}, bf16[2,512,512]{2,1,0:T(8,128)(2,1)}, bf16[2,512,512]{2,1,0:T(8,128)(2,1)}, bf16[2,512,512]{2,1,0:T(8,128)...) custom-call(s32[8,4,256]{2,1,0:T(4,128)} %copy.241.slots, ...), custom_call_target="tpu_custom_call", output_to_operand_aliasing={{5}: (8, {}), {6}: (9, {}), {7}: (10, {}), {8}: (11, {})} | custom-call | flops 6979321856 | bytes 41943040 | tf_op jit(solution)/shard_map/group_1_1/pallas_call | solution.py:667
  509.3 22.0 %group_2_0.1 = (bf16[2,512,512]{2,1,0:T(8,128)(2,1)}, bf16[2,512,512]{2,1,0:T(8,128)(2,1)}, bf16[2,512,512]{2,1,0:T(8,128)(2,1)}, bf16[2,512,512]{2,1,0:T(8,128)...) custom-call(s32[8,4,256]{2,1,0:T(4,128)} %copy.241.slots, ...), custom_call_target="tpu_custom_call", output_to_operand_aliasing={{5}: (8, {}), {6}: (9, {}), {7}: (10, {}), {8}: (11, {})} | custom-call | flops 6979321856 | bytes 41943040 | tf_op jit(solution)/shard_map/group_2_0/pallas_call | solution.py:667
  531.8 22.0 %group_2_1.1 = (bf16[2,512,512]{2,1,0:T(8,128)(2,1)}, bf16[2,512,512]{2,1,0:T(8,128)(2,1)}, bf16[2,512,512]{2,1,0:T(8,128)(2,1)}, bf16[2,512,512]{2,1,0:T(8,128)...) custom-call(s32[8,4,256]{2,1,0:T(4,128)} %copy.241.slots, ...), custom_call_target="tpu_custom_call", output_to_operand_aliasing={{5}: (8, {}), {6}: (9, {}), {7}: (10, {}), {8}: (11, {})} | custom-call | flops 6979321856 | bytes 41943040 | tf_op jit(solution)/shard_map/group_2_1/pallas_call | solution.py:667
  554.1 21.8 %group_3_0.1 = (bf16[2,512,512]{2,1,0:T(8,128)(2,1)}, bf16[2,512,512]{2,1,0:T(8,128)(2,1)}, bf16[2,512,512]{2,1,0:T(8,128)(2,1)}, bf16[2,512,512]{2,1,0:T(8,128)...) custom-call(s32[8,4,256]{2,1,0:T(4,128)} %copy.241.slots, ...), custom_call_target="tpu_custom_call", output_to_operand_aliasing={{5}: (8, {}), {6}: (9, {}), {7}: (10, {}), {8}: (11, {})} | custom-call | flops 6979321856 | bytes 41943040 | tf_op jit(solution)/shard_map/group_3_0/pallas_call | solution.py:667
  576.9 22.0 %group_3_1.1 = (bf16[2,512,512]{2,1,0:T(8,128)(2,1)}, bf16[2,512,512]{2,1,0:T(8,128)(2,1)}, bf16[2,512,512]{2,1,0:T(8,128)(2,1)}, bf16[2,512,512]{2,1,0:T(8,128)...) custom-call(s32[8,4,256]{2,1,0:T(4,128)} %copy.241.slots, ...), custom_call_target="tpu_custom_call", output_to_operand_aliasing={{5}: (8, {}), {6}: (9, {}), {7}: (10, {}), {8}: (11, {})} | custom-call | flops 6979321856 | bytes 41943040 | tf_op jit(solution)/shard_map/group_3_1/pallas_call | solution.py:667
  598.9 10.7 %add_convert_fusion = bf16[384,2048]{1,0:T(8,128)(2,1)S(1)} fusion(f32[384,2048]{1,0:T(8,128)} %get-tuple-element.175, f32[384,2048]{1,0:T(8,128)} %get-tuple-element.174, f32[384,2048]{1,0:T(8,128)} %get-tuple-element.173, f32[384,2048]{1,0:T(8,128)} %get-tuple-element.172, f32[384,2048]{1,0:T(8,128)} %get-tuple-element.171, ...), kind=kLoop, calls=%fused_computation.42 | loop fusion | flops 6291456 | bytes 26738688 | tf_op jit(solution)/shard_map/convert.27
  611.3 5.0 all-to-all-start.1
  616.3 32.8 %weight_grads.1 = (f32[2,2048,352]{2,1,0:T(8,128)}, f32[2,2048,352]{2,1,0:T(8,128)}, f32[2,352,2048]{2,1,0:T(8,128)}) custom-call(bf16[2,8,256,2048]{3,2,1,0:T(8,128)(2,1)} %get-tuple-element.176.xs, bf16[2,8,256,2048]{3,2,1,0:T(8,128)(2,1)} %get-tuple-element.177.gs, bf16[2,8,256,768]{3,2,1,0:T(8,128)(2,1)} %get-tuple-element.178.gu, ...), custom_call_target="tpu_custom_call" | custom-call | flops 19327352832 | bytes 67108864 | tf_op jit(solution)/shard_map/weight_grads/pallas_call | solution.py:749
  649.1 6.4 copy.228
  655.5 6.5 copy.229
  682.4 8.4 collective-permute-done.89
  692.8 43.0 %collective-permute-done.71 = bf16[512,512]{1,0:T(8,128)(2,1)S(1)} collective-permute-done((bf16[512,512]{1,0:T(8,128)(2,1)S(1)}, bf16[512,512]{1,0:T(8,128)(2,1)S(1)}, u32[]{:S(2)}, u32[]{:S(2)}) %collective-permute-start.71) | collective-permute-done | bytes 524320 | tf_op jit(solution)/shard_map/ppermute | solution.py:799
  739.1 18.5 %collective-permute-done.77 = bf16[512,512]{1,0:T(8,128)(2,1)S(1)} collective-permute-done((bf16[512,512]{1,0:T(8,128)(2,1)S(1)}, bf16[512,512]{1,0:T(8,128)(2,1)S(1)}, u32[]{:S(2)}, u32[]{:S(2)}) %collective-permute-start.77) | collective-permute-done | bytes 524320 | tf_op jit(solution)/shard_map/ppermute | solution.py:799
  762.4 10.1 collective-permute-done.50
  774.9 7.4 collective-permute-done.83
  788.6 8.7 collective-permute-done.41
  800.6 10.2 collective-permute-done.81
  810.8 8.6 collective-permute-done.60
  824.9 7.6 collective-permute-done.42
  836.6 10.7 %collective-permute-done.66 = bf16[512,512]{1,0:T(8,128)(2,1)S(1)} collective-permute-done((bf16[512,512]{1,0:T(8,128)(2,1)S(1)}, bf16[512,512]{1,0:T(8,128)(2,1)S(1)}, u32[]{:S(2)}, u32[]{:S(2)}) %collective-permute-start.66) | collective-permute-done | bytes 524320 | tf_op jit(solution)/shard_map/ppermute | solution.py:799
  853.5 5.0 collective-permute-done.56
  862.1 15.1 %collective-permute-done.91 = bf16[512,512]{1,0:T(8,128)(2,1)} collective-permute-done((bf16[512,512]{1,0:T(8,128)(2,1)S(1)}, bf16[512,512]{1,0:T(8,128)(2,1)}, u32[]{:S(2)}, u32[]{:S(2)}) %collective-permute-start.91) | collective-permute-done | bytes 524320 | tf_op jit(solution)/shard_map/ppermute | solution.py:799
  882.7 4.6 fusion.3
  887.3 4.2 fusion.9
  891.5 4.3 copy.207
  921.4 3.9 copy.212
  946.8 13.7 %collective-permute-done.119 = bf16[256,512]{1,0:T(8,128)(2,1)} collective-permute-done((bf16[256,512]{1,0:T(8,128)(2,1)}, bf16[256,512]{1,0:T(8,128)(2,1)}, u32[]{:S(2)}, u32[]{:S(2)}) %collective-permute-start.119) | collective-permute-done | bytes 262176 | tf_op jit(solution)/shard_map/ppermute | solution.py:812
  979.1 3.9 collective-permute-done.112
  991.0 3.9 collective-permute-done.95
  1011.6 6.3 collective-permute-done.101
  1021.3 4.2 collective-permute-done.104
  1030.0 5.2 collective-permute-done.105
  1036.1 3.8 collective-permute-done.107
  (687 shorter events, 291.5 us)
Async XLA Ops:
  7.2 397.4 %all-gather.3.cloned.1.call-start = ((), (), s32[]{:S(2)}) async-start(), calls=%async_computation.2 | async-start | bytes 17301504 | tf_op jit(solution)/shard_map/all_gather | solution.py:1004
  12.0 39.2 %collective-permute-start.3 = (bf16[65,576]{1,0:T(8,128)(2,1)S(1)}, bf16[65,576]{1,0:T(8,128)(2,1)S(1)}, u32[]{:S(2)}, u32[]{:S(2)}) collective-permute-start(bf16[65,576]{1,0:T(8,128)(2,1)S(1)} %pad_maximum_fusion.16.refs_0_), channel_id=1, source_target_pairs={{0,4},{4,0},{8,12},{12,8},{16,20},{20,16},{24,28},{28,24},{1,5},{5... | collective-permute-start | bytes 224648 | tf_op jit(solution)/shard_map/ppermute | solution.py:812
  13.5 54.3 %collective-permute-start = (bf16[512,512]{1,0:T(8,128)(2,1)}, bf16[512,512]{1,0:T(8,128)(2,1)}, u32[]{:S(2)}, u32[]{:S(2)}) collective-permute-start(bf16[512,512]{1,0:T(8,128)(2,1)} %param.17), channel_id=1, source_target_pairs={{0,2},{1,3},{2,0},{3,1},{4,6},{5,7},{6,4},{7,5},{8,10},{9,11},{10,... | collective-permute-start | bytes 1572872 | tf_op jit(solution)/shard_map/ppermute | solution.py:799
  17.0 51.8 %collective-permute-start.14 = (bf16[256,1536]{1,0:T(8,128)(2,1)S(1)}, bf16[256,1536]{1,0:T(8,128)(2,1)S(1)}, u32[]{:S(2)}, u32[]{:S(2)}) collective-permute-start(bf16[256,1536]{1,0:T(8,128)(2,1)S(1)} %maximum_maximum_fusion.refs_0_), channel_id=1, source_target_pairs={{0,8},{4,12},{8,16},{12,20},{16,24},{20,28},{24,0},{28,4},{1,9},{5... | collective-permute-start | bytes 2359304 | tf_op jit(solution)/shard_map/ppermute | solution.py:817
  18.6 31.9 %collective-permute-start.6 = (bf16[65,576]{1,0:T(8,128)(2,1)S(1)}, bf16[65,576]{1,0:T(8,128)(2,1)S(1)}, u32[]{:S(2)}, u32[]{:S(2)}) collective-permute-start(bf16[65,576]{1,0:T(8,128)(2,1)S(1)} %collective-permute-done.4.refs_2_), channel_id=1, source_target_pairs={{0,8},{4,12},{8,16},{12,20},{16,24},{20,28},{24,0},{28,4},{1,9},{5... | collective-permute-start | bytes 224648 | tf_op jit(solution)/shard_map/ppermute | solution.py:817
  61.1 76.3 %collective-permute-start.13 = (bf16[256,1536]{1,0:T(8,128)(2,1)S(1)}, bf16[256,1536]{1,0:T(8,128)(2,1)S(1)}, u32[]{:S(2)}, u32[]{:S(2)}) collective-permute-start(bf16[256,1536]{1,0:T(8,128)(2,1)S(1)} %maximum_maximum_fusion.refs_0_), channel_id=1, source_target_pairs={{0,4},{4,0},{8,12},{12,8},{16,20},{20,16},{24,28},{28,24},{1,5},{5... | collective-permute-start | bytes 2359304 | tf_op jit(solution)/shard_map/ppermute | solution.py:812
  68.8 30.2 %collective-permute-start.16 = (bf16[256,1536]{1,0:T(8,128)(2,1)S(1)}, bf16[256,1536]{1,0:T(8,128)(2,1)}, u32[]{:S(2)}, u32[]{:S(2)}) collective-permute-start(bf16[256,1536]{1,0:T(8,128)(2,1)S(1)} %collective-permute-done.14.refs_2_), channel_id=1, source_target_pairs={{0,8},{4,12},{8,16},{12,20},{16,24},{20,28},{24,0},{28,4},{1,9},{5... | collective-permute-start | bytes 2359304 | tf_op jit(solution)/shard_map/ppermute | solution.py:817
  79.7 57.8 %collective-permute-start.15 = (bf16[256,1536]{1,0:T(8,128)(2,1)S(1)}, bf16[256,1536]{1,0:T(8,128)(2,1)}, u32[]{:S(2)}, u32[]{:S(2)}) collective-permute-start(bf16[256,1536]{1,0:T(8,128)(2,1)S(1)} %collective-permute-done.14.refs_2_), channel_id=1, source_target_pairs={{0,4},{4,0},{8,12},{12,8},{16,20},{20,16},{24,28},{28,24},{1,5},{5... | collective-permute-start | bytes 2359304 | tf_op jit(solution)/shard_map/ppermute | solution.py:812
  99.0 34.1 %collective-permute-start.18 = (bf16[256,1536]{1,0:T(8,128)(2,1)}, bf16[256,1536]{1,0:T(8,128)(2,1)}, u32[]{:S(2)}, u32[]{:S(2)}) collective-permute-start(bf16[256,1536]{1,0:T(8,128)(2,1)} %collective-permute-done.16.refs_4_), channel_id=1, source_target_pairs={{0,8},{4,12},{8,16},{12,20},{16,24},{20,28},{24,0},{28,4},{1,9},{5... | collective-permute-start | bytes 2359304 | tf_op jit(solution)/shard_map/ppermute | solution.py:817
  103.0 40.6 %collective-permute-start.17 = (bf16[256,1536]{1,0:T(8,128)(2,1)}, bf16[256,1536]{1,0:T(8,128)(2,1)}, u32[]{:S(2)}, u32[]{:S(2)}) collective-permute-start(bf16[256,1536]{1,0:T(8,128)(2,1)} %collective-permute-done.16.refs_4_), channel_id=1, source_target_pairs={{0,4},{4,0},{8,12},{12,8},{16,20},{20,16},{24,28},{28,24},{1,5},{5... | collective-permute-start | bytes 2359304 | tf_op jit(solution)/shard_map/ppermute | solution.py:812
  133.1 37.6 %collective-permute-start.19 = (bf16[256,1536]{1,0:T(8,128)(2,1)}, bf16[256,1536]{1,0:T(8,128)(2,1)}, u32[]{:S(2)}, u32[]{:S(2)}) collective-permute-start(bf16[256,1536]{1,0:T(8,128)(2,1)} %collective-permute-done.18.refs_6_), channel_id=1, source_target_pairs={{0,4},{4,0},{8,12},{12,8},{16,20},{20,16},{24,28},{28,24},{1,5},{5... | collective-permute-start | bytes 2359304 | tf_op jit(solution)/shard_map/ppermute | solution.py:812
  216.1 25.3 %collective-permute-start.21 = (bf16[512,2,512]{2,0,1:T(8,128)(2,1)S(1)}, bf16[512,2,512]{2,0,1:T(8,128)(2,1)S(1)}, u32[]{:S(2)}, u32[]{:S(2)}) collective-permute-start(bf16[512,2,512]{2,0,1:T(8,128)(2,1)S(1)} %fusion.24), channel_id=1, source_target_pairs={{0,2},{1,3},{2,0},{3,1},{4,6},{5,7},{6,4},{7,5},{8,10},{9,11},{10,... | collective-permute-start | bytes 3145736 | tf_op jit(solution)/shard_map/ppermute | solution.py:799
  276.8 28.1 %collective-permute-start.30 = (bf16[2,512,512]{2,1,0:T(8,128)(2,1)}, bf16[2,512,512]{2,1,0:T(8,128)(2,1)}, u32[]{:S(2)}, u32[]{:S(2)}) collective-permute-start(bf16[2,512,512]{2,1,0:T(8,128)(2,1)} %pad_maximum_fusion.4.mx_own), channel_id=1, source_target_pairs={{0,8},{4,12},{8,16},{12,20},{16,24},{20,28},{24,0},{28,4},{1,9},{5... | collective-permute-start | bytes 3145736 | tf_op jit(solution)/shard_map/ppermute | solution.py:817
  278.0 120.6 %all-to-all-start = ((bf16[8,264,256]{2,1,0:T(8,128)(2,1)}), bf16[8,264,256]{2,1,0:T(8,128)(2,1)}, u32[]{:S(2)}, u32[]{:S(2)}) async-start(bf16[8,264,256]{2,1,0:T(8,128)(2,1)} %bitcast.452), calls=%async_computation | async-start | bytes 2162688 | tf_op jit(solution)/shard_map/all_to_all | solution.py:999
  304.9 83.1 %collective-permute-start.43 = (bf16[2,512,512]{2,1,0:T(8,128)(2,1)}, bf16[2,512,512]{2,1,0:T(8,128)(2,1)}, u32[]{:S(2)}, u32[]{:S(2)}) collective-permute-start(bf16[2,512,512]{2,1,0:T(8,128)(2,1)} %collective-permute-done.30.mx_own), channel_id=1, source_target_pairs={{0,8},{4,12},{8,16},{12,20},{16,24},{20,28},{24,0},{28,4},{1,9},{5... | collective-permute-start | bytes 3145736 | tf_op jit(solution)/shard_map/ppermute | solution.py:817
  305.3 39.7 %collective-permute-start.24 = (f32[12,512]{1,0:T(8,128)S(1)}, f32[12,512]{1,0:T(8,128)S(1)}, u32[]{:S(2)}, u32[]{:S(2)}) collective-permute-start(f32[12,512]{1,0:T(8,128)S(1)} %pad_maximum_fusion.18.refs_0_), channel_id=1, source_target_pairs={{0,8},{4,12},{8,16},{12,20},{16,24},{20,28},{24,0},{28,4},{1,9},{5... | collective-permute-start | bytes 73736 | tf_op jit(solution)/shard_map/ppermute | solution.py:817
  360.9 31.2 %collective-permute-start.32 = (bf16[2,512,512]{2,1,0:T(8,128)(2,1)}, bf16[2,512,512]{2,1,0:T(8,128)(2,1)}, u32[]{:S(2)}, u32[]{:S(2)}) collective-permute-start(bf16[2,512,512]{2,1,0:T(8,128)(2,1)} %pad_maximum_fusion.4.mx_own), channel_id=1, source_target_pairs={{0,4},{4,0},{8,12},{12,8},{16,20},{20,16},{24,28},{28,24},{1,5},{5... | collective-permute-start | bytes 3145736 | tf_op jit(solution)/shard_map/ppermute | solution.py:812
  387.9 29.1 %collective-permute-start.34 = (bf16[2,512,512]{2,1,0:T(8,128)(2,1)}, bf16[2,512,512]{2,1,0:T(8,128)(2,1)}, u32[]{:S(2)}, u32[]{:S(2)}) collective-permute-start(bf16[2,512,512]{2,1,0:T(8,128)(2,1)} %pad_maximum_fusion.4.mx_own), channel_id=1, source_target_pairs={{0,1},{1,0},{2,3},{3,2},{4,5},{5,4},{6,7},{7,6},{8,9},{9,8},{10,11... | collective-permute-start | bytes 3145736 | tf_op jit(solution)/shard_map/ppermute | solution.py:799
  388.0 29.3 %collective-permute-start.53 = (bf16[2,512,512]{2,1,0:T(8,128)(2,1)}, bf16[2,512,512]{2,1,0:T(8,128)(2,1)}, u32[]{:S(2)}, u32[]{:S(2)}) collective-permute-start(bf16[2,512,512]{2,1,0:T(8,128)(2,1)} %collective-permute-done.43.mx_own), channel_id=1, source_target_pairs={{0,8},{4,12},{8,16},{12,20},{16,24},{20,28},{24,0},{28,4},{1,9},{5... | collective-permute-start | bytes 3145736 | tf_op jit(solution)/shard_map/ppermute | solution.py:817
  390.4 51.0 %collective-permute-start.37 = (bf16[2,512,512]{2,1,0:T(8,128)(2,1)}, bf16[2,512,512]{2,1,0:T(8,128)(2,1)}, u32[]{:S(2)}, u32[]{:S(2)}) collective-permute-start(bf16[2,512,512]{2,1,0:T(8,128)(2,1)} %collective-permute-done.30.mx_own), channel_id=1, source_target_pairs={{0,4},{4,0},{8,12},{12,8},{16,20},{20,16},{24,28},{28,24},{1,5},{5... | collective-permute-start | bytes 3145736 | tf_op jit(solution)/shard_map/ppermute | solution.py:812
  392.1 49.2 %collective-permute-start.33 = (bf16[2,512,512]{2,1,0:T(8,128)(2,1)}, bf16[2,512,512]{2,1,0:T(8,128)(2,1)}, u32[]{:S(2)}, u32[]{:S(2)}) collective-permute-start(bf16[2,512,512]{2,1,0:T(8,128)(2,1)} %collective-permute-done.32.mx_own), channel_id=1, source_target_pairs={{0,1},{1,0},{2,3},{3,2},{4,5},{5,4},{6,7},{7,6},{8,9},{9,8},{10,11... | collective-permute-start | bytes 3145736 | tf_op jit(solution)/shard_map/ppermute | solution.py:799
  404.1 59.5 %collective-permute-start.31 = (bf16[2,512,512]{2,1,0:T(8,128)(2,1)}, bf16[2,512,512]{2,1,0:T(8,128)(2,1)S(1)}, u32[]{:S(2)}, u32[]{:S(2)}) collective-permute-start(bf16[2,512,512]{2,1,0:T(8,128)(2,1)} %collective-permute-done.30.mx_own), channel_id=1, source_target_pairs={{0,1},{1,0},{2,3},{3,2},{4,5},{5,4},{6,7},{7,6},{8,9},{9,8},{10,11... | collective-permute-start | bytes 3145736 | tf_op jit(solution)/shard_map/ppermute | solution.py:799
  417.0 46.8 %collective-permute-start.47 = (bf16[2,512,512]{2,1,0:T(8,128)(2,1)}, bf16[2,512,512]{2,1,0:T(8,128)(2,1)S(1)}, u32[]{:S(2)}, u32[]{:S(2)}) collective-permute-start(bf16[2,512,512]{2,1,0:T(8,128)(2,1)} %collective-permute-done.43.mx_own), channel_id=1, source_target_pairs={{0,4},{4,0},{8,12},{12,8},{16,20},{20,16},{24,28},{28,24},{1,5},{5... | collective-permute-start | bytes 3145736 | tf_op jit(solution)/shard_map/ppermute | solution.py:812
  417.3 47.5 %collective-permute-start.57 = (bf16[2,512,512]{2,1,0:T(8,128)(2,1)}, bf16[2,512,512]{2,1,0:T(8,128)(2,1)S(1)}, u32[]{:S(2)}, u32[]{:S(2)}) collective-permute-start(bf16[2,512,512]{2,1,0:T(8,128)(2,1)} %collective-permute-done.53.mx_own), channel_id=1, source_target_pairs={{0,4},{4,0},{8,12},{12,8},{16,20},{20,16},{24,28},{28,24},{1,5},{5... | collective-permute-start | bytes 3145736 | tf_op jit(solution)/shard_map/ppermute | solution.py:812
  441.3 67.8 %collective-permute-start.44 = (bf16[2,512,512]{2,1,0:T(8,128)(2,1)}, bf16[2,512,512]{2,1,0:T(8,128)(2,1)}, u32[]{:S(2)}, u32[]{:S(2)}) collective-permute-start(bf16[2,512,512]{2,1,0:T(8,128)(2,1)} %collective-permute-done.43.mx_own), channel_id=1, source_target_pairs={{0,1},{1,0},{2,3},{3,2},{4,5},{5,4},{6,7},{7,6},{8,9},{9,8},{10,11... | collective-permute-start | bytes 3145736 | tf_op jit(solution)/shard_map/ppermute | solution.py:799
  441.3 45.4 %collective-permute-start.38 = (bf16[2,512,512]{2,1,0:T(8,128)(2,1)}, bf16[2,512,512]{2,1,0:T(8,128)(2,1)}, u32[]{:S(2)}, u32[]{:S(2)}) collective-permute-start(bf16[2,512,512]{2,1,0:T(8,128)(2,1)} %collective-permute-done.37.mx_own), channel_id=1, source_target_pairs={{0,1},{1,0},{2,3},{3,2},{4,5},{5,4},{6,7},{7,6},{8,9},{9,8},{10,11... | collective-permute-start | bytes 3145736 | tf_op jit(solution)/shard_map/ppermute | solution.py:799
  463.6 90.2 %collective-permute-start.54 = (bf16[2,512,512]{2,1,0:T(8,128)(2,1)}, bf16[2,512,512]{2,1,0:T(8,128)(2,1)}, u32[]{:S(2)}, u32[]{:S(2)}) collective-permute-start(bf16[2,512,512]{2,1,0:T(8,128)(2,1)} %collective-permute-done.53.mx_own), channel_id=1, source_target_pairs={{0,1},{1,0},{2,3},{3,2},{4,5},{5,4},{6,7},{7,6},{8,9},{9,8},{10,11... | collective-permute-start | bytes 3145736 | tf_op jit(solution)/shard_map/ppermute | solution.py:799
  463.8 67.5 %collective-permute-start.48 = (bf16[2,512,512]{2,1,0:T(8,128)(2,1)S(1)}, bf16[2,512,512]{2,1,0:T(8,128)(2,1)}, u32[]{:S(2)}, u32[]{:S(2)}) collective-permute-start(bf16[2,512,512]{2,1,0:T(8,128)(2,1)S(1)} %collective-permute-done.47.mx_own), channel_id=1, source_target_pairs={{0,1},{1,0},{2,3},{3,2},{4,5},{5,4},{6,7},{7,6},{8,9},{9,8},{10,11... | collective-permute-start | bytes 3145736 | tf_op jit(solution)/shard_map/ppermute | solution.py:799
  464.8 111.1 %collective-permute-start.58 = (bf16[2,512,512]{2,1,0:T(8,128)(2,1)S(1)}, bf16[2,512,512]{2,1,0:T(8,128)(2,1)S(1)}, u32[]{:S(2)}, u32[]{:S(2)}) collective-permute-start(bf16[2,512,512]{2,1,0:T(8,128)(2,1)S(1)} %collective-permute-done.57.mx_own), channel_id=1, source_target_pairs={{0,1},{1,0},{2,3},{3,2},{4,5},{5,4},{6,7},{7,6},{8,9},{9,8},{10,11... | collective-permute-start | bytes 3145736 | tf_op jit(solution)/shard_map/ppermute | solution.py:799
  486.8 175.2 %collective-permute-start.63 = (bf16[2,512,512]{2,1,0:T(8,128)(2,1)}, bf16[2,512,512]{2,1,0:T(8,128)(2,1)}, u32[]{:S(2)}, u32[]{:S(2)}) collective-permute-start(bf16[2,512,512]{2,1,0:T(8,128)(2,1)} %get-tuple-element.140), channel_id=1, source_target_pairs={{0,1},{1,0},{2,3},{3,2},{4,5},{5,4},{6,7},{7,6},{8,9},{9,8},{10,11... | collective-permute-start | bytes 3145736 | tf_op jit(solution)/shard_map/ppermute | solution.py:799
  509.1 154.3 %collective-permute-start.86 = (bf16[2,512,512]{2,1,0:T(8,128)(2,1)}, bf16[2,512,512]{2,1,0:T(8,128)(2,1)}, u32[]{:S(2)}, u32[]{:S(2)}) collective-permute-start(bf16[2,512,512]{2,1,0:T(8,128)(2,1)} %get-tuple-element.156), channel_id=1, source_target_pairs={{0,1},{1,0},{2,3},{3,2},{4,5},{5,4},{6,7},{7,6},{8,9},{9,8},{10,11... | collective-permute-start | bytes 3145736 | tf_op jit(solution)/shard_map/ppermute | solution.py:799
  531.3 134.1 %collective-permute-start.65 = (bf16[2,512,512]{2,1,0:T(8,128)(2,1)}, bf16[2,512,512]{2,1,0:T(8,128)(2,1)}, u32[]{:S(2)}, u32[]{:S(2)}) collective-permute-start(bf16[2,512,512]{2,1,0:T(8,128)(2,1)} %get-tuple-element.142), channel_id=1, source_target_pairs={{0,1},{1,0},{2,3},{3,2},{4,5},{5,4},{6,7},{7,6},{8,9},{9,8},{10,11... | collective-permute-start | bytes 3145736 | tf_op jit(solution)/shard_map/ppermute | solution.py:799
  553.9 113.1 %collective-permute-start.88 = (bf16[2,512,512]{2,1,0:T(8,128)(2,1)}, bf16[2,512,512]{2,1,0:T(8,128)(2,1)}, u32[]{:S(2)}, u32[]{:S(2)}) collective-permute-start(bf16[2,512,512]{2,1,0:T(8,128)(2,1)} %get-tuple-element.158), channel_id=1, source_target_pairs={{0,1},{1,0},{2,3},{3,2},{4,5},{5,4},{6,7},{7,6},{8,9},{9,8},{10,11... | collective-permute-start | bytes 3145736 | tf_op jit(solution)/shard_map/ppermute | solution.py:799
  575.9 92.9 %collective-permute-start.35 = (bf16[2,512,512]{2,1,0:T(8,128)(2,1)}, bf16[2,512,512]{2,1,0:T(8,128)(2,1)}, u32[]{:S(2)}, u32[]{:S(2)}) collective-permute-start(bf16[2,512,512]{2,1,0:T(8,128)(2,1)} %get-tuple-element.108), channel_id=1, source_target_pairs={{0,1},{1,0},{2,3},{3,2},{4,5},{5,4},{6,7},{7,6},{8,9},{9,8},{10,11... | collective-permute-start | bytes 3145736 | tf_op jit(solution)/shard_map/ppermute | solution.py:799
  611.3 250.5 %all-to-all-start.1 = ((bf16[8,264,256]{2,1,0:T(8,128)(2,1)}), bf16[8,264,256]{2,1,0:T(8,128)(2,1)S(1)}, u32[]{:S(2)}, u32[]{:S(2)}) async-start(bf16[8,264,256]{2,1,0:T(8,128)(2,1)} %bitcast.145), calls=%async_computation.1 | async-start | bytes 2162688 | tf_op jit(solution)/shard_map/all_to_all | solution.py:1115
  676.9 110.9 %collective-permute-start.36 = (bf16[512,512]{1,0:T(8,128)(2,1)S(1)}, bf16[512,512]{1,0:T(8,128)(2,1)S(1)}, u32[]{:S(2)}, u32[]{:S(2)}) collective-permute-start(bf16[512,512]{1,0:T(8,128)(2,1)S(1)} %fusion.68), channel_id=1, source_target_pairs={{0,2},{1,3},{2,0},{3,1},{4,6},{5,7},{6,4},{7,5},{8,10},{9,11},{10,... | collective-permute-start | bytes 1572872 | tf_op jit(solution)/shard_map/ppermute | solution.py:799
  679.0 79.5 %collective-permute-start.69 = (bf16[512,512]{1,0:T(8,128)(2,1)S(1)}, bf16[512,512]{1,0:T(8,128)(2,1)S(1)}, u32[]{:S(2)}, u32[]{:S(2)}) collective-permute-start(bf16[512,512]{1,0:T(8,128)(2,1)S(1)} %fusion.76), channel_id=1, source_target_pairs={{0,2},{1,3},{2,0},{3,1},{4,6},{5,7},{6,4},{7,5},{8,10},{9,11},{10,... | collective-permute-start | bytes 1572872 | tf_op jit(solution)/shard_map/ppermute | solution.py:799
  679.9 56.7 %collective-permute-start.40 = (bf16[512,512]{1,0:T(8,128)(2,1)S(1)}, bf16[512,512]{1,0:T(8,128)(2,1)S(1)}, u32[]{:S(2)}, u32[]{:S(2)}) collective-permute-start(bf16[512,512]{1,0:T(8,128)(2,1)S(1)} %fusion.69), channel_id=1, source_target_pairs={{0,2},{1,3},{2,0},{3,1},{4,6},{5,7},{6,4},{7,5},{8,10},{9,11},{10,... | collective-permute-start | bytes 1572872 | tf_op jit(solution)/shard_map/ppermute | solution.py:799
  681.5 54.3 %collective-permute-start.71 = (bf16[512,512]{1,0:T(8,128)(2,1)S(1)}, bf16[512,512]{1,0:T(8,128)(2,1)S(1)}, u32[]{:S(2)}, u32[]{:S(2)}) collective-permute-start(bf16[512,512]{1,0:T(8,128)(2,1)S(1)} %fusion.77), channel_id=1, source_target_pairs={{0,2},{1,3},{2,0},{3,1},{4,6},{5,7},{6,4},{7,5},{8,10},{9,11},{10,... | collective-permute-start | bytes 1572872 | tf_op jit(solution)/shard_map/ppermute | solution.py:799
  690.8 93.8 %collective-permute-start.75 = (bf16[512,512]{1,0:T(8,128)(2,1)S(1)}, bf16[512,512]{1,0:T(8,128)(2,1)S(1)}, u32[]{:S(2)}, u32[]{:S(2)}) collective-permute-start(bf16[512,512]{1,0:T(8,128)(2,1)S(1)} %fusion.78), channel_id=1, source_target_pairs={{0,2},{1,3},{2,0},{3,1},{4,6},{5,7},{6,4},{7,5},{8,10},{9,11},{10,... | collective-permute-start | bytes 1572872 | tf_op jit(solution)/shard_map/ppermute | solution.py:799
  735.7 21.9 %collective-permute-start.77 = (bf16[512,512]{1,0:T(8,128)(2,1)S(1)}, bf16[512,512]{1,0:T(8,128)(2,1)S(1)}, u32[]{:S(2)}, u32[]{:S(2)}) collective-permute-start(bf16[512,512]{1,0:T(8,128)(2,1)S(1)} %fusion.79), channel_id=1, source_target_pairs={{0,2},{1,3},{2,0},{3,1},{4,6},{5,7},{6,4},{7,5},{8,10},{9,11},{10,... | collective-permute-start | bytes 1572872 | tf_op jit(solution)/shard_map/ppermute | solution.py:799
  736.7 23.3 %collective-permute-start.72 = (bf16[512,512]{1,0:T(8,128)(2,1)S(1)}, bf16[512,512]{1,0:T(8,128)(2,1)S(1)}, u32[]{:S(2)}, u32[]{:S(2)}) collective-permute-start(bf16[512,512]{1,0:T(8,128)(2,1)S(1)} %fusion.44), channel_id=1, source_target_pairs={{0,4},{4,0},{8,12},{12,8},{16,20},{20,16},{24,28},{28,24},{1,5},{5... | collective-permute-start | bytes 1572872 | tf_op jit(solution)/shard_map/ppermute | solution.py:812
  758.6 23.7 %collective-permute-start.83 = (bf16[512,512]{1,0:T(8,128)(2,1)S(1)}, bf16[512,512]{1,0:T(8,128)(2,1)S(1)}, u32[]{:S(2)}, u32[]{:S(2)}) collective-permute-start(bf16[512,512]{1,0:T(8,128)(2,1)S(1)} %fusion.81), channel_id=1, source_target_pairs={{0,2},{1,3},{2,0},{3,1},{4,6},{5,7},{6,4},{7,5},{8,10},{9,11},{10,... | collective-permute-start | bytes 1572872 | tf_op jit(solution)/shard_map/ppermute | solution.py:799
  760.0 25.5 %collective-permute-start.78 = (bf16[512,512]{1,0:T(8,128)(2,1)S(1)}, bf16[512,512]{1,0:T(8,128)(2,1)S(1)}, u32[]{:S(2)}, u32[]{:S(2)}) collective-permute-start(bf16[512,512]{1,0:T(8,128)(2,1)S(1)} %fusion.42), channel_id=1, source_target_pairs={{0,4},{4,0},{8,12},{12,8},{16,20},{20,16},{24,28},{28,24},{1,5},{5... | collective-permute-start | bytes 1572872 | tf_op jit(solution)/shard_map/ppermute | solution.py:812
  784.7 38.9 %collective-permute-start.46 = (bf16[512,512]{1,0:T(8,128)(2,1)S(1)}, bf16[512,512]{1,0:T(8,128)(2,1)S(1)}, u32[]{:S(2)}, u32[]{:S(2)}) collective-permute-start(bf16[512,512]{1,0:T(8,128)(2,1)S(1)} %fusion.70), channel_id=1, source_target_pairs={{0,2},{1,3},{2,0},{3,1},{4,6},{5,7},{6,4},{7,5},{8,10},{9,11},{10,... | collective-permute-start | bytes 1572872 | tf_op jit(solution)/shard_map/ppermute | solution.py:799
  785.4 25.4 %collective-permute-start.81 = (bf16[512,512]{1,0:T(8,128)(2,1)S(1)}, bf16[512,512]{1,0:T(8,128)(2,1)S(1)}, u32[]{:S(2)}, u32[]{:S(2)}) collective-permute-start(bf16[512,512]{1,0:T(8,128)(2,1)S(1)} %fusion.80), channel_id=1, source_target_pairs={{0,2},{1,3},{2,0},{3,1},{4,6},{5,7},{6,4},{7,5},{8,10},{9,11},{10,... | collective-permute-start | bytes 1572872 | tf_op jit(solution)/shard_map/ppermute | solution.py:799
  786.8 32.6 %collective-permute-start.60 = (bf16[512,512]{1,0:T(8,128)(2,1)S(1)}, bf16[512,512]{1,0:T(8,128)(2,1)S(1)}, u32[]{:S(2)}, u32[]{:S(2)}) collective-permute-start(bf16[512,512]{1,0:T(8,128)(2,1)S(1)} %fusion.73), channel_id=1, source_target_pairs={{0,2},{1,3},{2,0},{3,1},{4,6},{5,7},{6,4},{7,5},{8,10},{9,11},{10,... | collective-permute-start | bytes 1572872 | tf_op jit(solution)/shard_map/ppermute | solution.py:799
  787.8 33.2 %collective-permute-start.84 = (bf16[512,512]{1,0:T(8,128)(2,1)S(1)}, bf16[512,512]{1,0:T(8,128)(2,1)S(1)}, u32[]{:S(2)}, u32[]{:S(2)}) collective-permute-start(bf16[512,512]{1,0:T(8,128)(2,1)S(1)} %fusion.40), channel_id=1, source_target_pairs={{0,4},{4,0},{8,12},{12,8},{16,20},{20,16},{24,28},{28,24},{1,5},{5... | collective-permute-start | bytes 1572872 | tf_op jit(solution)/shard_map/ppermute | solution.py:812
  797.3 24.6 %collective-permute-start.79 = (bf16[512,512]{1,0:T(8,128)(2,1)S(1)}, bf16[512,512]{1,0:T(8,128)(2,1)S(1)}, u32[]{:S(2)}, u32[]{:S(2)}) collective-permute-start(bf16[512,512]{1,0:T(8,128)(2,1)S(1)} %add_convert_fusion.13), channel_id=1, source_target_pairs={{0,8},{4,12},{8,16},{12,20},{16,24},{20,28},{24,0},{28,4},{1,9},{5... | collective-permute-start | bytes 1572872 | tf_op jit(solution)/shard_map/ppermute | solution.py:817
  821.9 25.4 %collective-permute-start.66 = (bf16[512,512]{1,0:T(8,128)(2,1)S(1)}, bf16[512,512]{1,0:T(8,128)(2,1)S(1)}, u32[]{:S(2)}, u32[]{:S(2)}) collective-permute-start(bf16[512,512]{1,0:T(8,128)(2,1)S(1)} %fusion.75), channel_id=1, source_target_pairs={{0,2},{1,3},{2,0},{3,1},{4,6},{5,7},{6,4},{7,5},{8,10},{9,11},{10,... | collective-permute-start | bytes 1572872 | tf_op jit(solution)/shard_map/ppermute | solution.py:799
  823.6 34.9 %collective-permute-start.56 = (bf16[512,512]{1,0:T(8,128)(2,1)S(1)}, bf16[512,512]{1,0:T(8,128)(2,1)S(1)}, u32[]{:S(2)}, u32[]{:S(2)}) collective-permute-start(bf16[512,512]{1,0:T(8,128)(2,1)S(1)} %fusion.72), channel_id=1, source_target_pairs={{0,2},{1,3},{2,0},{3,1},{4,6},{5,7},{6,4},{7,5},{8,10},{9,11},{10,... | collective-permute-start | bytes 1572872 | tf_op jit(solution)/shard_map/ppermute | solution.py:799
  824.3 26.4 %collective-permute-start.90 = (bf16[512,512]{1,0:T(8,128)(2,1)S(1)}, bf16[512,512]{1,0:T(8,128)(2,1)S(1)}, u32[]{:S(2)}, u32[]{:S(2)}) collective-permute-start(bf16[512,512]{1,0:T(8,128)(2,1)S(1)} %fusion.38), channel_id=1, source_target_pairs={{0,4},{4,0},{8,12},{12,8},{16,20},{20,16},{24,28},{28,24},{1,5},{5... | collective-permute-start | bytes 1572872 | tf_op jit(solution)/shard_map/ppermute | solution.py:812
  836.0 23.2 %collective-permute-start.61 = (bf16[512,512]{1,0:T(8,128)(2,1)S(1)}, bf16[512,512]{1,0:T(8,128)(2,1)S(1)}, u32[]{:S(2)}, u32[]{:S(2)}) collective-permute-start(bf16[512,512]{1,0:T(8,128)(2,1)S(1)} %fusion.48), channel_id=1, source_target_pairs={{0,4},{4,0},{8,12},{12,8},{16,20},{20,16},{24,28},{28,24},{1,5},{5... | collective-permute-start | bytes 1572872 | tf_op jit(solution)/shard_map/ppermute | solution.py:812
  850.8 27.8 %collective-permute-start.64 = (bf16[512,512]{1,0:T(8,128)(2,1)S(1)}, bf16[512,512]{1,0:T(8,128)(2,1)}, u32[]{:S(2)}, u32[]{:S(2)}) collective-permute-start(bf16[512,512]{1,0:T(8,128)(2,1)S(1)} %fusion.74), channel_id=1, source_target_pairs={{0,2},{1,3},{2,0},{3,1},{4,6},{5,7},{6,4},{7,5},{8,10},{9,11},{10,... | collective-permute-start | bytes 1572872 | tf_op jit(solution)/shard_map/ppermute | solution.py:799
  851.5 27.1 %collective-permute-start.67 = (bf16[512,512]{1,0:T(8,128)(2,1)}, bf16[512,512]{1,0:T(8,128)(2,1)}, u32[]{:S(2)}, u32[]{:S(2)}) collective-permute-start(bf16[512,512]{1,0:T(8,128)(2,1)} %fusion.46), channel_id=1, source_target_pairs={{0,4},{4,0},{8,12},{12,8},{16,20},{20,16},{24,28},{28,24},{1,5},{5... | collective-permute-start | bytes 1572872 | tf_op jit(solution)/shard_map/ppermute | solution.py:812
  935.2 32.9 %collective-permute-start.96 = (bf16[512,576]{0,1:T(8,128)(2,1)}, bf16[512,576]{0,1:T(8,128)(2,1)}, u32[]{:S(2)}, u32[]{:S(2)}) collective-permute-start(bf16[512,576]{0,1:T(8,128)(2,1)} %pad_maximum_fusion.9), channel_id=1, source_target_pairs={{0,1},{1,0},{2,3},{3,2},{4,5},{5,4},{6,7},{7,6},{8,9},{9,8},{10,11... | collective-permute-start | bytes 1769480 | tf_op jit(solution)/shard_map/ppermute | solution.py:799
  940.4 24.3 %collective-permute-start.110 = (bf16[256,1024]{1,0:T(8,128)(2,1)}, bf16[256,1024]{1,0:T(8,128)(2,1)}, u32[]{:S(2)}, u32[]{:S(2)}) collective-permute-start(bf16[256,1024]{1,0:T(8,128)(2,1)} %get-tuple-element.253), channel_id=1, source_target_pairs={{0,4},{4,0},{8,12},{12,8},{16,20},{20,16},{24,28},{28,24},{1,5},{5... | collective-permute-start | bytes 1572872 | tf_op jit(solution)/shard_map/ppermute | solution.py:812
  946.7 29.8 %collective-permute-start.94 = (bf16[512,2,512]{2,0,1:T(8,128)(2,1)}, bf16[512,2,512]{2,0,1:T(8,128)(2,1)}, u32[]{:S(2)}, u32[]{:S(2)}) collective-permute-start(bf16[512,2,512]{2,0,1:T(8,128)(2,1)} %select_bitcast_fusion), channel_id=1, source_target_pairs={{0,1},{1,0},{2,3},{3,2},{4,5},{5,4},{6,7},{7,6},{8,9},{9,8},{10,11... | collective-permute-start | bytes 3145736 | tf_op jit(solution)/shard_map/ppermute | solution.py:799
  966.7 34.9 %collective-permute-start.111 = (bf16[256,1024]{1,0:T(8,128)(2,1)}, bf16[256,1024]{1,0:T(8,128)(2,1)}, u32[]{:S(2)}, u32[]{:S(2)}) collective-permute-start(bf16[256,1024]{1,0:T(8,128)(2,1)} %fusion.36), channel_id=1, source_target_pairs={{0,8},{4,12},{8,16},{12,20},{16,24},{20,28},{24,0},{28,4},{1,9},{5... | collective-permute-start | bytes 1572872 | tf_op jit(solution)/shard_map/ppermute | solution.py:817
  974.2 31.3 %collective-permute-start.123 = (bf16[256,512]{1,0:T(8,128)(2,1)}, bf16[256,512]{1,0:T(8,128)(2,1)S(1)}, u32[]{:S(2)}, u32[]{:S(2)}) collective-permute-start(bf16[256,512]{1,0:T(8,128)(2,1)} %get-tuple-element.167), channel_id=1, source_target_pairs={{0,4},{4,0},{8,12},{12,8},{16,20},{20,16},{24,28},{28,24},{1,5},{5... | collective-permute-start | bytes 786440 | tf_op jit(solution)/shard_map/ppermute | solution.py:812
  976.5 30.5 %collective-permute-start.122 = (bf16[256,512]{1,0:T(8,128)(2,1)}, bf16[256,512]{1,0:T(8,128)(2,1)}, u32[]{:S(2)}, u32[]{:S(2)}) collective-permute-start(bf16[256,512]{1,0:T(8,128)(2,1)} %add_convert_fusion.35), channel_id=1, source_target_pairs={{0,8},{4,12},{8,16},{12,20},{16,24},{20,28},{24,0},{28,4},{1,9},{5... | collective-permute-start | bytes 786440 | tf_op jit(solution)/shard_map/ppermute | solution.py:817
  985.9 23.0 %collective-permute-start.114 = (bf16[256,1024]{1,0:T(8,128)(2,1)}, bf16[256,1024]{1,0:T(8,128)(2,1)}, u32[]{:S(2)}, u32[]{:S(2)}) collective-permute-start(bf16[256,1024]{1,0:T(8,128)(2,1)} %get-tuple-element.163), channel_id=1, source_target_pairs={{0,4},{4,0},{8,12},{12,8},{16,20},{20,16},{24,28},{28,24},{1,5},{5... | collective-permute-start | bytes 1572872 | tf_op jit(solution)/shard_map/ppermute | solution.py:812
  1009.0 38.5 %collective-permute-start.116 = (bf16[256,1024]{1,0:T(8,128)(2,1)}, bf16[256,1024]{1,0:T(8,128)(2,1)}, u32[]{:S(2)}, u32[]{:S(2)}) collective-permute-start(bf16[256,1024]{1,0:T(8,128)(2,1)} %get-tuple-element.164), channel_id=1, source_target_pairs={{0,4},{4,0},{8,12},{12,8},{16,20},{20,16},{24,28},{28,24},{1,5},{5... | collective-permute-start | bytes 1572872 | tf_op jit(solution)/shard_map/ppermute | solution.py:812
  1020.2 27.2 %collective-permute-start.115 = (bf16[256,1024]{1,0:T(8,128)(2,1)}, bf16[256,1024]{1,0:T(8,128)(2,1)}, u32[]{:S(2)}, u32[]{:S(2)}) collective-permute-start(bf16[256,1024]{1,0:T(8,128)(2,1)} %add_convert_fusion.3), channel_id=1, source_target_pairs={{0,8},{4,12},{8,16},{12,20},{16,24},{20,28},{24,0},{28,4},{1,9},{5... | collective-permute-start | bytes 1572872 | tf_op jit(solution)/shard_map/ppermute | solution.py:817
  (188 other events, 2199.7 us)
Sparse Core Ops, SparseCore 0:
  10.9 174.1 all-gather.2

commit v3 on v2

--- a/solution.py
+++ b/solution.py
@@ -525,198 +525,429 @@
     )
 
 
-def group_kernel(
-    k,
-    xr,
-    seqs,
+MESH = pl.DeviceIdType.MESH
+
+
+def mixer_kernel(
     cap,
-    slots, gates, mx_own, mx_peer, og_all, wgu, wd, shared,
-    s_xs, s_gs, s_gu, s_hid,
-    back_keep, back_send, rout_keep, rout_send, d_shared, o_xs, o_gs, o_gu, o_hid,
-    full_x, og, full_og, xs, gs, parts, backs, hid_s, gu_s, sem,
+    slots, gates, mx_in, og_all, wgu, wd, shared,
+    back_sum, routed, d_shared, o_xs, o_gs, o_gu, o_hid, mxb, mxp, cb,
+    wgu_v, wd_v, shared_v, full_x, full_og, xs, gs, gu_b, hid_b, parts, backs, hid_s, gu_s,
+    rstage, keep0, keep2, send, cstage, ysend, yb, xb, zsend, zb,
+    az_s, az_r, ax_s, ax_r, ac_s, ac_r, rc_s, rc_r, ry_s, ry_r, rx_s, rx_r, rz_s, rz_r,
+    w_sem, in_sem, og_sem, save_sem, rout_sem, cst_sem,
 ):
-    del s_xs, s_gs, s_gu, s_hid
-    e = pl.program_id(0)
-    place = lax.axis_index("tensor")
-    mine = lax.axis_index("expert")
-    ring = lax.axis_size("expert") // 2
-    group = lax.rem(mine // 2 + ring - k, ring) * 2 + jnp.bitwise_xor(lax.rem(mine, 2), xr)
-    width = og_all.shape[-1]
+    groups, tensors, count, width = og_all.shape
+    ring = groups // 2
+    seqs = count // SEQ
     half = wd.shape[1]
     units = shared.shape[0] // 3
+    chunks = D // width
+    mine = lax.axis_index("expert")
+    place_t = lax.axis_index("tensor")
+    z = lax.div(mine, 2)
+    x = lax.rem(mine, 2)
+    y = lax.div(place_t, 2)
+    c = lax.rem(place_t, 2)
+    at_x = (z * 2 + 1 - x, place_t)
+    at_y = (mine, (1 - y) * 2 + c)
+    at_c = (mine, y * 2 + 1 - c)
+    at_z = (lax.rem(z + 1, ring) * 2 + x, place_t)
+    from_z = (lax.rem(z + ring - 1, ring) * 2 + x, place_t)
+
+    def remote(src, dst, s_sem, r_sem, to):
+        return pltpu.make_async_remote_copy(
+            src_ref=src, dst_ref=dst, send_sem=s_sem, recv_sem=r_sem, device_id=to, device_id_type=MESH
+        )
+
+    def place_of(rel):
+        return lax.rem(y + rel // 2, 2) * 2 + lax.rem(c + rel % 2, 2)
 
     def cols_of(rel):
-        return pl.ds(pl.multiple_of(jnp.bitwise_xor(place, rel) * width, width), width)
+        return pl.ds(pl.multiple_of(place_of(rel) * width, width), width)
+
+    def group_of(i):
+        k = lax.div(i, 2)
+        return lax.rem(z + ring - k, ring) * 2 + lax.rem(x + lax.rem(i, 2), 2)
+
+    loads = [
+        pltpu.make_async_copy(shared, shared_v, w_sem.at[0]),
+        pltpu.make_async_copy(wgu, wgu_v, w_sem.at[1]),
+        pltpu.make_async_copy(wd, wd_v, w_sem.at[2]),
+    ]
+    for load in loads:
+        load.start()
+
+    def og_copies(i, slot):
+        g = group_of(i)
+        return [
+            pltpu.make_async_copy(
+                og_all.at[g, t],
+                full_og.at[slot, :, pl.ds(t * width, width)],
+                og_sem.at[slot, t],
+            )
+            for t in range(tensors)
+        ]
+
+    for copy in og_copies(0, 0):
+        copy.start()
+
+    barrier = pltpu.get_barrier_semaphore()
+    for to in (at_x, at_y, at_c, at_z, from_z):
+        pl.semaphore_signal(barrier, inc=1, device_id=to, device_id_type=MESH)
+    pl.semaphore_wait(barrier, 5)
+
+    def z_hop(k, src):
+        return remote(src, mxb.at[2 * k + 2], az_s.at[k], az_r.at[k], at_z)
+
+    def x_hop(k, src):
+        return remote(src, mxb.at[2 * k + 1], ax_s.at[k], ax_r.at[k], at_x)
+
+    def c_hop(i, src):
+        return remote(src, mxp.at[i], ac_s.at[i], ac_r.at[i], at_c)
+
+    z_hop(0, mx_in).start()
+    x_hop(0, mx_in).start()
+    c_hop(0, mx_in).start()
+    d_shared[...] = jnp.zeros_like(d_shared)
+    loads[0].wait()
 
     iota = lax.broadcasted_iota(jnp.int32, (cap, SEQ), 0)
 
-    def pick_of(s):
-        chosen = []
-        for j in range(EXP_DEV):
-            row = s * EXP_DEV + j
-            chosen.append((iota == slots[group, row : row + 1, :]).astype(F32).astype(BF))
-        return jnp.concatenate(chosen, axis=0)
-
-    def gate_of(s, j):
-        row = s * EXP_DEV + j
-        hit = iota == slots[group, pl.ds(row, 1), :]
-        return jnp.sum(jnp.where(hit, gates[group, pl.ds(row, 1), :], 0.0), axis=1, keepdims=True)
-
-    @pl.when(e == 0)
-    def _():
-        fetch = pltpu.make_async_copy(og_all.at[group], og, sem)
-        fetch.start()
-        for rel, ref in ((0, mx_own.at[0]), (2, mx_own.at[1]), (1, mx_peer.at[0]), (3, mx_peer.at[1])):
-            full_x[:, cols_of(rel)] = ref[...]
-        fetch.wait()
-        for t in range(D // width):
-            full_og[:, t * width : (t + 1) * width] = og[t]
+    def save_copies(i):
+        return [
+            pltpu.make_async_copy(xs, o_xs.at[:, i], save_sem.at[0]),
+            pltpu.make_async_copy(gs, o_gs.at[:, i], save_sem.at[1]),
+            pltpu.make_async_copy(gu_b, o_gu.at[:, i], save_sem.at[2]),
+            pltpu.make_async_copy(hid_b, o_hid.at[:, i], save_sem.at[3]),
+        ]
+
+    def rout_copies(i):
+        g = group_of(i)
+        return [
+            pltpu.make_async_copy(rstage.at[rel], routed.at[g, place_of(rel)], rout_sem.at[rel])
+            for rel in range(4)
+        ]
+
+    def c_back(i):
+        return remote(send.at[lax.rem(i, 2)], cb.at[i], rc_s.at[i], rc_r.at[i], at_c)
+
+    def y_back(i):
+        return remote(ysend.at[lax.rem(i, 2)], yb.at[i], ry_s.at[i], ry_r.at[i], at_y)
+
+    def x_back(k):
+        return remote(keep0.at[2 * k + 1], xb.at[k], rx_s.at[k], rx_r.at[k], at_x)
+
+    def z_back(n):
+        return remote(zsend.at[n], zb.at[n], rz_s.at[n], rz_r.at[n], at_z)
+
+    def compute(i):
+        slot = lax.rem(i, 2)
+        g = group_of(i)
+
+        @pl.when(i + 1 < groups)
+        def _():
+            for copy in og_copies(i + 1, 1 - slot):
+                copy.start()
+
+        peer = [
+            pltpu.make_async_copy(mxp.at[i, n], full_x.at[:, cols_of(2 * n + 1)], in_sem.at[2 + n])
+            for n in range(2)
+        ]
+
+        @pl.when(i == 0)
+        def _():
+            own = [
+                pltpu.make_async_copy(mx_in.at[n], full_x.at[:, cols_of(2 * n)], in_sem.at[n])
+                for n in range(2)
+            ]
+            for copy in own:
+                copy.start()
+            for copy in own:
+                copy.wait()
+
+        @pl.when(i > 0)
+        def _():
+            own = [
+                pltpu.make_async_copy(mxb.at[i, n], full_x.at[:, cols_of(2 * n)], in_sem.at[n])
+                for n in range(2)
+            ]
+            for copy in own:
+                copy.start()
+            for copy in own:
+                copy.wait()
+
+        for copy in peer:
+            copy.start()
+        for copy in peer:
+            copy.wait()
+        for copy in og_copies(i, slot):
+            copy.wait()
+
+        @pl.when(i > 0)
+        def _():
+            for copy in save_copies(i - 1):
+                copy.wait()
+
+        picks = []
+        gate_cols = []
         for s in range(seqs):
-            pick = pick_of(s)
-            gate_cols = [gate_of(s, j) for j in range(EXP_DEV)]
+            chosen = []
+            for e in range(EXP_DEV):
+                row = s * EXP_DEV + e
+                hit = iota == slots[g, row : row + 1, :]
+                gate_cols.append(
+                    jnp.sum(jnp.where(hit, gates[g, row : row + 1, :], 0.0), axis=1, keepdims=True)
+                )
+                chosen.append(hit.astype(F32).astype(BF))
+            picks.append(jnp.concatenate(chosen, axis=0))
+        for s in range(seqs):
             rows = slice(s * SEQ, (s + 1) * SEQ)
-            for c in range(D // width):
-                cols = slice(c * width, (c + 1) * width)
-                got = matmul(pick, full_x[rows, cols])
-                grad = matmul(pick, full_og[rows, cols])
-                for j in range(EXP_DEV):
-                    here = slice(s * cap, (s + 1) * cap)
-                    xs[j, here, cols] = got[j * cap : (j + 1) * cap].astype(BF)
-                    gs[j, here, cols] = (grad[j * cap : (j + 1) * cap] * gate_cols[j]).astype(BF)
-        both = matmul_rows(full_x[...], shared[: 2 * units])
+            here = slice(s * cap, (s + 1) * cap)
+            for n in range(chunks):
+                cols = slice(n * width, (n + 1) * width)
+                got = matmul(picks[s], full_x[rows, cols])
+                grad = matmul(picks[s], full_og[slot, rows, cols])
+                for e in range(EXP_DEV):
+                    xs[e, here, cols] = got[e * cap : (e + 1) * cap].astype(BF)
+                    gs[e, here, cols] = (
+                        grad[e * cap : (e + 1) * cap] * gate_cols[s * EXP_DEV + e]
+                    ).astype(BF)
+        both = matmul_rows(full_x[...], shared_v[: 2 * units])
         gated = both[:, :units]
         upper = both[:, units:]
         sig = jax.nn.sigmoid(gated)
         act = gated * sig
-        grad = matmul_rows(full_og[...], shared[2 * units :])
+        grad = matmul_rows(full_og[slot], shared_v[2 * units :])
         hid_s[...] = (act * upper).astype(BF)
         gu_s[:, :units] = (grad * upper * sig * (1.0 + gated * (1.0 - sig))).astype(BF)
         gu_s[:, units:] = (grad * act).astype(BF)
-        d_shared[: 2 * units] = matmul_cols(gu_s[...], full_x[...])
-        d_shared[2 * units :] = matmul_cols(hid_s[...], full_og[...])
-
-    x_rows = xs[e]
-    g_rows = gs[e]
-    both = matmul(x_rows, wgu[0])
-    gated = both[:, :half]
-    upper = both[:, half:]
-    sig = jax.nn.sigmoid(gated)
-    act = gated * sig
-    hidden = (act * upper).astype(BF)
-    grad_hidden = matmul_rows(g_rows, wd[0])
-    grad_gu = jnp.concatenate(
-        [
-            (grad_hidden * upper * sig * (1.0 + gated * (1.0 - sig))).astype(BF),
-            (grad_hidden * act).astype(BF),
-        ],
-        axis=1,
-    )
-    o_xs[0, 0] = x_rows
-    o_gs[0, 0] = g_rows
-    o_gu[0, 0] = grad_gu
-    o_hid[0, 0] = hidden
-    gate_col = jnp.concatenate([gate_of(s, e) for s in range(seqs)], axis=0)
-    part = (matmul(hidden, wd[0]) * gate_col).astype(BF)
-    back = matmul_rows(grad_gu, wgu[0]).astype(BF)
-    for s in range(seqs):
-        here = pl.ds(pl.multiple_of(e * cap, cap), cap)
-        parts[s, here, :] = part[s * cap : (s + 1) * cap]
-        backs[s, here, :] = back[s * cap : (s + 1) * cap]
-
-    @pl.when(e == EXP_DEV - 1)
-    def _():
-        for s in range(seqs):
-            pick = pick_of(s)
-            rows = slice(s * SEQ, (s + 1) * SEQ)
-            for rel, b_ref, r_ref, at in (
-                (0, back_keep, rout_keep, 0),
-                (2, back_keep, rout_keep, 1),
-                (1, back_send, rout_send, 0),
-                (3, back_send, rout_send, 1),
-            ):
-                cols = cols_of(rel)
-                b_ref[at, rows, :] = (
-                    matmul_cols(pick, backs[s, :, cols])
-                    + matmul(gu_s[rows, :], shared[: 2 * units, cols])
+        for n in range(chunks):
+            cols = slice(n * width, (n + 1) * width)
+            d_shared[: 2 * units, cols] += matmul_cols(gu_s[...], full_x[:, cols])
+            d_shared[2 * units :, cols] += matmul_cols(hid_s[...], full_og[slot, :, cols])
+
+        @pl.when(i == 0)
+        def _():
+            loads[1].wait()
+            loads[2].wait()
+
+        for e in range(EXP_DEV):
+            gate_col = jnp.concatenate([gate_cols[s * EXP_DEV + e] for s in range(seqs)], axis=0)
+            both = matmul(xs[e], wgu_v[e])
+            gated = both[:, :half]
+            upper = both[:, half:]
+            sig = jax.nn.sigmoid(gated)
+            act = gated * sig
+            hid_b[e] = (act * upper).astype(BF)
+            grad = matmul_rows(gs[e], wd_v[e])
+            gu_b[e, :, :half] = (grad * upper * sig * (1.0 + gated * (1.0 - sig))).astype(BF)
+            gu_b[e, :, half:] = (grad * act).astype(BF)
+            for n in range(chunks):
+                cols = slice(n * width, (n + 1) * width)
+                part = (matmul(hid_b[e], wd_v[e, :, cols]) * gate_col).astype(BF)
+                back = matmul_rows(gu_b[e], wgu_v[e, cols, :]).astype(BF)
+                for s in range(seqs):
+                    there = slice(e * cap, (e + 1) * cap)
+                    parts[s, there, cols] = part[s * cap : (s + 1) * cap]
+                    backs[s, there, cols] = back[s * cap : (s + 1) * cap]
+        for copy in save_copies(i):
+            copy.start()
+
+        @pl.when(i >= 2)
+        def _():
+            c_back(i - 2).wait_send()
+
+        @pl.when(i >= 1)
+        def _():
+            for copy in rout_copies(i - 1):
+                copy.wait()
+
+        for rel in (1, 3, 0, 2):
+            cols = cols_of(rel)
+            for s in range(seqs):
+                rows = slice(s * SEQ, (s + 1) * SEQ)
+                back = (
+                    matmul_cols(picks[s], backs[s, :, cols])
+                    + matmul(gu_s[rows, :], shared_v[: 2 * units, cols])
                 ).astype(BF)
-                r_ref[at, rows, :] = (
-                    matmul_cols(pick, parts[s, :, cols])
-                    + matmul(hid_s[rows, :], shared[2 * units :, cols])
+                if rel == 0:
+                    keep0[i, rows, :] = back
+                elif rel == 2:
+                    keep2[slot, rows, :] = back
+                else:
+                    send[slot, rel // 2, rows, :] = back
+            if rel == 3:
+                c_back(i).start()
+        for rel in range(4):
+            cols = cols_of(rel)
+            for s in range(seqs):
+                rows = slice(s * SEQ, (s + 1) * SEQ)
+                rstage[rel, rows, :] = (
+                    matmul_cols(picks[s], parts[s, :, cols])
+                    + matmul(hid_s[rows, :], shared_v[2 * units :, cols])
                 ).astype(BF)
-
-
-def run_group(k, xr, cap, slots, gates, mx, og, wgu, wd, shared, saved):
-    count, width = og.shape[-2:]
+        for copy in rout_copies(i):
+            copy.start()
+
+    def step(i, carry):
+        k = lax.div(i, 2)
+        odd = lax.rem(i, 2) == 1
+
+        @pl.when(jnp.logical_and(odd, i < groups))
+        def _():
+            x_hop(k, mxb.at[2 * k]).wait_recv()
+            c_hop(i, mxb.at[i]).start()
+
+        @pl.when(jnp.logical_and(odd, i < groups - 1))
+        def _():
+            z_hop(k, mxb.at[2 * k]).wait_recv()
+
+            @pl.when(k + 2 < ring)
+            def _():
+                z_hop(k + 1, mxb.at[2 * k + 2]).start()
+
+            x_hop(k + 1, mxb.at[2 * k + 2]).start()
+            c_hop(i + 1, mxb.at[i + 1]).start()
+
+        @pl.when(i < groups)
+        def _():
+            c_hop(i, mxb.at[i]).wait_recv()
+            compute(i)
+
+        @pl.when(jnp.logical_and(i >= 1, i < groups + 1))
+        def _():
+            j = i - 1
+            c_back(j).wait_recv()
+            fetch = pltpu.make_async_copy(cb.at[j], cstage, cst_sem)
+            fetch.start()
+
+            @pl.when(j >= 2)
+            def _():
+                y_back(j - 2).wait_send()
+
+            fetch.wait()
+            ysend[lax.rem(j, 2)] = (
+                keep2[lax.rem(j, 2)].astype(F32) + cstage[1].astype(F32)
+            ).astype(BF)
+            y_back(j).start()
+            keep0[j] = (keep0[j].astype(F32) + cstage[0].astype(F32)).astype(BF)
+
+        @pl.when(jnp.logical_and(i >= 3, i < groups + 3))
+        def _():
+            j = i - 3
+            y_back(j).wait_recv()
+            keep0[j] = (keep0[j].astype(F32) + yb[j].astype(F32)).astype(BF)
+
+            @pl.when(lax.rem(j, 2) == 1)
+            def _():
+                x_back(lax.div(j, 2)).start()
+
+        for p in range(ring):
+
+            @pl.when(i == 2 * p + 6)
+            def _():
+                x_back(p).wait_recv()
+                total = keep0[2 * p].astype(F32) + xb[p].astype(F32)
+                if p == 0:
+                    keep0[0] = total.astype(BF)
+                elif p == 1:
+                    zsend[0] = total.astype(BF)
+                    z_back(0).start()
+                else:
+                    z_back(p - 2).wait_recv()
+                    zsend[p - 1] = (total + zb[p - 2].astype(F32)).astype(BF)
+                    z_back(p - 1).start()
+
+        return carry
+
+    lax.fori_loop(0, groups + 5, step, 0)
+    z_back(ring - 2).wait_recv()
+    back_sum[...] = (keep0[0].astype(F32) + zb[ring - 2].astype(F32)).astype(BF)
+    for copy in save_copies(groups - 1):
+        copy.wait()
+    for copy in rout_copies(groups - 1):
+        copy.wait()
+    for n in range(ring - 1):
+        z_hop(n, mx_in).wait_send()
+        z_back(n).wait_send()
+    for n in range(ring):
+        x_hop(n, mx_in).wait_send()
+        x_back(n).wait_send()
+    for n in range(groups):
+        c_hop(n, mx_in).wait_send()
+    for n in (groups - 2, groups - 1):
+        c_back(n).wait_send()
+        y_back(n).wait_send()
+
+
+def run_mixer(cap, slots, gates, mx, og_all, wgu, wd, shared):
+    groups, tensors, count, width = og_all.shape
     seqs = count // SEQ
     half = wd.shape[1]
     units = shared.shape[0] // 3
-    call = k * 2 + xr
-    groups = slots.shape[0]
-    whole = lambda shape: pl.BlockSpec(shape, lambda e: (0,) * len(shape))
-    slab = lambda last: pl.BlockSpec((1, 1, seqs * cap, last), lambda e: (e, call, 0, 0))
+    ring = groups // 2
+    rows = seqs * cap
     hbm = pl.BlockSpec(memory_space=pl.ANY)
-    slab_shape = lambda last: jax.ShapeDtypeStruct((EXP_DEV, groups, seqs * cap, last), BF)
-    pair = jax.ShapeDtypeStruct((2, count, width), BF)
-    first = 8
-    args = [slots, gates, *mx, og, wgu, wd, shared]
-    aliases = {}
-    if saved is None:
-        saved = [jnp.zeros((8, 128), BF)] * 4
-    else:
-        aliases = {first + i: 5 + i for i in range(4)}
+    vmem = pl.BlockSpec(memory_space=pltpu.VMEM)
+    block = (count, width)
+    dma = pltpu.SemaphoreType.DMA
+    out = lambda shape, dtype=BF: jax.ShapeDtypeStruct(shape, dtype)
     return pl.pallas_call(
-        functools.partial(group_kernel, k, xr, seqs, cap),
-        grid=(EXP_DEV,),
-        in_specs=[
-            whole(slots.shape),
-            whole(gates.shape),
-            whole((2, count, width)),
-            whole((2, count, width)),
-            hbm,
-            pl.BlockSpec((1, D, 2 * half), lambda e: (e, 0, 0)),
-            pl.BlockSpec((1, half, D), lambda e: (e, 0, 0)),
-            whole(shared.shape),
-            hbm, hbm, hbm, hbm,
-        ],
-        out_specs=[
-            whole((2, count, width)),
-            whole((2, count, width)),
-            whole((2, count, width)),
-            whole((2, count, width)),
-            whole((3 * units, D)),
-            slab(D),
-            slab(D),
-            slab(2 * half),
-            slab(half),
-        ],
+        functools.partial(mixer_kernel, cap),
+        in_specs=[vmem, vmem, hbm, hbm, hbm, hbm, hbm],
+        out_specs=[vmem, hbm, vmem, hbm, hbm, hbm, hbm, hbm, hbm, hbm],
         out_shape=[
-            pair, pair, pair, pair,
-            jax.ShapeDtypeStruct((3 * units, D), F32),
-            slab_shape(D), slab_shape(D), slab_shape(2 * half), slab_shape(half),
+            out(block),
+            out(og_all.shape),
+            out((3 * units, D), F32),
+            out((EXP_DEV, groups, rows, D)),
+            out((EXP_DEV, groups, rows, D)),
+            out((EXP_DEV, groups, rows, 2 * half)),
+            out((EXP_DEV, groups, rows, half)),
+            out((groups, 2, *block)),
+            out((groups, 2, *block)),
+            out((groups, 2, *block)),
         ],
         scratch_shapes=[
+            pltpu.VMEM(wgu.shape, BF),
+            pltpu.VMEM(wd.shape, BF),
+            pltpu.VMEM(shared.shape, BF),
             pltpu.VMEM((count, D), BF),
-            pltpu.VMEM((D // width, count, width), BF),
-            pltpu.VMEM((count, D), BF),
-            pltpu.VMEM((EXP_DEV, seqs * cap, D), BF),
-            pltpu.VMEM((EXP_DEV, seqs * cap, D), BF),
+            pltpu.VMEM((2, count, D), BF),
+            pltpu.VMEM((EXP_DEV, rows, D), BF),
+            pltpu.VMEM((EXP_DEV, rows, D), BF),
+            pltpu.VMEM((EXP_DEV, rows, 2 * half), BF),
+            pltpu.VMEM((EXP_DEV, rows, half), BF),
             pltpu.VMEM((seqs, EXP_DEV * cap, D), BF),
             pltpu.VMEM((seqs, EXP_DEV * cap, D), BF),
             pltpu.VMEM((count, units), BF),
             pltpu.VMEM((count, 2 * units), BF),
-            pltpu.SemaphoreType.DMA,
+            pltpu.VMEM((4, *block), BF),
+            pltpu.VMEM((groups, *block), BF),
+            pltpu.VMEM((2, *block), BF),
+            pltpu.VMEM((2, 2, *block), BF),
+            pltpu.VMEM((2, *block), BF),
+            pltpu.VMEM((2, *block), BF),
+            pltpu.VMEM((groups, *block), BF),
+            pltpu.VMEM((ring, *block), BF),
+            pltpu.VMEM((ring - 1, *block), BF),
+            pltpu.VMEM((ring - 1, *block), BF),
+            dma((ring - 1,)), dma((ring - 1,)), dma((ring,)), dma((ring,)), dma((groups,)), dma((groups,)),
+            dma((groups,)), dma((groups,)), dma((groups,)), dma((groups,)), dma((ring,)), dma((ring,)),
+            dma((ring - 1,)), dma((ring - 1,)),
+            dma((3,)), dma((4,)), dma((2, tensors)), dma((4,)), dma((4,)), dma,
         ],
-        input_output_aliases=aliases,
         compiler_params=pltpu.CompilerParams(
-            dimension_semantics=("arbitrary",), vmem_limit_bytes=60 * 1024 * 1024
+            collective_id=1, has_side_effects=True, vmem_limit_bytes=60 * 1024 * 1024
         ),
         cost_estimate=pl.CostEstimate(
-            flops=EXP_DEV * seqs * cap * D * (half * 12 + SEQ * 8),
-            bytes_accessed=40 * 1024 * 1024,
-            transcendentals=EXP_DEV * seqs * cap * half,
+            flops=80_000_000_000,
+            bytes_accessed=200 * 1024 * 1024,
+            transcendentals=8_000_000,
         ),
-        name=f"group_{k}_{xr}",
-    )(*args, *saved)
+        name="mixer",
+    )(slots, gates, mx, og_all, wgu, wd, shared)
 
 
 def weight_kernel(xs, gs, gu, hid, d_gate, d_up, d_down, acc_gu, acc_d):
@@ -1055,7 +1286,6 @@
     mixer_half = jnp.stack(
         [jnp.where(low_y, view[:, 0], view[:, 1]), jnp.where(low_y, view[:, 1], view[:, 0])]
     )
-    mixer_pairs = gather_pairs(mixer_half)
 
     local_experts = (mine * EXP_DEV + jnp.arange(EXP_DEV, dtype=jnp.int32)).astype(F32)
     route_t = table[:, :TOP].reshape(groups, TOP, seqs, SEQ)
@@ -1076,40 +1306,19 @@
     wide = ((0, 0), (0, 0), (0, half - ff))
     wgu = jnp.concatenate([jnp.pad(expert_gate, wide), jnp.pad(expert_up, wide)], axis=2)
     wd = jnp.pad(expert_down, ((0, 0), (0, half - ff), (0, 0)))
-    saved = None
-    outs = {}
-    d_shared = []
-    for k in range(ring):
-        for xr in range(2):
-            rows = mixer_pairs[k][xr]
-            *out, d_sh, s0, s1, s2, s3 = run_group(
-                k, xr, cap, slot_of, gate_of, (rows, to_core(rows)), og_all, wgu, wd, shared_w, saved
-            )
-            saved = [s0, s1, s2, s3]
-            outs[k, xr] = out
-            d_shared.append(d_sh)
-
-    def over_tensor(keep, send):
-        came = to_core(send)
-        return add(keep[0], came[0], to_y(add(keep[1], came[1])))
-
-    def combine(at):
-        def total(k):
-            other = over_tensor(outs[k, 1][at], outs[k, 1][at + 1])
-            return add(over_tensor(outs[k, 0][at], outs[k, 0][at + 1]), to_x(other))
-
-        return ring_sum([functools.partial(total, k) for k in range(ring)])
-
-    back_sum = add(*combine(0))
-    rout_sum = combine(2)
+    back_sum, rout, shared_step, *saved = run_mixer(
+        cap, slot_of, gate_of, mixer_half, og_all, wgu, wd, shared_w
+    )
+    saved = saved[:4]
+    rout_sum = lax.psum_scatter(
+        rout.reshape(groups * tensors * count, width),
+        ("expert", "tensor"),
+        scatter_dimension=0,
+        tiled=True,
+    )
     total_gate, total_up, total_down = weight_grads(*saved, ff)
     middle_slice = lax.dynamic_slice_in_dim(middle, place_t * width, width, 1)
-    block_out = (
-        middle_slice + rout_sum[0].astype(F32) + rout_sum[1].astype(F32)
-    ).astype(BF)
-    shared_step = d_shared[0]
-    for term in d_shared[1:]:
-        shared_step = shared_step + term
+    block_out = (middle_slice + rout_sum.astype(F32)).astype(BF)
     shared_step = shared_step.reshape(3, wide_units, groups, rows_dev)[:, :units].astype(BF)
     shared_step = shared_step.transpose(2, 0, 1, 3).reshape(groups, 3 * units, rows_dev)
     shared_step = lax.all_to_all(shared_step, "expert", split_axis=0, concat_axis=0, tiled=True)

time: 1070 us -> 815 us (0.76)
  waiting for transfers between devices: 440 us -> 203 us
  Pallas kernels: 212 us -> 255 us
  starting transfers between devices: 106 us -> 71.7 us
  other arithmetic: 114 us -> 93.8 us
    ppermute x61 -> x21, waiting for transfers between devices: 192 us -> 43.5 us  [flip_tensor(): return lax.ppermute(x, 'tensor', [(i, i ^ mask) for i in range(size)])]
    ppermute x27 -> x18, waiting for transfers between devices: 161 us -> 103 us  [to_z(): return lax.ppermute(x, 'expert', [(i, (i + 2) % size) for i in range(size)])]
    pallas_call x8 -> x1, Pallas kernels: 175 us -> 218 us  [run_mixer(): pl.pallas_call(functools.partial(mixer_kernel, cap), in_specs=[vmem, vmem...]
    ppermute x36 -> x24, waiting for transfers between devices: 86.1 us -> 55.6 us  [to_x(): return lax.ppermute(x, 'expert', [(i, i ^ 1) for i in range(size)])]
    ppermute x61 -> x21, starting transfers between devices: 28.5 us -> 10.9 us  [flip_tensor(): return lax.ppermute(x, 'tensor', [(i, i ^ mask) for i in range(size)])]
    convert_element_type x45 -> x14, other arithmetic: 33.1 us -> 18.5 us  [add(): return total.astype(BF)]
    ppermute x36 -> x24, starting transfers between devices: 33.9 us -> 20.1 us  [to_x(): return lax.ppermute(x, 'expert', [(i, i ^ 1) for i in range(size)])]
    unnamed x268 -> x196, local copies, waits for them, and re-layouts: 46.2 us -> 50.3 us
  transfers between devices with their start and end apart: 127 -> 67, of which waited for: 46 -> 24; matrix products, arithmetic and copies ran while one was open for 21% -> 30% of each run, Pallas kernels for 20% -> 5%
where the time goes in v3:
time: 815 us; the launch traced here: 808 us
  Pallas kernels  255 us (31%)
  waiting for transfers between devices  203 us (25%)
  local copies, waits for them, and re-layouts  133 us (16%)
  other arithmetic  93.8 us (12%)
  starting transfers between devices  71.7 us (9%)
  matrix products  35.1 us (4%)
  between operations  16.3 us (2%)
    pallas_call x1, Pallas kernels, run_mixer(): pl.pallas_call(functools.partial(mixer_kernel, cap), in_specs=[vmem, vmem...  218 us
    ppermute x18, waiting for transfers between devices, to_z(): return lax.ppermute(x, 'expert', [(i, (i + 2) % size) for i in range(size)])  103 us
    ppermute x24, waiting for transfers between devices, to_x(): return lax.ppermute(x, 'expert', [(i, i ^ 1) for i in range(size)])  55.6 us
    unnamed x196, local copies, waits for them, and re-layouts  50.3 us
    ppermute x21, waiting for transfers between devices, flip_tensor(): return lax.ppermute(x, 'tensor', [(i, i ^ mask) for i in range(size)])  43.5 us
    pallas_call x1, Pallas kernels, weight_grads(): pl.pallas_call(weight_kernel, grid=(EXP_DEV, groups // step), in_specs=[s...  32.9 us
    ppermute x18, starting transfers between devices, to_z(): return lax.ppermute(x, 'expert', [(i, (i + 2) % size) for i in range(size)])  30.9 us
    ppermute x24, starting transfers between devices, to_x(): return lax.ppermute(x, 'expert', [(i, i ^ 1) for i in range(size)])  20.1 us
  transfers between devices with their start and end apart: 67, of which 24 were waited for; matrix products, arithmetic and copies ran while one was open for 30% of the time, Pallas kernels for 5%

profile of v3, /device:TPU:0, one launch (start us, length us, event | category | flops | bytes accessed | tf_op | source)
XLA Modules:
  0.0 807.6 jit_solution(4208160695628435128)
XLA Ops:
  9.1 3.1 collective-permute-start.4
  20.4 30.3 %collective-permute-done.6.refs_4_ = bf16[65,576]{1,0:T(8,128)(2,1)S(1)} collective-permute-done((bf16[65,576]{1,0:T(8,128)(2,1)S(1)}, bf16[65,576]{1,0:T(8,128)(2,1)S(1)}, u32[]{:S(2)}, u32[]{:S(2)}) %collective-permute-start.6) | collective-permute-done | bytes 74912 | tf_op jit(solution)/shard_map/ppermute | solution.py:1048
  52.9 5.9 collective-permute-done.8.refs_6_
  59.0 2.3 collective-permute-done.7.refs_5_
  61.7 4.7 collective-permute-done.9.refs_7_
  69.7 10.3 %collective-permute-done.10 = bf16[8,64,576]{2,1,0:T(8,128)(2,1)} collective-permute-done((bf16[8,64,576]{2,1,0:T(8,128)(2,1)}, bf16[8,64,576]{2,1,0:T(8,128)(2,1)}, u32[]{:S(2)}, u32[]{:S(2)}) %collective-permute-start.10) | collective-permute-done | bytes 589856 | tf_op jit(solution)/shard_map/ppermute | solution.py:1030
  85.7 14.4 %collective-permute-done.16.refs_4_ = bf16[256,1536]{1,0:T(8,128)(2,1)} collective-permute-done((bf16[256,1536]{1,0:T(8,128)(2,1)S(1)}, bf16[256,1536]{1,0:T(8,128)(2,1)}, u32[]{:S(2)}, u32[]{:S(2)}) %collective-permute-start.16) | collective-permute-done | bytes 786464 | tf_op jit(solution)/shard_map/ppermute | solution.py:1048
  104.5 30.5 %collective-permute-done.18.refs_6_ = bf16[256,1536]{1,0:T(8,128)(2,1)} collective-permute-done((bf16[256,1536]{1,0:T(8,128)(2,1)}, bf16[256,1536]{1,0:T(8,128)(2,1)}, u32[]{:S(2)}, u32[]{:S(2)}) %collective-permute-start.18) | collective-permute-done | bytes 786464 | tf_op jit(solution)/shard_map/ppermute | solution.py:1048
  139.3 4.1 collective-permute-done.17.refs_5_
  143.4 27.4 %collective-permute-done.19.refs_7_ = bf16[256,1536]{1,0:T(8,128)(2,1)} collective-permute-done((bf16[256,1536]{1,0:T(8,128)(2,1)}, bf16[256,1536]{1,0:T(8,128)(2,1)}, u32[]{:S(2)}, u32[]{:S(2)}) %collective-permute-start.19) | collective-permute-done | bytes 786464 | tf_op jit(solution)/shard_map/ppermute | solution.py:1043
  170.8 2.6 place.4
  178.5 4.9 copy.155
  183.4 3.9 fusion.14
  197.4 4.4 convolution_convert_fusion.3
  201.8 3.9 copy.160
  205.7 3.0 fusion.115
  214.0 2.6 collective-permute-done.20
  220.5 4.3 collective-permute-done.24.refs_2_
  226.0 5.1 all-to-all-start
  231.4 4.6 copy.173
  235.9 4.6 copy.174
  242.5 6.6 fusion.2.wgu
  253.5 2.8 add_convert_fusion
  263.8 2.6 fusion.112
  266.4 6.6 reshape.724
  279.4 5.2 copy.163
  284.6 5.4 copy.164
  290.0 5.6 multiply_reduce_fusion.1
  298.7 217.7 %mixer.1 = (bf16[512,512]{1,0:T(8,128)(2,1)}, bf16[8,4,512,512]{3,2,1,0:T(8,128)(2,1)}, f32[384,2048]{1,0:T(8,128)}, bf16[2,8,256,2048]{3,2,1,0:T(8,128)(2,1)}, ...) custom-call(s32[8,4,256]{2,1,0:T(4,128)} %copy.213.slots, ...), custom_call_target="tpu_custom_call" | custom-call | flops 80000000000 | bytes 209715200 | tf_op jit(solution)/shard_map/mixer/pallas_call | solution.py:896
  521.3 4.6 copy.178
  526.9 32.9 %weight_grads.1 = (f32[2,2048,352]{2,1,0:T(8,128)}, f32[2,2048,352]{2,1,0:T(8,128)}, f32[2,352,2048]{2,1,0:T(8,128)}) custom-call(bf16[2,8,256,2048]{3,2,1,0:T(8,128)(2,1)} %get-tuple-element.46.xs, bf16[2,8,256,2048]{3,2,1,0:T(8,128)(2,1)} %get-tuple-element.47.gs, bf16[2,8,256,768]{3,2,1,0:T(8,128)(2,1)} %get-tuple-element.48.gu, ...), custom_call_target="tpu_custom_call" | custom-call | flops 19327352832 | bytes 67108864 | tf_op jit(solution)/shard_map/weight_grads/pallas_call | solution.py:980
  560.4 4.2 convert_bitcast_fusion
  564.6 6.4 copy.200
  571.0 6.4 copy.201
  577.4 5.3 copy.176
  589.2 4.5 all-to-all-start.1
  596.6 4.1 fusion.3
  600.8 4.1 fusion.9
  604.9 2.9 copy.179
  612.6 3.0 convolution_convert_fusion.7
  629.1 4.7 convolution_convert_fusion
  639.9 3.2 convolution_convert_fusion.2
  643.1 3.9 copy.184
  647.0 3.0 fusion.114
  652.4 2.3 copy.224
  658.9 2.3 select_bitcast_fusion
  661.2 7.2 collective-permute-done.58
  668.5 2.6 collective-permute-start.60
  672.3 3.3 collective-permute-start.59
  681.3 3.3 collective-permute-start.36
  684.6 2.4 collective-permute-done.59
  691.6 6.6 collective-permute-done.51
  698.1 3.8 collective-permute-start.61
  702.0 2.9 collective-permute-start.53
  707.5 9.2 %collective-permute-done.36 = bf16[512,576]{0,1:T(8,128)(2,1)} collective-permute-done((bf16[512,576]{0,1:T(8,128)(2,1)}, bf16[512,576]{0,1:T(8,128)(2,1)}, u32[]{:S(2)}, u32[]{:S(2)}) %collective-permute-start.36) | collective-permute-done | bytes 589856 | tf_op jit(solution)/shard_map/ppermute | solution.py:1030
  721.3 17.5 %collective-permute-done.34 = bf16[512,512]{1,0:T(8,128)(2,1)} collective-permute-done((bf16[512,512]{1,0:T(8,128)(2,1)}, bf16[512,512]{1,0:T(8,128)(2,1)}, u32[]{:S(2)}, u32[]{:S(2)}) %collective-permute-start.34) | collective-permute-done | bytes 524320 | tf_op jit(solution)/shard_map/ppermute | solution.py:1030
  738.7 3.8 multiply_reduce_fusion.5
  746.0 5.4 collective-permute-start.52
  751.5 3.3 collective-permute-start.40
  758.8 4.2 collective-permute-done.40
  773.6 9.0 %collective-permute-done.44 = bf16[65,576]{1,0:T(8,128)(2,1)S(1)} collective-permute-done((bf16[65,576]{1,0:T(8,128)(2,1)S(1)}, bf16[65,576]{1,0:T(8,128)(2,1)S(1)}, u32[]{:S(2)}, u32[]{:S(2)}) %collective-permute-start.44) | collective-permute-done | bytes 74912 | tf_op jit(solution)/shard_map/ppermute | solution.py:1048
  783.6 3.8 collective-permute-done.46
  787.3 3.3 fusion.31
  798.0 2.3 add_convert_fusion.4
  (458 shorter events, 170.3 us)
Async XLA Ops:
  7.2 291.5 %all-gather.3.cloned.1.call-start = ((), (), s32[]{:S(2)}) async-start(), calls=%async_computation.4 | async-start | bytes 17301504 | tf_op jit(solution)/shard_map/all_gather | solution.py:1235
  9.1 9.7 %collective-permute-start.4 = (bf16[65,576]{1,0:T(8,128)(2,1)S(1)}, bf16[65,576]{1,0:T(8,128)(2,1)S(1)}, u32[]{:S(2)}, u32[]{:S(2)}) collective-permute-start(bf16[65,576]{1,0:T(8,128)(2,1)S(1)} %pad_maximum_fusion.16.refs_0_), channel_id=1, source_target_pairs={{0,8},{4,12},{8,16},{12,20},{16,24},{20,28},{24,0},{28,4},{1,9},{5... | collective-permute-start | bytes 224648 | tf_op jit(solution)/shard_map/ppermute | solution.py:1048
  12.2 39.2 %collective-permute-start.3 = (bf16[65,576]{1,0:T(8,128)(2,1)S(1)}, bf16[65,576]{1,0:T(8,128)(2,1)S(1)}, u32[]{:S(2)}, u32[]{:S(2)}) collective-permute-start(bf16[65,576]{1,0:T(8,128)(2,1)S(1)} %pad_maximum_fusion.16.refs_0_), channel_id=1, source_target_pairs={{0,4},{4,0},{8,12},{12,8},{16,20},{20,16},{24,28},{28,24},{1,5},{5... | collective-permute-start | bytes 224648 | tf_op jit(solution)/shard_map/ppermute | solution.py:1043
  13.7 54.5 %collective-permute-start = (bf16[512,512]{1,0:T(8,128)(2,1)}, bf16[512,512]{1,0:T(8,128)(2,1)}, u32[]{:S(2)}, u32[]{:S(2)}) collective-permute-start(bf16[512,512]{1,0:T(8,128)(2,1)} %param.17), channel_id=1, source_target_pairs={{0,2},{1,3},{2,0},{3,1},{4,6},{5,7},{6,4},{7,5},{8,10},{9,11},{10,... | collective-permute-start | bytes 1572872 | tf_op jit(solution)/shard_map/ppermute | solution.py:1030
  17.2 52.6 %collective-permute-start.14 = (bf16[256,1536]{1,0:T(8,128)(2,1)S(1)}, bf16[256,1536]{1,0:T(8,128)(2,1)S(1)}, u32[]{:S(2)}, u32[]{:S(2)}) collective-permute-start(bf16[256,1536]{1,0:T(8,128)(2,1)S(1)} %maximum_maximum_fusion.refs_0_), channel_id=1, source_target_pairs={{0,8},{4,12},{8,16},{12,20},{16,24},{20,28},{24,0},{28,4},{1,9},{5... | collective-permute-start | bytes 2359304 | tf_op jit(solution)/shard_map/ppermute | solution.py:1048
  18.8 31.9 %collective-permute-start.6 = (bf16[65,576]{1,0:T(8,128)(2,1)S(1)}, bf16[65,576]{1,0:T(8,128)(2,1)S(1)}, u32[]{:S(2)}, u32[]{:S(2)}) collective-permute-start(bf16[65,576]{1,0:T(8,128)(2,1)S(1)} %collective-permute-done.4.refs_2_), channel_id=1, source_target_pairs={{0,8},{4,12},{8,16},{12,20},{16,24},{20,28},{24,0},{28,4},{1,9},{5... | collective-permute-start | bytes 224648 | tf_op jit(solution)/shard_map/ppermute | solution.py:1048
  50.7 8.2 %collective-permute-start.8 = (bf16[65,576]{1,0:T(8,128)(2,1)S(1)}, bf16[65,576]{1,0:T(8,128)(2,1)S(1)}, u32[]{:S(2)}, u32[]{:S(2)}) collective-permute-start(bf16[65,576]{1,0:T(8,128)(2,1)S(1)} %collective-permute-done.6.refs_4_), channel_id=1, source_target_pairs={{0,8},{4,12},{8,16},{12,20},{16,24},{20,28},{24,0},{28,4},{1,9},{5... | collective-permute-start | bytes 224648 | tf_op jit(solution)/shard_map/ppermute | solution.py:1048
  50.8 8.1 collective-permute-start.5
  51.4 9.8 %collective-permute-start.7 = (bf16[65,576]{1,0:T(8,128)(2,1)S(1)}, bf16[65,576]{1,0:T(8,128)(2,1)S(1)}, u32[]{:S(2)}, u32[]{:S(2)}) collective-permute-start(bf16[65,576]{1,0:T(8,128)(2,1)S(1)} %collective-permute-done.6.refs_4_), channel_id=1, source_target_pairs={{0,4},{4,0},{8,12},{12,8},{16,20},{20,16},{24,28},{28,24},{1,5},{5... | collective-permute-start | bytes 224648 | tf_op jit(solution)/shard_map/ppermute | solution.py:1043
  58.9 7.5 collective-permute-start.9
  58.9 10.3 %collective-permute-start.1 = (bf16[512,512]{1,0:T(8,128)(2,1)}, bf16[512,512]{1,0:T(8,128)(2,1)}, u32[]{:S(2)}, u32[]{:S(2)}) collective-permute-start(bf16[512,512]{1,0:T(8,128)(2,1)} %param.17), channel_id=1, source_target_pairs={{0,1},{1,0},{2,3},{3,2},{4,5},{5,4},{6,7},{7,6},{8,9},{9,8},{10,11... | collective-permute-start | bytes 1572872 | tf_op jit(solution)/shard_map/ppermute | solution.py:1030
  61.3 78.0 %collective-permute-start.13 = (bf16[256,1536]{1,0:T(8,128)(2,1)S(1)}, bf16[256,1536]{1,0:T(8,128)(2,1)S(1)}, u32[]{:S(2)}, u32[]{:S(2)}) collective-permute-start(bf16[256,1536]{1,0:T(8,128)(2,1)S(1)} %maximum_maximum_fusion.refs_0_), channel_id=1, source_target_pairs={{0,4},{4,0},{8,12},{12,8},{16,20},{20,16},{24,28},{28,24},{1,5},{5... | collective-permute-start | bytes 2359304 | tf_op jit(solution)/shard_map/ppermute | solution.py:1043
  68.2 11.8 %collective-permute-start.10 = (bf16[8,64,576]{2,1,0:T(8,128)(2,1)}, bf16[8,64,576]{2,1,0:T(8,128)(2,1)}, u32[]{:S(2)}, u32[]{:S(2)}) collective-permute-start(bf16[8,64,576]{2,1,0:T(8,128)(2,1)} %slice.284), channel_id=1, source_target_pairs={{0,2},{1,3},{2,0},{3,1},{4,6},{5,7},{6,4},{7,5},{8,10},{9,11},{10,... | collective-permute-start | bytes 1769480 | tf_op jit(solution)/shard_map/ppermute | solution.py:1030
  68.2 12.2 %collective-permute-start.2 = (bf16[512,512]{1,0:T(8,128)(2,1)}, bf16[512,512]{1,0:T(8,128)(2,1)}, u32[]{:S(2)}, u32[]{:S(2)}) collective-permute-start(bf16[512,512]{1,0:T(8,128)(2,1)} %collective-permute-done), channel_id=1, source_target_pairs={{0,1},{1,0},{2,3},{3,2},{4,5},{5,4},{6,7},{7,6},{8,9},{9,8},{10,11... | collective-permute-start | bytes 1572872 | tf_op jit(solution)/shard_map/ppermute | solution.py:1030
  69.2 14.2 %collective-permute-start.11 = (bf16[8,64,576]{2,1,0:T(8,128)(2,1)}, bf16[8,64,576]{2,1,0:T(8,128)(2,1)}, u32[]{:S(2)}, u32[]{:S(2)}) collective-permute-start(bf16[8,64,576]{2,1,0:T(8,128)(2,1)} %slice.284), channel_id=1, source_target_pairs={{0,1},{1,0},{2,3},{3,2},{4,5},{5,4},{6,7},{7,6},{8,9},{9,8},{10,11... | collective-permute-start | bytes 1769480 | tf_op jit(solution)/shard_map/ppermute | solution.py:1030
  69.7 30.3 %collective-permute-start.16 = (bf16[256,1536]{1,0:T(8,128)(2,1)S(1)}, bf16[256,1536]{1,0:T(8,128)(2,1)}, u32[]{:S(2)}, u32[]{:S(2)}) collective-permute-start(bf16[256,1536]{1,0:T(8,128)(2,1)S(1)} %collective-permute-done.14.refs_2_), channel_id=1, source_target_pairs={{0,8},{4,12},{8,16},{12,20},{16,24},{20,28},{24,0},{28,4},{1,9},{5... | collective-permute-start | bytes 2359304 | tf_op jit(solution)/shard_map/ppermute | solution.py:1048
  80.1 59.2 %collective-permute-start.15 = (bf16[256,1536]{1,0:T(8,128)(2,1)S(1)}, bf16[256,1536]{1,0:T(8,128)(2,1)}, u32[]{:S(2)}, u32[]{:S(2)}) collective-permute-start(bf16[256,1536]{1,0:T(8,128)(2,1)S(1)} %collective-permute-done.14.refs_2_), channel_id=1, source_target_pairs={{0,4},{4,0},{8,12},{12,8},{16,20},{20,16},{24,28},{28,24},{1,5},{5... | collective-permute-start | bytes 2359304 | tf_op jit(solution)/shard_map/ppermute | solution.py:1043
  100.1 34.9 %collective-permute-start.18 = (bf16[256,1536]{1,0:T(8,128)(2,1)}, bf16[256,1536]{1,0:T(8,128)(2,1)}, u32[]{:S(2)}, u32[]{:S(2)}) collective-permute-start(bf16[256,1536]{1,0:T(8,128)(2,1)} %collective-permute-done.16.refs_4_), channel_id=1, source_target_pairs={{0,8},{4,12},{8,16},{12,20},{16,24},{20,28},{24,0},{28,4},{1,9},{5... | collective-permute-start | bytes 2359304 | tf_op jit(solution)/shard_map/ppermute | solution.py:1048
  104.4 39.0 %collective-permute-start.17 = (bf16[256,1536]{1,0:T(8,128)(2,1)}, bf16[256,1536]{1,0:T(8,128)(2,1)}, u32[]{:S(2)}, u32[]{:S(2)}) collective-permute-start(bf16[256,1536]{1,0:T(8,128)(2,1)} %collective-permute-done.16.refs_4_), channel_id=1, source_target_pairs={{0,4},{4,0},{8,12},{12,8},{16,20},{20,16},{24,28},{28,24},{1,5},{5... | collective-permute-start | bytes 2359304 | tf_op jit(solution)/shard_map/ppermute | solution.py:1043
  134.9 35.9 %collective-permute-start.19 = (bf16[256,1536]{1,0:T(8,128)(2,1)}, bf16[256,1536]{1,0:T(8,128)(2,1)}, u32[]{:S(2)}, u32[]{:S(2)}) collective-permute-start(bf16[256,1536]{1,0:T(8,128)(2,1)} %collective-permute-done.18.refs_6_), channel_id=1, source_target_pairs={{0,4},{4,0},{8,12},{12,8},{16,20},{20,16},{24,28},{28,24},{1,5},{5... | collective-permute-start | bytes 2359304 | tf_op jit(solution)/shard_map/ppermute | solution.py:1043
  218.1 35.4 %collective-permute-start.21 = (bf16[512,2,512]{2,0,1:T(8,128)(2,1)}, bf16[512,2,512]{2,0,1:T(8,128)(2,1)}, u32[]{:S(2)}, u32[]{:S(2)}) collective-permute-start(bf16[512,2,512]{2,0,1:T(8,128)(2,1)} %fusion.24), channel_id=1, source_target_pairs={{0,2},{1,3},{2,0},{3,1},{4,6},{5,7},{6,4},{7,5},{8,10},{9,11},{10,... | collective-permute-start | bytes 3145736 | tf_op jit(solution)/shard_map/ppermute | solution.py:1030
  219.1 5.8 collective-permute-start.24
  220.5 37.9 %collective-permute-start.23 = (f32[12,512]{1,0:T(8,128)S(1)}, f32[12,512]{1,0:T(8,128)S(1)}, u32[]{:S(2)}, u32[]{:S(2)}) collective-permute-start(f32[12,512]{1,0:T(8,128)S(1)} %pad_maximum_fusion.18.refs_0_), channel_id=1, source_target_pairs={{0,4},{4,0},{8,12},{12,8},{16,20},{20,16},{24,28},{28,24},{1,5},{5... | collective-permute-start | bytes 73736 | tf_op jit(solution)/shard_map/ppermute | solution.py:1043
  224.8 15.7 %collective-permute-start.26 = (f32[12,512]{1,0:T(8,128)S(1)}, f32[12,512]{1,0:T(8,128)S(1)}, u32[]{:S(2)}, u32[]{:S(2)}) collective-permute-start(f32[12,512]{1,0:T(8,128)S(1)} %collective-permute-done.24.refs_2_), channel_id=1, source_target_pairs={{0,8},{4,12},{8,16},{12,20},{16,24},{20,28},{24,0},{28,4},{1,9},{5... | collective-permute-start | bytes 73736 | tf_op jit(solution)/shard_map/ppermute | solution.py:1048
  226.0 47.0 %all-to-all-start = ((bf16[8,264,256]{2,1,0:T(8,128)(2,1)}), bf16[8,264,256]{2,1,0:T(8,128)(2,1)S(1)}, u32[]{:S(2)}, u32[]{:S(2)}) async-start(bf16[8,264,256]{2,1,0:T(8,128)(2,1)} %bitcast.325), calls=%async_computation | async-start | bytes 2162688 | tf_op jit(solution)/shard_map/all_to_all | solution.py:1230
  231.1 566.9 %reduce-scatter.2.cloned.1.call-start = ((), (), s32[]{:S(2)}) async-start(), calls=%async_computation.3 | async-start | bytes 17301504 | tf_op jit(solution)/shard_map/reduce_scatter | solution.py:1313
  240.5 11.6 %collective-permute-start.28 = (f32[12,512]{1,0:T(8,128)S(1)}, f32[12,512]{1,0:T(8,128)S(1)}, u32[]{:S(2)}, u32[]{:S(2)}) collective-permute-start(f32[12,512]{1,0:T(8,128)S(1)} %collective-permute-done.26.refs_4_), channel_id=1, source_target_pairs={{0,8},{4,12},{8,16},{12,20},{16,24},{20,28},{24,0},{28,4},{1,9},{5... | collective-permute-start | bytes 73736 | tf_op jit(solution)/shard_map/ppermute | solution.py:1048
  249.1 9.4 %collective-permute-start.25 = (f32[12,512]{1,0:T(8,128)S(1)}, f32[12,512]{1,0:T(8,128)S(1)}, u32[]{:S(2)}, u32[]{:S(2)}) collective-permute-start(f32[12,512]{1,0:T(8,128)S(1)} %collective-permute-done.24.refs_2_), channel_id=1, source_target_pairs={{0,4},{4,0},{8,12},{12,8},{16,20},{20,16},{24,28},{28,24},{1,5},{5... | collective-permute-start | bytes 73736 | tf_op jit(solution)/shard_map/ppermute | solution.py:1043
  250.5 7.9 collective-permute-start.27
  252.2 6.3 collective-permute-start.29
  256.3 18.1 %collective-permute-start.22 = (bf16[512,2,512]{2,0,1:T(8,128)(2,1)}, bf16[512,2,512]{2,0,1:T(8,128)(2,1)}, u32[]{:S(2)}, u32[]{:S(2)}) collective-permute-start(bf16[512,2,512]{2,0,1:T(8,128)(2,1)} %add_convert_fusion), channel_id=1, source_target_pairs={{0,1},{1,0},{2,3},{3,2},{4,5},{5,4},{6,7},{7,6},{8,9},{9,8},{10,11... | collective-permute-start | bytes 3145736 | tf_op jit(solution)/shard_map/ppermute | solution.py:1030
  525.9 33.9 %collective-permute-start.30 = (bf16[512,512]{1,0:T(8,128)(2,1)}, bf16[512,512]{1,0:T(8,128)(2,1)}, u32[]{:S(2)}, u32[]{:S(2)}) collective-permute-start(bf16[512,512]{1,0:T(8,128)(2,1)} %get-tuple-element.35), channel_id=1, source_target_pairs={{0,2},{1,3},{2,0},{3,1},{4,6},{5,7},{6,4},{7,5},{8,10},{9,11},{10,... | collective-permute-start | bytes 1572872 | tf_op jit(solution)/shard_map/ppermute | solution.py:1030
  526.9 66.8 %collective-permute-start.31 = (bf16[512,512]{1,0:T(8,128)(2,1)}, bf16[512,512]{1,0:T(8,128)(2,1)}, u32[]{:S(2)}, u32[]{:S(2)}) collective-permute-start(bf16[512,512]{1,0:T(8,128)(2,1)} %get-tuple-element.35), channel_id=1, source_target_pairs={{0,1},{1,0},{2,3},{3,2},{4,5},{5,4},{6,7},{7,6},{8,9},{9,8},{10,11... | collective-permute-start | bytes 1572872 | tf_op jit(solution)/shard_map/ppermute | solution.py:1030
  559.8 33.9 %collective-permute-start.32 = (bf16[512,512]{1,0:T(8,128)(2,1)}, bf16[512,512]{1,0:T(8,128)(2,1)}, u32[]{:S(2)}, u32[]{:S(2)}) collective-permute-start(bf16[512,512]{1,0:T(8,128)(2,1)} %collective-permute-done.30), channel_id=1, source_target_pairs={{0,1},{1,0},{2,3},{3,2},{4,5},{5,4},{6,7},{7,6},{8,9},{9,8},{10,11... | collective-permute-start | bytes 1572872 | tf_op jit(solution)/shard_map/ppermute | solution.py:1030
  589.2 99.5 %all-to-all-start.1 = ((bf16[8,264,256]{2,1,0:T(8,128)(2,1)}), bf16[8,264,256]{2,1,0:T(8,128)(2,1)}, u32[]{:S(2)}, u32[]{:S(2)}) async-start(bf16[8,264,256]{2,1,0:T(8,128)(2,1)} %bitcast.114), calls=%async_computation.2 | async-start | bytes 2162688 | tf_op jit(solution)/shard_map/all_to_all | solution.py:1324
  610.7 43.9 %collective-permute-start.56 = (bf16[256,512]{1,0:T(8,128)(2,1)}, bf16[256,512]{1,0:T(8,128)(2,1)}, u32[]{:S(2)}, u32[]{:S(2)}) collective-permute-start(bf16[256,512]{1,0:T(8,128)(2,1)} %get-tuple-element.137), channel_id=1, source_target_pairs={{0,4},{4,0},{8,12},{12,8},{16,20},{20,16},{24,28},{28,24},{1,5},{5... | collective-permute-start | bytes 786440 | tf_op jit(solution)/shard_map/ppermute | solution.py:1043
  635.3 40.3 %collective-permute-start.49 = (bf16[256,1024]{1,0:T(8,128)(2,1)}, bf16[256,1024]{1,0:T(8,128)(2,1)}, u32[]{:S(2)}, u32[]{:S(2)}) collective-permute-start(bf16[256,1024]{1,0:T(8,128)(2,1)} %get-tuple-element.123), channel_id=1, source_target_pairs={{0,4},{4,0},{8,12},{12,8},{16,20},{20,16},{24,28},{28,24},{1,5},{5... | collective-permute-start | bytes 1572872 | tf_op jit(solution)/shard_map/ppermute | solution.py:1043
  639.9 37.8 %collective-permute-start.35 = (bf16[512,576]{0,1:T(8,128)(2,1)}, bf16[512,576]{0,1:T(8,128)(2,1)}, u32[]{:S(2)}, u32[]{:S(2)}) collective-permute-start(bf16[512,576]{0,1:T(8,128)(2,1)} %pad_maximum_fusion.9), channel_id=1, source_target_pairs={{0,1},{1,0},{2,3},{3,2},{4,5},{5,4},{6,7},{7,6},{8,9},{9,8},{10,11... | collective-permute-start | bytes 1769480 | tf_op jit(solution)/shard_map/ppermute | solution.py:1030
  654.7 13.8 %collective-permute-start.58 = (bf16[256,512]{1,0:T(8,128)(2,1)}, bf16[256,512]{1,0:T(8,128)(2,1)}, u32[]{:S(2)}, u32[]{:S(2)}) collective-permute-start(bf16[256,512]{1,0:T(8,128)(2,1)} %get-tuple-element.42), channel_id=1, source_target_pairs={{0,4},{4,0},{8,12},{12,8},{16,20},{20,16},{24,28},{28,24},{1,5},{5... | collective-permute-start | bytes 786440 | tf_op jit(solution)/shard_map/ppermute | solution.py:1043
  657.4 13.7 %collective-permute-start.57 = (bf16[256,512]{1,0:T(8,128)(2,1)}, bf16[256,512]{1,0:T(8,128)(2,1)}, u32[]{:S(2)}, u32[]{:S(2)}) collective-permute-start(bf16[256,512]{1,0:T(8,128)(2,1)} %fusion.65), channel_id=1, source_target_pairs={{0,8},{4,12},{8,16},{12,20},{16,24},{20,28},{24,0},{28,4},{1,9},{5... | collective-permute-start | bytes 786440 | tf_op jit(solution)/shard_map/ppermute | solution.py:1048
  661.2 40.8 %collective-permute-start.33 = (bf16[512,2,512]{2,0,1:T(8,128)(2,1)}, bf16[512,2,512]{2,0,1:T(8,128)(2,1)}, u32[]{:S(2)}, u32[]{:S(2)}) collective-permute-start(bf16[512,2,512]{2,0,1:T(8,128)(2,1)} %select_bitcast_fusion), channel_id=1, source_target_pairs={{0,1},{1,0},{2,3},{3,2},{4,5},{5,4},{6,7},{7,6},{8,9},{9,8},{10,11... | collective-permute-start | bytes 3145736 | tf_op jit(solution)/shard_map/ppermute | solution.py:1030
  668.5 12.8 %collective-permute-start.60 = (bf16[256,512]{1,0:T(8,128)(2,1)}, bf16[256,512]{1,0:T(8,128)(2,1)S(1)}, u32[]{:S(2)}, u32[]{:S(2)}) collective-permute-start(bf16[256,512]{1,0:T(8,128)(2,1)} %get-tuple-element.43), channel_id=1, source_target_pairs={{0,4},{4,0},{8,12},{12,8},{16,20},{20,16},{24,28},{28,24},{1,5},{5... | collective-permute-start | bytes 786440 | tf_op jit(solution)/shard_map/ppermute | solution.py:1043
  672.3 14.7 %collective-permute-start.59 = (bf16[256,512]{1,0:T(8,128)(2,1)S(1)}, bf16[256,512]{1,0:T(8,128)(2,1)S(1)}, u32[]{:S(2)}, u32[]{:S(2)}) collective-permute-start(bf16[256,512]{1,0:T(8,128)(2,1)S(1)} %add_convert_fusion.6), channel_id=1, source_target_pairs={{0,8},{4,12},{8,16},{12,20},{16,24},{20,28},{24,0},{28,4},{1,9},{5... | collective-permute-start | bytes 786440 | tf_op jit(solution)/shard_map/ppermute | solution.py:1048
  675.6 22.5 %collective-permute-start.51 = (bf16[256,1024]{1,0:T(8,128)(2,1)}, bf16[256,1024]{1,0:T(8,128)(2,1)}, u32[]{:S(2)}, u32[]{:S(2)}) collective-permute-start(bf16[256,1024]{1,0:T(8,128)(2,1)} %get-tuple-element.39), channel_id=1, source_target_pairs={{0,4},{4,0},{8,12},{12,8},{16,20},{20,16},{24,28},{28,24},{1,5},{5... | collective-permute-start | bytes 1572872 | tf_op jit(solution)/shard_map/ppermute | solution.py:1043
  677.7 66.8 %collective-permute-start.50 = (bf16[256,1024]{1,0:T(8,128)(2,1)}, bf16[256,1024]{1,0:T(8,128)(2,1)}, u32[]{:S(2)}, u32[]{:S(2)}) collective-permute-start(bf16[256,1024]{1,0:T(8,128)(2,1)} %fusion.36), channel_id=1, source_target_pairs={{0,8},{4,12},{8,16},{12,20},{16,24},{20,28},{24,0},{28,4},{1,9},{5... | collective-permute-start | bytes 1572872 | tf_op jit(solution)/shard_map/ppermute | solution.py:1048
  681.3 35.4 %collective-permute-start.36 = (bf16[512,576]{0,1:T(8,128)(2,1)}, bf16[512,576]{0,1:T(8,128)(2,1)}, u32[]{:S(2)}, u32[]{:S(2)}) collective-permute-start(bf16[512,576]{0,1:T(8,128)(2,1)} %add_convert_fusion.1), channel_id=1, source_target_pairs={{0,2},{1,3},{2,0},{3,1},{4,6},{5,7},{6,4},{7,5},{8,10},{9,11},{10,... | collective-permute-start | bytes 1769480 | tf_op jit(solution)/shard_map/ppermute | solution.py:1030
  687.0 64.5 %collective-permute-start.62 = (bf16[256,512]{1,0:T(8,128)(2,1)}, bf16[256,512]{1,0:T(8,128)(2,1)S(1)}, u32[]{:S(2)}, u32[]{:S(2)}) collective-permute-start(bf16[256,512]{1,0:T(8,128)(2,1)} %get-tuple-element.44), channel_id=1, source_target_pairs={{0,4},{4,0},{8,12},{12,8},{16,20},{20,16},{24,28},{28,24},{1,5},{5... | collective-permute-start | bytes 786440 | tf_op jit(solution)/shard_map/ppermute | solution.py:1043
  698.1 56.7 %collective-permute-start.61 = (bf16[256,512]{1,0:T(8,128)(2,1)}, bf16[256,512]{1,0:T(8,128)(2,1)}, u32[]{:S(2)}, u32[]{:S(2)}) collective-permute-start(bf16[256,512]{1,0:T(8,128)(2,1)} %add_convert_fusion.5), channel_id=1, source_target_pairs={{0,8},{4,12},{8,16},{12,20},{16,24},{20,28},{24,0},{28,4},{1,9},{5... | collective-permute-start | bytes 786440 | tf_op jit(solution)/shard_map/ppermute | solution.py:1048
  702.0 54.7 %collective-permute-start.53 = (bf16[256,1024]{1,0:T(8,128)(2,1)}, bf16[256,1024]{1,0:T(8,128)(2,1)}, u32[]{:S(2)}, u32[]{:S(2)}) collective-permute-start(bf16[256,1024]{1,0:T(8,128)(2,1)} %get-tuple-element.40), channel_id=1, source_target_pairs={{0,4},{4,0},{8,12},{12,8},{16,20},{20,16},{24,28},{28,24},{1,5},{5... | collective-permute-start | bytes 1572872 | tf_op jit(solution)/shard_map/ppermute | solution.py:1043
  716.7 22.0 %collective-permute-start.34 = (bf16[512,512]{1,0:T(8,128)(2,1)}, bf16[512,512]{1,0:T(8,128)(2,1)}, u32[]{:S(2)}, u32[]{:S(2)}) collective-permute-start(bf16[512,512]{1,0:T(8,128)(2,1)} %select_bitcast_fusion.4), channel_id=1, source_target_pairs={{0,2},{1,3},{2,0},{3,1},{4,6},{5,7},{6,4},{7,5},{8,10},{9,11},{10,... | collective-permute-start | bytes 1572872 | tf_op jit(solution)/shard_map/ppermute | solution.py:1030
  743.8 7.5 collective-permute-start.39
  746.0 19.3 %collective-permute-start.52 = (bf16[256,1024]{1,0:T(8,128)(2,1)S(1)}, bf16[256,1024]{1,0:T(8,128)(2,1)S(1)}, u32[]{:S(2)}, u32[]{:S(2)}) collective-permute-start(bf16[256,1024]{1,0:T(8,128)(2,1)S(1)} %add_convert_fusion.3), channel_id=1, source_target_pairs={{0,8},{4,12},{8,16},{12,20},{16,24},{20,28},{24,0},{28,4},{1,9},{5... | collective-permute-start | bytes 1572872 | tf_op jit(solution)/shard_map/ppermute | solution.py:1048
  751.3 5.4 collective-permute-start.41
  751.5 11.5 %collective-permute-start.40 = (bf16[65,576]{1,0:T(8,128)(2,1)S(1)}, bf16[65,576]{1,0:T(8,128)(2,1)S(1)}, u32[]{:S(2)}, u32[]{:S(2)}) collective-permute-start(bf16[65,576]{1,0:T(8,128)(2,1)S(1)} %fusion.84), channel_id=1, source_target_pairs={{0,8},{4,12},{8,16},{12,20},{16,24},{20,28},{24,0},{28,4},{1,9},{5... | collective-permute-start | bytes 224648 | tf_op jit(solution)/shard_map/ppermute | solution.py:1048
  756.7 38.1 %collective-permute-start.55 = (bf16[256,1024]{1,0:T(8,128)(2,1)}, bf16[256,1024]{1,0:T(8,128)(2,1)}, u32[]{:S(2)}, u32[]{:S(2)}) collective-permute-start(bf16[256,1024]{1,0:T(8,128)(2,1)} %get-tuple-element.41), channel_id=1, source_target_pairs={{0,4},{4,0},{8,12},{12,8},{16,20},{20,16},{24,28},{28,24},{1,5},{5... | collective-permute-start | bytes 1572872 | tf_op jit(solution)/shard_map/ppermute | solution.py:1043
  756.7 12.4 %collective-permute-start.43 = (bf16[65,576]{1,0:T(8,128)(2,1)S(1)}, bf16[65,576]{1,0:T(8,128)(2,1)S(1)}, u32[]{:S(2)}, u32[]{:S(2)}) collective-permute-start(bf16[65,576]{1,0:T(8,128)(2,1)S(1)} %get-tuple-element.37), channel_id=1, source_target_pairs={{0,4},{4,0},{8,12},{12,8},{16,20},{20,16},{24,28},{28,24},{1,5},{5... | collective-permute-start | bytes 224648 | tf_op jit(solution)/shard_map/ppermute | solution.py:1043
  763.0 7.1 collective-permute-start.42
  767.4 27.4 %collective-permute-start.54 = (bf16[256,1024]{1,0:T(8,128)(2,1)}, bf16[256,1024]{1,0:T(8,128)(2,1)}, u32[]{:S(2)}, u32[]{:S(2)}) collective-permute-start(bf16[256,1024]{1,0:T(8,128)(2,1)} %add_convert_fusion.2), channel_id=1, source_target_pairs={{0,8},{4,12},{8,16},{12,20},{16,24},{20,28},{24,0},{28,4},{1,9},{5... | collective-permute-start | bytes 1572872 | tf_op jit(solution)/shard_map/ppermute | solution.py:1048
  769.1 4.6 collective-permute-start.45
  770.2 12.5 %collective-permute-start.44 = (bf16[65,576]{1,0:T(8,128)(2,1)S(1)}, bf16[65,576]{1,0:T(8,128)(2,1)S(1)}, u32[]{:S(2)}, u32[]{:S(2)}) collective-permute-start(bf16[65,576]{1,0:T(8,128)(2,1)S(1)} %add_convert_fusion.9), channel_id=1, source_target_pairs={{0,8},{4,12},{8,16},{12,20},{16,24},{20,28},{24,0},{28,4},{1,9},{5... | collective-permute-start | bytes 224648 | tf_op jit(solution)/shard_map/ppermute | solution.py:1048
  771.0 12.6 %collective-permute-start.38 = (f32[4,128]{1,0:T(4,128)S(1)}, f32[4,128]{1,0:T(4,128)S(1)}, u32[]{:S(2)}, u32[]{:S(2)}) collective-permute-start(f32[4,128]{1,0:T(4,128)S(1)} %bitcast_add_fusion.1), channel_id=1, source_target_pairs={{0,2},{1,3},{2,0},{3,1},{4,6},{5,7},{6,4},{7,5},{8,10},{9,11},{10,... | collective-permute-start | bytes 6152 | tf_op jit(solution)/shard_map/ppermute | solution.py:1030
  782.7 4.6 collective-permute-start.46
  783.5 7.1 collective-permute-start.47
  787.3 3.3 collective-permute-start.48
  (93 other events, 1017.1 us)
Sparse Core Ops, SparseCore 0:
  10.9 172.3 all-gather.2
  516.5 220.5 reduce-scatter.1
